TPU v7x, 32 devices: a whole 2x2x4 slice. The times are simulated.
32 devices in a mesh: data: 8 (over z, y), expert: 4 (over x, core).
Axes of the slice: x: 2, y: 2, z: 4, core: 2. Of those that a mesh axis runs over, the one named last changes fastest.
Arguments:
- dy: bfloat16 [32768, 768], P(('data', 'expert'))
- gates: float32 [32768, 1], P(('data', 'expert'))
- topk_idx: int32 [32768, 1], P(('data', 'expert'))
- slot: int32 [32768, 1], P(('data', 'expert'))
- yd: bfloat16 [32768, 1, 768], P(('data', 'expert'))
- xd: bfloat16 [64, 640, 768], P(('data', 'expert'))
- h1: bfloat16 [64, 640, 3072], P(('data', 'expert'))
- h3: bfloat16 [64, 640, 3072], P(('data', 'expert'))
- w1: bfloat16 [8, 768, 3072], P('expert')
- w3: bfloat16 [8, 768, 3072], P('expert')
- w2: bfloat16 [8, 3072, 768], P('expert')
Outputs:
- output 1: bfloat16 [32768, 768], P(('data', 'expert'))
- output 2: float32 [32768, 1], P(('data', 'expert'))
- output 3: float32 [8, 768, 3072], P('expert', None, 'data')
- output 4: float32 [8, 768, 3072], P('expert', None, 'data')
- output 5: float32 [8, 3072, 768], P('expert', 'data')
All inputs are finite; a program needn't handle non-finite values.
Results may differ from a plain program's by a relative error of at most 0.00861423.
Values are sent between devices in bfloat16 or wider.
A program may use at most 1 GiB of HBM per device.

v0:
```python
import functools

import jax
import jax.numpy as jnp
from jax import lax
from jax.experimental import pallas as pl
from jax.experimental.pallas import tpu as pltpu
from jax.sharding import PartitionSpec as P


F32 = jnp.float32
BF16 = jnp.bfloat16


RING = (0, 2, 4, 6, 7, 5, 3, 1)
RIGHT = [(RING[i], RING[(i + 1) % 8]) for i in range(8)]
LEFT = [(RING[(i + 1) % 8], RING[i]) for i in range(8)]


def _dw_kernel(e, n, first, idx_ref, *refs):
    xs, ys = refs[:n], refs[n:2 * n]
    w1, w3, w2 = refs[2 * n:2 * n + 3]
    o1, o3, o2 = refs[-15:-12]
    x, y, w13, w2s, dh, a, acc13, acc2, wsem, xsem, ysem, osem = refs[-12:]
    rows = xs[0].shape[0]
    fs = w2s.shape[0]
    tile = 128
    per = rows // tile
    f0 = pl.multiple_of(idx_ref[0] * fs, 128)
    half = lambda j: pl.ds(j * fs, fs)

    def row_copy(src, dst, j, sem):
        return pltpu.make_async_copy(src, dst.at[pl.ds(pl.multiple_of(j * rows, 128), rows)], sem.at[j])

    wcp = [
        pltpu.make_async_copy(w1.at[e, :, pl.ds(f0, fs)], w13.at[:, half(0)], wsem.at[0]),
        pltpu.make_async_copy(w3.at[e, :, pl.ds(f0, fs)], w13.at[:, half(1)], wsem.at[1]),
        pltpu.make_async_copy(w2.at[e, pl.ds(f0, fs), :], w2s, wsem.at[2]),
    ]
    row_copy(xs[0], x, 0, xsem).start()
    for c in wcp:
        c.start()
    row_copy(ys[0], y, 0, ysem).start()
    for j in range(1, n):
        row_copy(xs[j], x, j, xsem).start()
        row_copy(ys[j], y, j, ysem).start()
    prev = []
    if not first:
        prev = [
            pltpu.make_async_copy(o1.at[e], acc13.at[:, half(0)], wsem.at[3]),
            pltpu.make_async_copy(o3.at[e], acc13.at[:, half(1)], wsem.at[4]),
            pltpu.make_async_copy(o2.at[e], acc2, wsem.at[5]),
        ]
        for c in prev:
            c.start()
    for c in wcp:
        c.wait()

    def rows_body(i, _):
        @pl.when(lax.rem(i, per) == 0)
        def _():
            row_copy(xs[0], x, i // per, xsem).wait()
            row_copy(ys[0], y, i // per, ysem).wait()

        r = pl.ds(pl.multiple_of(i * tile, 128), tile)
        h = jnp.dot(x[r, :], w13[...], preferred_element_type=F32).astype(BF16).astype(F32)
        da = lax.dot_general(y[r, :], w2s[...], (((1,), (1,)), ((), ())),
                             preferred_element_type=F32).astype(BF16).astype(F32)
        h1, h3 = h[:, :fs], h[:, fs:]
        s = jax.nn.sigmoid(h1)
        silu = h1 * s
        a[r, :] = (silu * h3).astype(BF16)
        dh[r, :fs] = (da * h3 * s * (1.0 + h1 * (1.0 - s))).astype(BF16)
        dh[r, fs:] = (da * silu).astype(BF16)
        return 0

    lax.fori_loop(0, per * n, rows_body, 0)
    for c in prev:
        c.wait()

    def acc(ref, m, val):
        if first:
            ref[m, :] = val
        else:
            ref[m, :] += val

    def out_copies(i):
        m = pl.ds(pl.multiple_of(i * 256, 256), 256)
        return (pltpu.make_async_copy(acc13.at[m, half(0)], o1.at[e, m], osem.at[0]),
                pltpu.make_async_copy(acc13.at[m, half(1)], o3.at[e, m], osem.at[1]))

    def d13_body(i, _):
        m = pl.ds(pl.multiple_of(i * 256, 256), 256)
        acc(acc13, m, lax.dot_general(x[:, m], dh[...], (((0,), (0,)), ((), ())), preferred_element_type=F32))
        for c in out_copies(i):
            c.start()
        return 0

    nm = x.shape[1] // 256
    lax.fori_loop(0, nm, d13_body, 0)

    def d2_copy(i):
        m = pl.ds(pl.multiple_of(i * 128, 128), 128)
        return pltpu.make_async_copy(acc2.at[m], o2.at[e, m], osem.at[2])

    def d2_body(i, _):
        m = pl.ds(pl.multiple_of(i * 128, 128), 128)
        acc(acc2, m, lax.dot_general(a[:, m], y[...], (((0,), (0,)), ((), ())), preferred_element_type=F32))
        d2_copy(i).start()
        return 0

    lax.fori_loop(0, fs // 128, d2_body, 0)

    def drain13(i, _):
        for c in out_copies(i):
            c.wait()
        return 0

    def drain2(i, _):
        d2_copy(i).wait()
        return 0

    lax.fori_loop(0, nm, drain13, 0)
    lax.fori_loop(0, fs // 128, drain2, 0)


def _dw_call(e, idx, xs, ys, w1, w3, w2, prev, first):
    el, d, f = w1.shape
    n, rows = len(xs), xs[0].shape[0]
    fs = f // 8
    anyspec = pl.BlockSpec(memory_space=pl.ANY)
    outs = [jax.ShapeDtypeStruct((el, d, fs), F32), jax.ShapeDtypeStruct((el, d, fs), F32),
            jax.ShapeDtypeStruct((el, fs, d), F32)]
    args = [idx, *xs, *ys, w1, w3, w2]
    alias = {}
    if prev is not None:
        alias = {len(args) + i: i for i in range(3)}
        args += list(prev)
    return pl.pallas_call(
        functools.partial(_dw_kernel, e, n, first),
        out_shape=outs,
        in_specs=[pl.BlockSpec(memory_space=pltpu.SMEM)] + [anyspec] * (len(args) - 1),
        out_specs=[anyspec] * 3,
        scratch_shapes=[
            pltpu.VMEM((n * rows, d), BF16),
            pltpu.VMEM((n * rows, d), BF16),
            pltpu.VMEM((d, 2 * fs), BF16),
            pltpu.VMEM((fs, d), BF16),
            pltpu.VMEM((n * rows, 2 * fs), BF16),
            pltpu.VMEM((n * rows, fs), BF16),
            pltpu.VMEM((d, 2 * fs), F32),
            pltpu.VMEM((fs, d), F32),
            pltpu.SemaphoreType.DMA((6,)),
            pltpu.SemaphoreType.DMA((n,)),
            pltpu.SemaphoreType.DMA((n,)),
            pltpu.SemaphoreType.DMA((3,)),
        ],
        input_output_aliases=alias,
        cost_estimate=pl.CostEstimate(flops=12 * n * rows * d * fs, bytes_accessed=n * 2 * 2**20 + 9 * 2**20,
                                      transcendentals=n * rows * fs),
    )(*args)


def solution(mesh):
    np_ = mesh.shape['expert']
    tok = P(('data', 'expert'), None)
    buf = P(('data', 'expert'), None, None)
    wsp = P('expert', None, None)

    def body(dy, gates, topk_idx, slot, yd, xd, h1, h3, w1, w3, w2):
        d = dy.shape[1]
        el = w1.shape[0]
        cap = xd.shape[1] // np_
        idx = lax.axis_index('data').astype(jnp.int32).reshape(1)

        def chain(c, last_right):
            r, l = [c], [c]
            for _ in range(3):
                r.append(lax.ppermute(r[-1], 'data', RIGHT))
                l.append(lax.ppermute(l[-1], 'data', LEFT))
            r.append(lax.ppermute(r[3], 'data', RIGHT) if last_right else lax.ppermute(l[3], 'data', LEFT))
            return r, l

        xch = [chain(xd[e], True) for e in range(el)]

        v = (gates[:, :, None] * dy.astype(F32)[:, None, :]).astype(BF16)
        col = jnp.where(slot >= 0, slot, cap)
        send = jnp.zeros((np_ * el, cap, d), BF16).at[topk_idx, col].set(v, mode='drop')
        recv = lax.all_to_all(send.reshape(np_, el, cap, d), 'expert', 0, 0, tiled=True)
        dyd = jnp.swapaxes(recv, 0, 1).reshape(el, np_ * cap, d)
        ych = [chain(dyd[e], False) for e in range(el)]
        dg = jnp.einsum('tkd,td->tk', yd, dy, preferred_element_type=F32)

        h1f = h1.astype(F32)
        h3f = h3.astype(F32)
        s = jax.nn.sigmoid(h1f)
        silu = h1f * s
        da = jnp.einsum('ecd,efd->ecf', dyd, w2, preferred_element_type=F32).astype(BF16).astype(F32)
        dh1 = (da * h3f * s * (1.0 + h1f * (1.0 - s))).astype(BF16)
        dh3 = (da * silu).astype(BF16)
        dxd = (jnp.einsum('ecf,edf->ecd', dh1, w1, preferred_element_type=F32)
               + jnp.einsum('ecf,edf->ecd', dh3, w3, preferred_element_type=F32)).astype(BF16)
        out = jnp.swapaxes(dxd.reshape(el, np_, cap, d), 0, 1)
        back = lax.all_to_all(out, 'expert', 0, 0, tiled=True).reshape(np_ * el, cap, d)
        got = back[topk_idx, jnp.minimum(col, cap - 1)].astype(F32)
        dx = jnp.sum(jnp.where((slot >= 0)[:, :, None], got, 0.0), axis=1).astype(BF16)

        acc = None
        steps = (lambda r, l: (r[0], r[1]), lambda r, l: (l[1], r[2]),
                 lambda r, l: (l[2], r[3], l[3]), lambda r, l: (r[4],))
        for k, pick in enumerate(steps):
            for e in range(el):
                acc = _dw_call(e, idx, pick(*xch[e]), pick(*ych[e]), w1, w3, w2, acc, k == 0)
        dw1, dw3, dw2 = acc
        return dx, dg, dw1, dw3, dw2

    return jax.shard_map(body, mesh=mesh,
                         in_specs=(tok, tok, tok, tok, buf, buf, buf, buf, wsp, wsp, wsp),
                         out_specs=(tok, tok, P('expert', None, 'data'), P('expert', None, 'data'), P('expert', 'data', None)),
                         check_vma=False)
```

profile of v0, /device:TPU:0, one launch (start us, length us, event | category | flops | bytes accessed | tf_op | source)
XLA Modules:
  0.0 330.0 jit_solution(18055922282474966347)
XLA Ops:
  2.9 7.3 %scatter_custom_fusion = bf16[1280,768]{1,0:T(8,128)(2,1)} fusion(s32[1024]{0:T(1024)S(1)} %broadcast_select_fusion, bf16[1024,768]{1,0:T(8,128)(2,1)} %param.11, f32[1024]{0:T(1024)} %bitcast.40, bf16[]{:T(256)} %constant.2.clone.1), kind=kCustom, calls=%fused_computation.26 | custom fusion | flops 2359296 | bytes 3543042
  10.2 4.2 %all-to-all-start = ((bf16[4,2,160,768]{3,2,1,0:T(8,128)(2,1)}), bf16[4,2,160,768]{3,2,1,0:T(8,128)(2,1)S(1)}, u32[]{:S(2)}, u32[]{:S(2)}) async-start(bf16[4,2,160,768]{3,2,1,0:T(8,128)(2,1)} %bitcast.37), calls=%async_computation | async-start | bytes 3932160 | tf_op jit(solution)/shard_map/all_to_all | solution.py:189
  14.4 1.6 slice_bitcast_fusion
  16.1 2.5 collective-permute-start.8
  18.6 1.6 collective-permute-start
  20.6 20.6 %collective-permute-done.8.refs_1_ = bf16[640,768]{1,0:T(8,128)(2,1)} collective-permute-done((bf16[640,768]{1,0:T(8,128)(2,1)S(1)}, bf16[640,768]{1,0:T(8,128)(2,1)}, u32[]{:S(2)}, u32[]{:S(2)}) %collective-permute-start.8) | collective-permute-done | bytes 983072 | tf_op jit(solution)/shard_map/ppermute | solution.py:179
  41.2 2.1 collective-permute-start.9
  43.3 19.0 %collective-permute-done.refs_1_ = bf16[640,768]{1,0:T(8,128)(2,1)} collective-permute-done((bf16[640,768]{1,0:T(8,128)(2,1)S(1)}, bf16[640,768]{1,0:T(8,128)(2,1)}, u32[]{:S(2)}, u32[]{:S(2)}) %collective-permute-start) | collective-permute-done | bytes 983072 | tf_op jit(solution)/shard_map/ppermute | solution.py:179
  62.3 2.1 collective-permute-start.1
  64.9 1.5 collective-permute-start.17
  68.5 12.1 %convolution_convert_fusion = bf16[2,640,3072]{2,1,0:T(8,128)(2,1)} fusion(bf16[2,640,768]{2,1,0:T(8,128)(2,1)S(1)} %bitcast.38, bf16[2,3072,768]{2,1,0:T(8,128)(2,1)} %refs_4_.11), kind=kOutput, calls=%fused_computation.17 | convolution fusion | flops 6043729920 | bytes 19267584 | tf_op jit(solution)/shard_map/ecd,efd->ecf/dot_general | solution.py:198
  80.6 15.1 %fusion.8 = f32[2,640,768]{2,1,0:T(8,128)} fusion(bf16[2,768,3072]{2,1,0:T(8,128)(2,1)} %refs_3_.3, bf16[2,640,3072]{2,1,0:T(8,128)(2,1)} %convolution_convert_fusion, bf16[2,640,3072]{2,1,0:T(8,128)(2,1)} %param.17), kind=kOutput, calls=%fused_computation.15 | convolution fusion | flops 6071255040 | bytes 29097984 | tf_op jit(solution)/shard_map/ecf,edf->ecd/dot_general | solution.py:202
  95.7 1.5 collective-permute-start.12
  97.2 7.2 %collective-permute-done.1.refs_1_ = bf16[640,768]{1,0:T(8,128)(2,1)} collective-permute-done((bf16[640,768]{1,0:T(8,128)(2,1)}, bf16[640,768]{1,0:T(8,128)(2,1)}, u32[]{:S(2)}, u32[]{:S(2)}) %collective-permute-start.1) | collective-permute-done | bytes 983072 | tf_op jit(solution)/shard_map/ppermute | solution.py:179
  104.4 2.1 collective-permute-start.19
  106.5 3.8 %collective-permute-done.17.refs_0_ = bf16[640,768]{1,0:T(8,128)(2,1)S(1)} collective-permute-done((bf16[640,768]{1,0:T(8,128)(2,1)}, bf16[640,768]{1,0:T(8,128)(2,1)S(1)}, u32[]{:S(2)}, u32[]{:S(2)}) %collective-permute-start.17) | collective-permute-done | bytes 983072 | tf_op jit(solution)/shard_map/ppermute | solution.py:180
  110.3 1.6 collective-permute-start.10
  111.9 18.3 %add_convert_fusion = bf16[2,640,768]{2,1,0:T(8,128)(2,1)S(1)} fusion(f32[2,640,768]{2,1,0:T(8,128)} %fusion.8, bf16[2,768,3072]{2,1,0:T(8,128)(2,1)} %refs_2_.3, bf16[2,640,3072]{2,1,0:T(8,128)(2,1)} %convolution_convert_fusion, bf16[2,640,3072]{2,1,0:T(8,128)(2,1)} %param.17, bf16[2,640,3072]{2,1,0:T(8,128)(2,1)} %param.18), kind=kOutput, calls=%fused_computation.18 | convolution fusion | flops 6092881920 | bytes 38928384 | tf_op jit(solution)/shard_map/ecf,edf->ecd/dot_general | solution.py:201
  130.1 1.4 copy.48
  131.6 3.7 %all-to-all-start.1 = ((bf16[4,2,160,768]{3,2,1,0:T(8,128)(2,1)}), bf16[4,2,160,768]{3,2,1,0:T(8,128)(2,1)S(1)}, u32[]{:S(2)}, u32[]{:S(2)}) async-start(bf16[4,2,160,768]{3,2,1,0:T(8,128)(2,1)} %bitcast.36), calls=%async_computation.1 | async-start | bytes 3932160 | tf_op jit(solution)/shard_map/all_to_all | solution.py:204
  135.8 2.5 fusion.13
  138.3 8.2 %collective-permute-done.19.refs_3_ = bf16[640,768]{1,0:T(8,128)(2,1)} collective-permute-done((bf16[640,768]{1,0:T(8,128)(2,1)}, bf16[640,768]{1,0:T(8,128)(2,1)}, u32[]{:S(2)}, u32[]{:S(2)}) %collective-permute-start.19) | collective-permute-done | bytes 983072 | tf_op jit(solution)/shard_map/ppermute | solution.py:179
  146.6 2.1 collective-permute-start.2
  148.6 1.6 collective-permute-start.26
  150.2 2.3 collective-permute-done.4.refs_2_
  152.5 15.1 %collective-permute-done.10.refs_1_ = bf16[640,768]{1,0:T(8,128)(2,1)} collective-permute-done((bf16[640,768]{1,0:T(8,128)(2,1)}, bf16[640,768]{1,0:T(8,128)(2,1)}, u32[]{:S(2)}, u32[]{:S(2)}) %collective-permute-start.10) | collective-permute-done | bytes 983072 | tf_op jit(solution)/shard_map/ppermute | solution.py:179
  167.6 2.0 collective-permute-start.5
  169.7 11.8 %shard_map.146 = (f32[2,768,384]{2,1,0:T(8,128)}, f32[2,768,384]{2,1,0:T(8,128)}, f32[2,384,768]{2,1,0:T(8,128)}) custom-call(s32[1]{0:T(128)} %bitcast.14.idx_ref, bf16[640,768]{1,0:T(8,128)(2,1)} %copy-done.1, bf16[640,768]{1,0:T(8,128)(2,1)} %collective-permute-done.8.refs_1_, bf16[640,768]{1,0:T(8,128)(2,1)} %bitcast.18.refs_2_, ...), custom_call_target="tpu_custom_call" | custom-call | flops 4529848320 | bytes 13631488 | tf_op jit(solution)/shard_map/pallas_call | solution.py:139
  181.6 11.8 %shard_map.147 = (f32[2,768,384]{2,1,0:T(8,128)}, f32[2,768,384]{2,1,0:T(8,128)}, f32[2,384,768]{2,1,0:T(8,128)}) custom-call(s32[1]{0:T(128)} %bitcast.14.idx_ref, bf16[640,768]{1,0:T(8,128)(2,1)} %copy-done.2, bf16[640,768]{1,0:T(8,128)(2,1)} %collective-permute-done.refs_1_, ...), custom_call_target="tpu_custom_call", output_to_operand_aliasing={{0}: (8, {}), {1}: (9, {}), {2}: (10, {})} | custom-call | flops 4529848320 | bytes 13631488 | tf_op jit(solution)/shard_map/pallas_call | solution.py:139
  193.4 8.8 %gather_fusion = bf16[1024,768]{1,0:T(8,128)(2,1)S(1)} fusion(bf16[8,160,768]{2,1,0:T(8,128)(2,1)S(1)} %bitcast.32, s32[1024]{0:T(1024)S(1)} %bitcast.33), kind=kCustom, calls=%fused_computation | custom fusion | bytes 3153920 | tf_op jit(solution)/shard_map/gather | solution.py:205
  202.2 2.0 collective-permute-start.18
  204.2 1.6 collective-permute-start.14
  205.8 3.9 %collective-permute-done.26.refs_3_ = bf16[640,768]{1,0:T(8,128)(2,1)} collective-permute-done((bf16[640,768]{1,0:T(8,128)(2,1)}, bf16[640,768]{1,0:T(8,128)(2,1)}, u32[]{:S(2)}, u32[]{:S(2)}) %collective-permute-start.26) | collective-permute-done | bytes 983072 | tf_op jit(solution)/shard_map/ppermute | solution.py:179
  209.8 2.1 collective-permute-start.27
  211.8 3.9 %collective-permute-done.5.refs_3_ = bf16[640,768]{1,0:T(8,128)(2,1)} collective-permute-done((bf16[640,768]{1,0:T(8,128)(2,1)}, bf16[640,768]{1,0:T(8,128)(2,1)}, u32[]{:S(2)}, u32[]{:S(2)}) %collective-permute-start.5) | collective-permute-done | bytes 983072 | tf_op jit(solution)/shard_map/ppermute | solution.py:180
  215.7 1.5 fusion.14
  217.2 12.2 %shard_map.148 = (f32[2,768,384]{2,1,0:T(8,128)}, f32[2,768,384]{2,1,0:T(8,128)}, f32[2,384,768]{2,1,0:T(8,128)}) custom-call(s32[1]{0:T(128)} %bitcast.14.idx_ref, bf16[640,768]{1,0:T(8,128)(2,1)} %collective-permute-done.22.refs_0_, bf16[640,768]{1,0:T(8,128)(2,1)} %collective-permute-done.9.refs_1_, ...), custom_call_target="tpu_custom_call", output_to_operand_aliasing={{0}: (8, {}), {1}: (9, {}), {2}: (10, {})} | custom-call | flops 4529848320 | bytes 13631488 | tf_op jit(solution)/shard_map/pallas_call | solution.py:139
  229.4 1.5 collective-permute-done.20.refs_3_
  230.8 2.1 collective-permute-start.21
  232.9 12.1 %shard_map.149 = (f32[2,768,384]{2,1,0:T(8,128)}, f32[2,768,384]{2,1,0:T(8,128)}, f32[2,384,768]{2,1,0:T(8,128)}) custom-call(s32[1]{0:T(128)} %bitcast.14.idx_ref, bf16[640,768]{1,0:T(8,128)(2,1)} %collective-permute-done.16.refs_0_, bf16[640,768]{1,0:T(8,128)(2,1)} %collective-permute-done.1.refs_1_, ...), custom_call_target="tpu_custom_call", output_to_operand_aliasing={{0}: (8, {}), {1}: (9, {}), {2}: (10, {})} | custom-call | flops 4529848320 | bytes 13631488 | tf_op jit(solution)/shard_map/pallas_call | solution.py:139
  245.0 1.6 collective-permute-start.11
  246.7 11.1 %collective-permute-done.14.refs_5_ = bf16[640,768]{1,0:T(8,128)(2,1)S(1)} collective-permute-done((bf16[640,768]{1,0:T(8,128)(2,1)}, bf16[640,768]{1,0:T(8,128)(2,1)S(1)}, u32[]{:S(2)}, u32[]{:S(2)}) %collective-permute-start.14) | collective-permute-done | bytes 983072 | tf_op jit(solution)/shard_map/ppermute | solution.py:180
  257.7 1.6 collective-permute-start.3
  259.8 19.0 %collective-permute-done.6.refs_5_ = bf16[640,768]{1,0:T(8,128)(2,1)S(1)} collective-permute-done((bf16[640,768]{1,0:T(8,128)(2,1)}, bf16[640,768]{1,0:T(8,128)(2,1)S(1)}, u32[]{:S(2)}, u32[]{:S(2)}) %collective-permute-start.6) | collective-permute-done | bytes 983072 | tf_op jit(solution)/shard_map/ppermute | solution.py:180
  278.8 16.3 %shard_map.150 = (f32[2,768,384]{2,1,0:T(8,128)}, f32[2,768,384]{2,1,0:T(8,128)}, f32[2,384,768]{2,1,0:T(8,128)}) custom-call(s32[1]{0:T(128)} %bitcast.14.idx_ref, bf16[640,768]{1,0:T(8,128)(2,1)} %collective-permute-done.23.refs_0_, ...), custom_call_target="tpu_custom_call", output_to_operand_aliasing={{0}: (10, {}), {1}: (11, {}), {2}: (12, {})} | custom-call | flops 6794772480 | bytes 15728640 | tf_op jit(solution)/shard_map/pallas_call | solution.py:139
  295.1 15.9 %shard_map.151 = (f32[2,768,384]{2,1,0:T(8,128)}, f32[2,768,384]{2,1,0:T(8,128)}, f32[2,384,768]{2,1,0:T(8,128)}) custom-call(s32[1]{0:T(128)} %bitcast.14.idx_ref, bf16[640,768]{1,0:T(8,128)(2,1)} %copy-done.3, bf16[640,768]{1,0:T(8,128)(2,1)} %collective-permute-done.2.refs_1_, ...), custom_call_target="tpu_custom_call", output_to_operand_aliasing={{0}: (10, {}), {1}: (11, {}), {2}: (12, {})} | custom-call | flops 6794772480 | bytes 15728640 | tf_op jit(solution)/shard_map/pallas_call | solution.py:139
  311.0 8.9 %shard_map.152 = (f32[2,768,384]{2,1,0:T(8,128)}, f32[2,768,384]{2,1,0:T(8,128)}, f32[2,384,768]{2,1,0:T(8,128)}) custom-call(s32[1]{0:T(128)} %bitcast.14.idx_ref, bf16[640,768]{1,0:T(8,128)(2,1)} %collective-permute-done.11.refs_0_, bf16[640,768]{1,0:T(8,128)(2,1)} %collective-permute-done.15.refs_1_, ...), custom_call_target="tpu_custom_call", output_to_operand_aliasing={{0}: (6, {}), {1}: (7, {}), {2}: (8, {})} | custom-call | flops 2264924160 | bytes 11534336 | tf_op jit(solution)/shard_map/pallas_call | solution.py:139
  320.9 8.9 %shard_map.153 = (f32[2,768,384]{2,1,0:T(8,128)}, f32[2,768,384]{2,1,0:T(8,128)}, f32[2,384,768]{2,1,0:T(8,128)}) custom-call(s32[1]{0:T(128)} %bitcast.14.idx_ref, bf16[640,768]{1,0:T(8,128)(2,1)} %copy-done.6, bf16[640,768]{1,0:T(8,128)(2,1)} %collective-permute-done.7.refs_1_, ...), custom_call_target="tpu_custom_call", output_to_operand_aliasing={{0}: (6, {}), {1}: (7, {}), {2}: (8, {})} | custom-call | flops 2264924160 | bytes 11534336 | tf_op jit(solution)/shard_map/pallas_call | solution.py:139
  (53 shorter events, 7.4 us)
Async XLA Ops:
  10.2 56.2 %all-to-all-start = ((bf16[4,2,160,768]{3,2,1,0:T(8,128)(2,1)}), bf16[4,2,160,768]{3,2,1,0:T(8,128)(2,1)S(1)}, u32[]{:S(2)}, u32[]{:S(2)}) async-start(bf16[4,2,160,768]{3,2,1,0:T(8,128)(2,1)} %bitcast.37), calls=%async_computation | async-start | bytes 3932160 | tf_op jit(solution)/shard_map/all_to_all | solution.py:189
  16.1 48.8 %copy-start.1 = (bf16[640,768]{1,0:T(8,128)(2,1)}, bf16[640,768]{1,0:T(8,128)(2,1)S(1)}, u32[]{:S(2)}) copy-start(bf16[640,768]{1,0:T(8,128)(2,1)S(1)} %get-tuple-element.55.refs_0_) | copy-start | bytes 2949124
  16.1 48.8 %copy-start.2 = (bf16[640,768]{1,0:T(8,128)(2,1)}, bf16[640,768]{1,0:T(8,128)(2,1)S(1)}, u32[]{:S(2)}) copy-start(bf16[640,768]{1,0:T(8,128)(2,1)S(1)} %get-tuple-element.56.refs_0_) | copy-start | bytes 2949124
  16.1 25.1 %collective-permute-start.8 = (bf16[640,768]{1,0:T(8,128)(2,1)S(1)}, bf16[640,768]{1,0:T(8,128)(2,1)}, u32[]{:S(2)}, u32[]{:S(2)}) collective-permute-start(bf16[640,768]{1,0:T(8,128)(2,1)S(1)} %get-tuple-element.55.refs_0_), channel_id=1, source_target_pairs={{0,8},{8,16},{16,24},{24,28},{28,20},{20,12},{12,4},{4,0},{1,9},{9... | collective-permute-start | bytes 2949128 | tf_op jit(solution)/shard_map/ppermute | solution.py:179
  18.6 43.7 %collective-permute-start = (bf16[640,768]{1,0:T(8,128)(2,1)S(1)}, bf16[640,768]{1,0:T(8,128)(2,1)}, u32[]{:S(2)}, u32[]{:S(2)}) collective-permute-start(bf16[640,768]{1,0:T(8,128)(2,1)S(1)} %get-tuple-element.56.refs_0_), channel_id=1, source_target_pairs={{0,8},{8,16},{16,24},{24,28},{28,20},{20,12},{12,4},{4,0},{1,9},{9... | collective-permute-start | bytes 2949128 | tf_op jit(solution)/shard_map/ppermute | solution.py:179
  20.1 44.2 %collective-permute-start.22 = (bf16[640,768]{1,0:T(8,128)(2,1)S(1)}, bf16[640,768]{1,0:T(8,128)(2,1)}, u32[]{:S(2)}, u32[]{:S(2)}) collective-permute-start(bf16[640,768]{1,0:T(8,128)(2,1)S(1)} %get-tuple-element.55.refs_0_), channel_id=1, source_target_pairs={{8,0},{16,8},{24,16},{28,24},{20,28},{12,20},{4,12},{0,4},{9,1},{1... | collective-permute-start | bytes 2949128 | tf_op jit(solution)/shard_map/ppermute | solution.py:180
  20.6 44.3 %collective-permute-start.16 = (bf16[640,768]{1,0:T(8,128)(2,1)S(1)}, bf16[640,768]{1,0:T(8,128)(2,1)}, u32[]{:S(2)}, u32[]{:S(2)}) collective-permute-start(bf16[640,768]{1,0:T(8,128)(2,1)S(1)} %get-tuple-element.56.refs_0_), channel_id=1, source_target_pairs={{8,0},{16,8},{24,16},{28,24},{20,28},{12,20},{4,12},{0,4},{9,1},{1... | collective-permute-start | bytes 2949128 | tf_op jit(solution)/shard_map/ppermute | solution.py:180
  41.2 54.5 %collective-permute-start.9 = (bf16[640,768]{1,0:T(8,128)(2,1)}, bf16[640,768]{1,0:T(8,128)(2,1)}, u32[]{:S(2)}, u32[]{:S(2)}) collective-permute-start(bf16[640,768]{1,0:T(8,128)(2,1)} %collective-permute-done.8.refs_1_), channel_id=1, source_target_pairs={{0,8},{8,16},{16,24},{24,28},{28,20},{20,12},{12,4},{4,0},{1,9},{9... | collective-permute-start | bytes 2949128 | tf_op jit(solution)/shard_map/ppermute | solution.py:179
  62.3 42.1 %collective-permute-start.1 = (bf16[640,768]{1,0:T(8,128)(2,1)}, bf16[640,768]{1,0:T(8,128)(2,1)}, u32[]{:S(2)}, u32[]{:S(2)}) collective-permute-start(bf16[640,768]{1,0:T(8,128)(2,1)} %collective-permute-done.refs_1_), channel_id=1, source_target_pairs={{0,8},{8,16},{16,24},{24,28},{28,20},{20,12},{12,4},{4,0},{1,9},{9... | collective-permute-start | bytes 2949128 | tf_op jit(solution)/shard_map/ppermute | solution.py:179
  64.4 42.1 %collective-permute-start.23 = (bf16[640,768]{1,0:T(8,128)(2,1)}, bf16[640,768]{1,0:T(8,128)(2,1)}, u32[]{:S(2)}, u32[]{:S(2)}) collective-permute-start(bf16[640,768]{1,0:T(8,128)(2,1)} %collective-permute-done.22.refs_0_), channel_id=1, source_target_pairs={{8,0},{16,8},{24,16},{28,24},{20,28},{12,20},{4,12},{0,4},{9,1},{1... | collective-permute-start | bytes 2949128 | tf_op jit(solution)/shard_map/ppermute | solution.py:180
  64.9 45.4 %collective-permute-start.17 = (bf16[640,768]{1,0:T(8,128)(2,1)}, bf16[640,768]{1,0:T(8,128)(2,1)S(1)}, u32[]{:S(2)}, u32[]{:S(2)}) collective-permute-start(bf16[640,768]{1,0:T(8,128)(2,1)} %collective-permute-done.16.refs_0_), channel_id=1, source_target_pairs={{8,0},{16,8},{24,16},{28,24},{20,28},{12,20},{4,12},{0,4},{9,1},{1... | collective-permute-start | bytes 2949128 | tf_op jit(solution)/shard_map/ppermute | solution.py:180
  67.9 67.4 %collective-permute-start.25 = (bf16[640,768]{1,0:T(8,128)(2,1)}, bf16[640,768]{1,0:T(8,128)(2,1)}, u32[]{:S(2)}, u32[]{:S(2)}) collective-permute-start(bf16[640,768]{1,0:T(8,128)(2,1)} %bitcast.18.refs_2_), channel_id=1, source_target_pairs={{0,8},{8,16},{16,24},{24,28},{28,20},{20,12},{12,4},{4,0},{1,9},{9... | collective-permute-start | bytes 2949128 | tf_op jit(solution)/shard_map/ppermute | solution.py:179
  95.7 53.0 %collective-permute-start.12 = (bf16[640,768]{1,0:T(8,128)(2,1)}, bf16[640,768]{1,0:T(8,128)(2,1)}, u32[]{:S(2)}, u32[]{:S(2)}) collective-permute-start(bf16[640,768]{1,0:T(8,128)(2,1)} %bitcast.18.refs_2_), channel_id=1, source_target_pairs={{8,0},{16,8},{24,16},{28,24},{20,28},{12,20},{4,12},{0,4},{9,1},{1... | collective-permute-start | bytes 2949128 | tf_op jit(solution)/shard_map/ppermute | solution.py:180
  104.4 42.1 %collective-permute-start.19 = (bf16[640,768]{1,0:T(8,128)(2,1)}, bf16[640,768]{1,0:T(8,128)(2,1)}, u32[]{:S(2)}, u32[]{:S(2)}) collective-permute-start(bf16[640,768]{1,0:T(8,128)(2,1)} %bitcast.16.refs_2_), channel_id=1, source_target_pairs={{0,8},{8,16},{16,24},{24,28},{28,20},{20,12},{12,4},{4,0},{1,9},{9... | collective-permute-start | bytes 2949128 | tf_op jit(solution)/shard_map/ppermute | solution.py:179
  106.5 46.0 %collective-permute-start.4 = (bf16[640,768]{1,0:T(8,128)(2,1)}, bf16[640,768]{1,0:T(8,128)(2,1)}, u32[]{:S(2)}, u32[]{:S(2)}) collective-permute-start(bf16[640,768]{1,0:T(8,128)(2,1)} %bitcast.16.refs_2_), channel_id=1, source_target_pairs={{8,0},{16,8},{24,16},{28,24},{20,28},{12,20},{4,12},{0,4},{9,1},{1... | collective-permute-start | bytes 2949128 | tf_op jit(solution)/shard_map/ppermute | solution.py:180
  110.3 19.8 %copy-start.3 = (bf16[640,768]{1,0:T(8,128)(2,1)}, bf16[640,768]{1,0:T(8,128)(2,1)S(1)}, u32[]{:S(2)}) copy-start(bf16[640,768]{1,0:T(8,128)(2,1)S(1)} %collective-permute-done.17.refs_0_) | copy-start | bytes 2949124
  110.3 57.3 %collective-permute-start.10 = (bf16[640,768]{1,0:T(8,128)(2,1)}, bf16[640,768]{1,0:T(8,128)(2,1)}, u32[]{:S(2)}, u32[]{:S(2)}) collective-permute-start(bf16[640,768]{1,0:T(8,128)(2,1)} %collective-permute-done.9.refs_1_), channel_id=1, source_target_pairs={{0,8},{8,16},{16,24},{24,28},{28,20},{20,12},{12,4},{4,0},{1,9},{9... | collective-permute-start | bytes 2949128 | tf_op jit(solution)/shard_map/ppermute | solution.py:179
  130.1 5.7 %copy-start = (bf16[1024,768]{1,0:T(8,128)(2,1)S(1)}, bf16[1024,768]{1,0:T(8,128)(2,1)}, u32[]{:S(2)}) copy-start(bf16[1024,768]{1,0:T(8,128)(2,1)} %param.11) | copy-start | bytes 4718596
  131.6 38.1 %copy-start.7 = (s32[1024,1]{0,1:T(1,128)S(1)}, s32[1024,1]{0,1:T(1,128)}, u32[]{:S(2)}) copy-start(s32[1024,1]{0,1:T(1,128)} %param.14) | copy-start | bytes 12292
  131.6 61.8 %all-to-all-start.1 = ((bf16[4,2,160,768]{3,2,1,0:T(8,128)(2,1)}), bf16[4,2,160,768]{3,2,1,0:T(8,128)(2,1)S(1)}, u32[]{:S(2)}, u32[]{:S(2)}) async-start(bf16[4,2,160,768]{3,2,1,0:T(8,128)(2,1)} %bitcast.36), calls=%async_computation.1 | async-start | bytes 3932160 | tf_op jit(solution)/shard_map/all_to_all | solution.py:204
  135.3 46.2 %collective-permute-start.24 = (bf16[640,768]{1,0:T(8,128)(2,1)}, bf16[640,768]{1,0:T(8,128)(2,1)}, u32[]{:S(2)}, u32[]{:S(2)}) collective-permute-start(bf16[640,768]{1,0:T(8,128)(2,1)} %collective-permute-done.23.refs_0_), channel_id=1, source_target_pairs={{8,0},{16,8},{24,16},{28,24},{20,28},{12,20},{4,12},{0,4},{9,1},{1... | collective-permute-start | bytes 2949128 | tf_op jit(solution)/shard_map/ppermute | solution.py:180
  146.6 55.6 %collective-permute-start.2 = (bf16[640,768]{1,0:T(8,128)(2,1)}, bf16[640,768]{1,0:T(8,128)(2,1)}, u32[]{:S(2)}, u32[]{:S(2)}) collective-permute-start(bf16[640,768]{1,0:T(8,128)(2,1)} %collective-permute-done.1.refs_1_), channel_id=1, source_target_pairs={{0,8},{8,16},{16,24},{24,28},{28,20},{20,12},{12,4},{4,0},{1,9},{9... | collective-permute-start | bytes 2949128 | tf_op jit(solution)/shard_map/ppermute | solution.py:179
  148.6 61.1 %collective-permute-start.26 = (bf16[640,768]{1,0:T(8,128)(2,1)}, bf16[640,768]{1,0:T(8,128)(2,1)}, u32[]{:S(2)}, u32[]{:S(2)}) collective-permute-start(bf16[640,768]{1,0:T(8,128)(2,1)} %collective-permute-done.25.refs_3_), channel_id=1, source_target_pairs={{0,8},{8,16},{16,24},{24,28},{28,20},{20,12},{12,4},{4,0},{1,9},{9... | collective-permute-start | bytes 2949128 | tf_op jit(solution)/shard_map/ppermute | solution.py:179
  152.5 51.7 %collective-permute-start.13 = (bf16[640,768]{1,0:T(8,128)(2,1)}, bf16[640,768]{1,0:T(8,128)(2,1)}, u32[]{:S(2)}, u32[]{:S(2)}) collective-permute-start(bf16[640,768]{1,0:T(8,128)(2,1)} %collective-permute-done.12.refs_2_), channel_id=1, source_target_pairs={{8,0},{16,8},{24,16},{28,24},{20,28},{12,20},{4,12},{0,4},{9,1},{1... | collective-permute-start | bytes 2949128 | tf_op jit(solution)/shard_map/ppermute | solution.py:180
  167.6 48.1 %collective-permute-start.5 = (bf16[640,768]{1,0:T(8,128)(2,1)}, bf16[640,768]{1,0:T(8,128)(2,1)}, u32[]{:S(2)}, u32[]{:S(2)}) collective-permute-start(bf16[640,768]{1,0:T(8,128)(2,1)} %collective-permute-done.4.refs_2_), channel_id=1, source_target_pairs={{8,0},{16,8},{24,16},{28,24},{20,28},{12,20},{4,12},{0,4},{9,1},{1... | collective-permute-start | bytes 2949128 | tf_op jit(solution)/shard_map/ppermute | solution.py:180
  181.5 49.3 %collective-permute-start.20 = (bf16[640,768]{1,0:T(8,128)(2,1)}, bf16[640,768]{1,0:T(8,128)(2,1)}, u32[]{:S(2)}, u32[]{:S(2)}) collective-permute-start(bf16[640,768]{1,0:T(8,128)(2,1)} %collective-permute-done.19.refs_3_), channel_id=1, source_target_pairs={{0,8},{8,16},{16,24},{24,28},{28,20},{20,12},{12,4},{4,0},{1,9},{9... | collective-permute-start | bytes 2949128 | tf_op jit(solution)/shard_map/ppermute | solution.py:179
  202.2 42.8 %collective-permute-start.18 = (bf16[640,768]{1,0:T(8,128)(2,1)}, bf16[640,768]{1,0:T(8,128)(2,1)}, u32[]{:S(2)}, u32[]{:S(2)}) collective-permute-start(bf16[640,768]{1,0:T(8,128)(2,1)} %copy-done.3), channel_id=1, source_target_pairs={{8,0},{16,8},{24,16},{28,24},{20,28},{12,20},{4,12},{0,4},{9,1},{1... | collective-permute-start | bytes 2949128 | tf_op jit(solution)/shard_map/ppermute | solution.py:180
  204.2 53.5 %collective-permute-start.14 = (bf16[640,768]{1,0:T(8,128)(2,1)}, bf16[640,768]{1,0:T(8,128)(2,1)S(1)}, u32[]{:S(2)}, u32[]{:S(2)}) collective-permute-start(bf16[640,768]{1,0:T(8,128)(2,1)} %collective-permute-done.13.refs_3_), channel_id=1, source_target_pairs={{8,0},{16,8},{24,16},{28,24},{20,28},{12,20},{4,12},{0,4},{9,1},{1... | collective-permute-start | bytes 2949128 | tf_op jit(solution)/shard_map/ppermute | solution.py:180
  209.8 49.6 %collective-permute-start.27 = (bf16[640,768]{1,0:T(8,128)(2,1)}, bf16[640,768]{1,0:T(8,128)(2,1)}, u32[]{:S(2)}, u32[]{:S(2)}) collective-permute-start(bf16[640,768]{1,0:T(8,128)(2,1)} %collective-permute-done.26.refs_3_), channel_id=1, source_target_pairs={{0,8},{8,16},{16,24},{24,28},{28,20},{20,12},{12,4},{4,0},{1,9},{9... | collective-permute-start | bytes 2949128 | tf_op jit(solution)/shard_map/ppermute | solution.py:179
  215.7 63.1 %collective-permute-start.6 = (bf16[640,768]{1,0:T(8,128)(2,1)}, bf16[640,768]{1,0:T(8,128)(2,1)S(1)}, u32[]{:S(2)}, u32[]{:S(2)}) collective-permute-start(bf16[640,768]{1,0:T(8,128)(2,1)} %collective-permute-done.5.refs_3_), channel_id=1, source_target_pairs={{8,0},{16,8},{24,16},{28,24},{20,28},{12,20},{4,12},{0,4},{9,1},{1... | collective-permute-start | bytes 2949128 | tf_op jit(solution)/shard_map/ppermute | solution.py:180
  230.8 64.3 %collective-permute-start.21 = (bf16[640,768]{1,0:T(8,128)(2,1)}, bf16[640,768]{1,0:T(8,128)(2,1)}, u32[]{:S(2)}, u32[]{:S(2)}) collective-permute-start(bf16[640,768]{1,0:T(8,128)(2,1)} %collective-permute-done.20.refs_3_), channel_id=1, source_target_pairs={{0,8},{8,16},{16,24},{24,28},{28,20},{20,12},{12,4},{4,0},{1,9},{9... | collective-permute-start | bytes 2949128 | tf_op jit(solution)/shard_map/ppermute | solution.py:179
  245.0 66.0 %collective-permute-start.11 = (bf16[640,768]{1,0:T(8,128)(2,1)}, bf16[640,768]{1,0:T(8,128)(2,1)}, u32[]{:S(2)}, u32[]{:S(2)}) collective-permute-start(bf16[640,768]{1,0:T(8,128)(2,1)} %collective-permute-done.10.refs_1_), channel_id=1, source_target_pairs={{0,8},{8,16},{16,24},{24,28},{28,20},{20,12},{12,4},{4,0},{1,9},{9... | collective-permute-start | bytes 2949128 | tf_op jit(solution)/shard_map/ppermute | solution.py:181
  257.7 21.1 %copy-start.5 = (bf16[640,768]{1,0:T(8,128)(2,1)}, bf16[640,768]{1,0:T(8,128)(2,1)S(1)}, u32[]{:S(2)}) copy-start(bf16[640,768]{1,0:T(8,128)(2,1)S(1)} %collective-permute-done.14.refs_5_) | copy-start | bytes 2949124
  257.7 62.2 %collective-permute-start.3 = (bf16[640,768]{1,0:T(8,128)(2,1)}, bf16[640,768]{1,0:T(8,128)(2,1)S(1)}, u32[]{:S(2)}, u32[]{:S(2)}) collective-permute-start(bf16[640,768]{1,0:T(8,128)(2,1)} %collective-permute-done.2.refs_1_), channel_id=1, source_target_pairs={{0,8},{8,16},{16,24},{24,28},{28,20},{20,12},{12,4},{4,0},{1,9},{9... | collective-permute-start | bytes 2949128 | tf_op jit(solution)/shard_map/ppermute | solution.py:181
  259.3 51.7 %collective-permute-start.15 = (bf16[640,768]{1,0:T(8,128)(2,1)S(1)}, bf16[640,768]{1,0:T(8,128)(2,1)}, u32[]{:S(2)}, u32[]{:S(2)}) collective-permute-start(bf16[640,768]{1,0:T(8,128)(2,1)S(1)} %collective-permute-done.14.refs_5_), channel_id=1, source_target_pairs={{8,0},{16,8},{24,16},{28,24},{20,28},{12,20},{4,12},{0,4},{9,1},{1... | collective-permute-start | bytes 2949128 | tf_op jit(solution)/shard_map/ppermute | solution.py:181
  278.8 16.3 %copy-start.4 = (bf16[640,768]{1,0:T(8,128)(2,1)}, bf16[640,768]{1,0:T(8,128)(2,1)S(1)}, u32[]{:S(2)}) copy-start(bf16[640,768]{1,0:T(8,128)(2,1)S(1)} %collective-permute-done.6.refs_5_) | copy-start | bytes 2949124
  278.8 41.2 %collective-permute-start.7 = (bf16[640,768]{1,0:T(8,128)(2,1)S(1)}, bf16[640,768]{1,0:T(8,128)(2,1)}, u32[]{:S(2)}, u32[]{:S(2)}) collective-permute-start(bf16[640,768]{1,0:T(8,128)(2,1)S(1)} %collective-permute-done.6.refs_5_), channel_id=1, source_target_pairs={{8,0},{16,8},{24,16},{28,24},{20,28},{12,20},{4,12},{0,4},{9,1},{1... | collective-permute-start | bytes 2949128 | tf_op jit(solution)/shard_map/ppermute | solution.py:181
  320.0 1.0 copy-start.6
where the time goes:
time: 330 us
  waiting for transfers between devices  116 us (35%)
  Pallas kernels  97.8 us (30%)
  matrix products  45.4 us (14%)
  starting transfers between devices  41.6 us (13%)
  local copies, waits for them, and re-layouts  14.4 us (4%)
  other arithmetic  13.6 us (4%)
    pallas_call x8, Pallas kernels, _dw_call(): pl.pallas_call(functools.partial(_dw_kernel, e, n, first), out_shape=outs...  97.8 us
    ppermute x12, waiting for transfers between devices, chain(): r.append(lax.ppermute(r[-1], 'data', RIGHT))  75.6 us
    ppermute x12, waiting for transfers between devices, chain(): l.append(lax.ppermute(l[-1], 'data', LEFT))  40.6 us
    ppermute x12, starting transfers between devices, chain(): r.append(lax.ppermute(r[-1], 'data', RIGHT))  20.3 us
    dot_general x1, matrix products, body(): jnp.einsum('ecf,edf->ecd', dh1, w1, preferred_element_type=F32)  18.3 us
    dot_general x1, matrix products, body(): jnp.einsum('ecf,edf->ecd', dh3, w3, preferred_element_type=F32)  15.1 us
    dot_general x1, matrix products, body(): jnp.einsum('ecd,efd->ecf', dyd, w2, preferred_element_type=F32).astype(BF16)  12.1 us
    ppermute x12, starting transfers between devices, chain(): l.append(lax.ppermute(l[-1], 'data', LEFT))  9.63 us
  transfers between devices with their start and end apart: 30, of which 13 were waited for; matrix products, arithmetic and copies ran while one was open for 19% of the time, Pallas kernels for 27%

commit v1 on v0

--- a/solution.py
+++ b/solution.py
@@ -12,9 +12,223 @@
 BF16 = jnp.bfloat16
 
 
+PACK = 1024
+META = 16
 RING = (0, 2, 4, 6, 7, 5, 3, 1)
 RIGHT = [(RING[i], RING[(i + 1) % 8]) for i in range(8)]
 LEFT = [(RING[(i + 1) % 8], RING[i]) for i in range(8)]
+
+
+def _pack_kernel(grouped, starts, pos_ref, meta_ref, src_ref, *refs):
+    n = len(starts)
+    outs, src, sem = refs[:n], refs[n], refs[n + 1]
+    cps = []
+    if grouped:
+        np_, el, cap, _ = src_ref.shape
+        for p in range(np_):
+            for e in range(el):
+                dst = src.at[pl.ds(e * np_ * cap + p * cap, cap)]
+                cps.append(pltpu.make_async_copy(src_ref.at[p, e], dst, sem.at[p * el + e]))
+    else:
+        el, rows, _ = src_ref.shape
+        for e in range(el):
+            cps.append(pltpu.make_async_copy(src_ref.at[e], src.at[pl.ds(e * rows, rows)], sem.at[e]))
+    for c in cps:
+        c.start()
+    for c in cps:
+        c.wait()
+    pos = pos_ref[...]
+    for o, (base, rows, meta) in zip(outs, starts):
+        def tile_body(i, _, o=o, base=base):
+            r = pl.multiple_of(i * 128, 128)
+            row = (lax.broadcasted_iota(jnp.int32, (128, 1), 0) + (r + base)).astype(F32)
+            hot = jnp.where(pos == row, 1.0, 0.0).astype(BF16)
+            o[pl.ds(r, 128), :] = jnp.dot(hot, src[...], preferred_element_type=F32).astype(BF16)
+            return 0
+
+        lax.fori_loop(0, rows // 128, tile_body, 0)
+        if meta:
+            k = lax.broadcasted_iota(jnp.int32, (META, o.shape[1]), 0)
+            v = jnp.where(k == 0, meta_ref[0], jnp.where(k == 1, meta_ref[1], meta_ref[2]))
+            o[pl.ds(rows, META), :] = v.astype(BF16)
+
+
+def _pack(src, pos, meta, starts):
+    d = src.shape[-1]
+    rows = pos.shape[1]
+    vspec = pl.BlockSpec(memory_space=pltpu.VMEM)
+    total = sum(r for _, r, _ in starts)
+    return pl.pallas_call(
+        functools.partial(_pack_kernel, src.ndim == 4, starts),
+        out_shape=[jax.ShapeDtypeStruct((r + META * m, d), BF16) for _, r, m in starts],
+        in_specs=[vspec, pl.BlockSpec(memory_space=pltpu.SMEM), pl.BlockSpec(memory_space=pl.ANY)],
+        out_specs=[vspec] * len(starts),
+        scratch_shapes=[pltpu.VMEM((rows, d), BF16), pltpu.SemaphoreType.DMA((8,))],
+        cost_estimate=pl.CostEstimate(flops=2 * total * rows * d, bytes_accessed=2 * (rows + total) * d, transcendentals=0),
+    )(pos, meta, src)
+
+
+def _dwp_kernel(n, first, idx_ref, *refs):
+    xc, yc = refs[:2 * n], refs[2 * n:4 * n]
+    w1, w3, w2 = refs[4 * n:4 * n + 3]
+    o1, o3, o2 = refs[-17:-14]
+    x, y, xm, w13, w2s, dh, a, acc13, acc2, wsem, xsem, ysem, msem, osem = refs[-14:]
+    el, fs, d = w2s.shape
+    hp = PACK // 2
+    rows = dh.shape[0] // n
+    gap = PACK - rows
+    f0 = pl.multiple_of(idx_ref[0] * fs, 128)
+    half = lambda j: pl.ds(j * fs, fs)
+
+    def w_copies(e):
+        return [pltpu.make_async_copy(w1.at[e, :, pl.ds(f0, fs)], w13.at[e, :, half(0)], wsem.at[0, e]),
+                pltpu.make_async_copy(w3.at[e, :, pl.ds(f0, fs)], w13.at[e, :, half(1)], wsem.at[1, e]),
+                pltpu.make_async_copy(w2.at[e, pl.ds(f0, fs), :], w2s.at[e], wsem.at[2, e])]
+
+    def prev_copies(e):
+        return [pltpu.make_async_copy(o1.at[e], acc13.at[e, :, half(0)], wsem.at[3, e]),
+                pltpu.make_async_copy(o3.at[e], acc13.at[e, :, half(1)], wsem.at[4, e]),
+                pltpu.make_async_copy(o2.at[e], acc2.at[e], wsem.at[5, e])]
+
+    def row_copies(c, s, refs_s):
+        lo, hi = refs_s
+        at = lambda k: pl.ds(pl.multiple_of(s * PACK + k * hp, 128), hp)
+        sem = xsem if c is x else ysem
+        cps = [pltpu.make_async_copy(lo.at[pl.ds(0, hp)], c.at[at(0)], sem.at[0, s]),
+               pltpu.make_async_copy(hi, c.at[at(1)], sem.at[1, s])]
+        if c is x:
+            cps.append(pltpu.make_async_copy(lo.at[pl.ds(hp, META)], xm.at[pl.ds(pl.multiple_of(s * META, META), META)], msem.at[s]))
+        return cps
+
+    for c in w_copies(0):
+        c.start()
+    for s in range(n):
+        for c in row_copies(x, s, xc[2 * s:2 * s + 2]) + row_copies(y, s, yc[2 * s:2 * s + 2]):
+            c.start()
+    for c in w_copies(1):
+        c.start()
+    if not first:
+        for e in range(el):
+            for c in prev_copies(e):
+                c.start()
+
+    per = rows // 128
+
+    def expert_body(e, _):
+        off = e * gap
+        sign = (1 - 2 * e).astype(F32)
+        for c in w_copies(e):
+            c.wait()
+
+        def rows_body(i, _):
+            s = i // per
+            t = i - s * per
+
+            @pl.when((e == 0) & (t == 0))
+            def _():
+                for c in row_copies(x, s, xc[:2]) + row_copies(y, s, yc[:2]):
+                    c.wait()
+
+            r = pl.ds(pl.multiple_of(s * PACK + off + t * 128, 128), 128)
+            m = xm[pl.ds(pl.multiple_of(s * META, META), META), :fs].astype(F32)
+            cut = m[0:1, :] * 8.0 + m[1:2, :]
+            row = (lax.broadcasted_iota(jnp.int32, (128, fs), 0) + (off + t * 128)).astype(F32)
+            keep = (cut - row - 0.5) * sign > 0.0
+            h = jnp.dot(x[r, :], w13[e], preferred_element_type=F32).astype(BF16).astype(F32)
+            da = lax.dot_general(y[r, :], w2s[e], (((1,), (1,)), ((), ())),
+                                 preferred_element_type=F32).astype(BF16).astype(F32)
+            h1 = jnp.where(keep, h[:, :fs], 0.0)
+            h3 = jnp.where(keep, h[:, fs:], 0.0)
+            da = jnp.where(keep, da, 0.0)
+            sg = jax.nn.sigmoid(h1)
+            silu = h1 * sg
+            o = pl.ds(pl.multiple_of(i * 128, 128), 128)
+            a[o, :] = (silu * h3).astype(BF16)
+            dh[o, :fs] = (da * h3 * sg * (1.0 + h1 * (1.0 - sg))).astype(BF16)
+            dh[o, fs:] = (da * silu).astype(BF16)
+            return 0
+
+        lax.fori_loop(0, per * n, rows_body, 0)
+        if not first:
+            for c in prev_copies(e):
+                c.wait()
+
+        def win(ref, s, cols):
+            return ref[pl.ds(pl.multiple_of(s * PACK + off, 128), rows), cols]
+
+        def acc(ref, m, parts):
+            val = parts[0]
+            for p in parts[1:]:
+                val = val + p
+            if first:
+                ref[e, m, :] = val
+            else:
+                ref[e, m, :] += val
+
+        def d13_body(i, _):
+            m = pl.ds(pl.multiple_of(i * 128, 128), 128)
+            acc(acc13, m, [lax.dot_general(win(x, s, m), dh[s * rows:(s + 1) * rows, :], (((0,), (0,)), ((), ())),
+                                           preferred_element_type=F32) for s in range(n)])
+            pltpu.make_async_copy(acc13.at[e, m, half(0)], o1.at[e, m], osem.at[0]).start()
+            pltpu.make_async_copy(acc13.at[e, m, half(1)], o3.at[e, m], osem.at[1]).start()
+            return 0
+
+        lax.fori_loop(0, d // 128, d13_body, 0)
+
+        def d2_body(i, _):
+            m = pl.ds(pl.multiple_of(i * 128, 128), 128)
+            acc(acc2, m, [lax.dot_general(a[s * rows:(s + 1) * rows, m], win(y, s, slice(None)), (((0,), (0,)), ((), ())),
+                                          preferred_element_type=F32) for s in range(n)])
+            pltpu.make_async_copy(acc2.at[e, m], o2.at[e, m], osem.at[2]).start()
+            return 0
+
+        lax.fori_loop(0, fs // 128, d2_body, 0)
+        return 0
+
+    lax.fori_loop(0, el, expert_body, 0)
+    for e in range(el):
+        pltpu.make_async_copy(acc13.at[e, :, half(0)], o1.at[e], osem.at[0]).wait()
+        pltpu.make_async_copy(acc13.at[e, :, half(1)], o3.at[e], osem.at[1]).wait()
+        pltpu.make_async_copy(acc2.at[e], o2.at[e], osem.at[2]).wait()
+
+
+def _dwp_call(idx, xs, ys, rows, w1, w3, w2, prev):
+    el, d, f = w1.shape
+    n = len(xs)
+    fs = f // 8
+    anyspec = pl.BlockSpec(memory_space=pl.ANY)
+    outs = [jax.ShapeDtypeStruct((el, d, fs), F32), jax.ShapeDtypeStruct((el, d, fs), F32),
+            jax.ShapeDtypeStruct((el, fs, d), F32)]
+    args = [idx, *(c for p in xs for c in p), *(c for p in ys for c in p), w1, w3, w2]
+    alias = {}
+    if prev is not None:
+        alias = {len(args) + i: i for i in range(3)}
+        args += list(prev)
+    return pl.pallas_call(
+        functools.partial(_dwp_kernel, n, prev is None),
+        out_shape=outs,
+        in_specs=[pl.BlockSpec(memory_space=pltpu.SMEM)] + [anyspec] * (len(args) - 1),
+        out_specs=[anyspec] * 3,
+        scratch_shapes=[
+            pltpu.VMEM((n * PACK, d), BF16),
+            pltpu.VMEM((n * PACK, d), BF16),
+            pltpu.VMEM((n * META, d), BF16),
+            pltpu.VMEM((el, d, 2 * fs), BF16),
+            pltpu.VMEM((el, fs, d), BF16),
+            pltpu.VMEM((n * rows, 2 * fs), BF16),
+            pltpu.VMEM((n * rows, fs), BF16),
+            pltpu.VMEM((el, d, 2 * fs), F32),
+            pltpu.VMEM((el, fs, d), F32),
+            pltpu.SemaphoreType.DMA((6, el)),
+            pltpu.SemaphoreType.DMA((2, n)),
+            pltpu.SemaphoreType.DMA((2, n)),
+            pltpu.SemaphoreType.DMA((n,)),
+            pltpu.SemaphoreType.DMA((3,)),
+        ],
+        input_output_aliases=alias,
+        cost_estimate=pl.CostEstimate(flops=24 * n * rows * d * fs, bytes_accessed=n * 4 * 2**20 + 18 * 2**20,
+                                      transcendentals=2 * n * rows * fs),
+    )(*args)
 
 
 def _dw_kernel(e, n, first, idx_ref, *refs):
@@ -173,22 +387,36 @@
         cap = xd.shape[1] // np_
         idx = lax.axis_index('data').astype(jnp.int32).reshape(1)
 
+        used = (jnp.max(jnp.abs(xd.astype(F32)), axis=-1) > 0.0).astype(BF16)
+        rows = xd.shape[1]
+        at = lax.broadcasted_iota(jnp.int32, (rows, rows), 0)
+        to = lax.broadcasted_iota(jnp.int32, (rows, rows), 1)
+        rank = jnp.dot(used, (at < to).astype(BF16), preferred_element_type=F32)
+        count = jnp.sum(used.astype(F32), axis=1)
+        room = PACK - count[0]
+        back = jnp.where(rank[1] < room, PACK - 1 - rank[1], PACK + rank[1] - room)
+        pos = jnp.where(used > 0, jnp.stack([rank[0], back]), -1.0).reshape(1, el * rows)
+        cut = jnp.stack([jnp.floor(count[0] / 8.0), count[0] - 8.0 * jnp.floor(count[0] / 8.0)])
+        halves = ((0, PACK // 2, True), (PACK // 2, PACK // 2, False))
+
         def chain(c, last_right):
             r, l = [c], [c]
             for _ in range(3):
-                r.append(lax.ppermute(r[-1], 'data', RIGHT))
-                l.append(lax.ppermute(l[-1], 'data', LEFT))
-            r.append(lax.ppermute(r[3], 'data', RIGHT) if last_right else lax.ppermute(l[3], 'data', LEFT))
+                r.append([lax.ppermute(v, 'data', RIGHT) for v in r[-1]])
+                l.append([lax.ppermute(v, 'data', LEFT) for v in l[-1]])
+            perm, last = (RIGHT, r[3]) if last_right else (LEFT, l[3])
+            r.append([lax.ppermute(v, 'data', perm) for v in last])
             return r, l
 
-        xch = [chain(xd[e], True) for e in range(el)]
+        xr, xl = chain(_pack(xd, pos, jnp.append(cut, 0.0), halves), True)
+        over = lax.pmax((count[0] + count[1] > PACK).astype(F32), 'expert')
 
         v = (gates[:, :, None] * dy.astype(F32)[:, None, :]).astype(BF16)
         col = jnp.where(slot >= 0, slot, cap)
         send = jnp.zeros((np_ * el, cap, d), BF16).at[topk_idx, col].set(v, mode='drop')
         recv = lax.all_to_all(send.reshape(np_, el, cap, d), 'expert', 0, 0, tiled=True)
         dyd = jnp.swapaxes(recv, 0, 1).reshape(el, np_ * cap, d)
-        ych = [chain(dyd[e], False) for e in range(el)]
+        yr, yl = chain(_pack(recv, pos, jnp.stack([over, over, over]), halves), False)
         dg = jnp.einsum('tkd,td->tk', yd, dy, preferred_element_type=F32)
 
         h1f = h1.astype(F32)
@@ -206,11 +434,27 @@
         dx = jnp.sum(jnp.where((slot >= 0)[:, :, None], got, 0.0), axis=1).astype(BF16)
 
         acc = None
-        steps = (lambda r, l: (r[0], r[1]), lambda r, l: (l[1], r[2]),
-                 lambda r, l: (l[2], r[3], l[3]), lambda r, l: (r[4],))
-        for k, pick in enumerate(steps):
-            for e in range(el):
-                acc = _dw_call(e, idx, pick(*xch[e]), pick(*ych[e]), w1, w3, w2, acc, k == 0)
+        for pick in (lambda r, l: (r[0], r[1], l[1]), lambda r, l: (r[2], l[2]),
+                     lambda r, l: (r[3], l[3]), lambda r, l: (r[4],)):
+            acc = _dwp_call(idx, pick(xr, xl), pick(yr, yl), rows, w1, w3, w2, acc)
+
+        flags = [c[0][PACK // 2, 0] for c in yr + yl[1:]]
+        some = functools.reduce(jnp.maximum, flags) > 0
+        rest = ((PACK, el * rows - PACK, False),)
+
+        def spill(acc):
+            zero = jnp.zeros(3, F32)
+            xo, = _pack(xd, pos, zero, rest)
+            yo, = _pack(recv, pos, zero, rest)
+
+            def hop(_, st):
+                xo, yo, acc = st
+                acc = _dw_call(1, idx, [xo], [yo], w1, w3, w2, acc, False)
+                return lax.ppermute(xo, 'data', RIGHT), lax.ppermute(yo, 'data', RIGHT), tuple(acc)
+
+            return lax.fori_loop(0, 8, hop, (xo, yo, acc))[2]
+
+        acc = lax.cond(some, spill, lambda acc: acc, tuple(acc))
         dw1, dw3, dw2 = acc
         return dx, dg, dw1, dw3, dw2
 

time: 330 us -> 351 us (1.064)
  waiting for transfers between devices: 116 us -> 69.9 us
  local copies, waits for them, and re-layouts: 14.4 us -> 38.8 us
  Pallas kernels: 97.8 us -> 112 us
  blocking collectives: 0 us -> 8.2 us
  between operations: 1.09 us -> 9.27 us
  starting transfers between devices: 41.6 us -> 48 us
  other arithmetic: 13.6 us -> 18.3 us
    ppermute x28, waiting for transfers between devices: 116 us -> 69.9 us  [the longest x12 32.3 us: chain(): r.append([lax.ppermute(v, 'data', RIGHT) for v in r[-1]])]
    gather x1, local copies, waits for them, and re-layouts: 8.79 us -> 23.8 us  [body(): got = back[topk_idx, jnp.minimum(col, cap - 1)].astype(F32)]
    pallas_call x8 -> x6, Pallas kernels: 97.8 us -> 112 us  [the longest x4 97.3 us: _dwp_call(): pl.pallas_call(functools.partial(_dwp_kernel, n, prev is None), out_shape...]
    slice x1 -> x9, local copies, waits for them, and re-layouts: 1.39 us -> 10.1 us  [the longest x8 9.47 us: body(): flags = [c[0][PACK // 2, 0] for c in yr + yl[1:]]]
    pmax x0 -> x1, blocking collectives: none -> 8.2 us  [body(): over = lax.pmax((count[0] + count[1] > PACK).astype(F32), 'expert')]
    ppermute x28, starting transfers between devices: 33.6 us -> 39.4 us  [the longest x12 18.6 us: chain(): r.append([lax.ppermute(v, 'data', RIGHT) for v in r[-1]])]
    unnamed x3 -> x4, other arithmetic: 8.1 us -> 8.12 us
  transfers between devices with their start and end apart: 30 -> 30, of which waited for: 13 -> 5; matrix products, arithmetic and copies ran while one was open for 19% -> 26% of each run, Pallas kernels for 27% -> 27%
where the time goes in v1:
time: 351 us; the launch traced here: 350 us
  Pallas kernels  112 us (32%)
  waiting for transfers between devices  69.9 us (20%)
  starting transfers between devices  48 us (14%)
  matrix products  45.7 us (13%)
  local copies, waits for them, and re-layouts  38.8 us (11%)
  other arithmetic  18.3 us (5%)
  between operations  9.27 us (3%)
  blocking collectives  8.2 us (2%)
    pallas_call x4, Pallas kernels, _dwp_call(): pl.pallas_call(functools.partial(_dwp_kernel, n, prev is None), out_shape...  97.3 us
    ppermute x12, waiting for transfers between devices, chain(): r.append([lax.ppermute(v, 'data', RIGHT) for v in r[-1]])  32.3 us
    ppermute x12, waiting for transfers between devices, chain(): l.append([lax.ppermute(v, 'data', LEFT) for v in l[-1]])  30.1 us
    gather x1, local copies, waits for them, and re-layouts, body(): got = back[topk_idx, jnp.minimum(col, cap - 1)].astype(F32)  23.8 us
    ppermute x12, starting transfers between devices, chain(): r.append([lax.ppermute(v, 'data', RIGHT) for v in r[-1]])  18.6 us
    dot_general x1, matrix products, body(): jnp.einsum('ecf,edf->ecd', dh1, w1, preferred_element_type=F32)  18.3 us
    ppermute x12, starting transfers between devices, chain(): l.append([lax.ppermute(v, 'data', LEFT) for v in l[-1]])  18.2 us
    dot_general x1, matrix products, body(): jnp.einsum('ecf,edf->ecd', dh3, w3, preferred_element_type=F32)  15.1 us
  transfers between devices with their start and end apart: 30, of which 5 were waited for; matrix products, arithmetic and copies ran while one was open for 26% of the time, Pallas kernels for 27%

profile of v1, /device:TPU:0, one launch (start us, length us, event | category | flops | bytes accessed | tf_op | source)
XLA Modules:
  0.0 349.9 jit_solution(1896053407944187130)
XLA Ops:
  2.9 7.3 %scatter_custom_fusion = bf16[1280,768]{1,0:T(8,128)(2,1)} fusion(s32[1024]{0:T(1024)S(1)} %broadcast_select_fusion, bf16[1024,768]{1,0:T(8,128)(2,1)} %param.15, f32[1024]{0:T(1024)} %bitcast.43, bf16[]{:T(256)} %constant.6.clone.1), kind=kCustom, calls=%fused_computation.29 | custom fusion | flops 2359296 | bytes 3543042
  10.2 4.2 %all-to-all-start = ((bf16[4,2,160,768]{3,2,1,0:T(8,128)(2,1)}), bf16[4,2,160,768]{3,2,1,0:T(8,128)(2,1)S(1)}, u32[]{:S(2)}, u32[]{:S(2)}) async-start(bf16[4,2,160,768]{3,2,1,0:T(8,128)(2,1)} %bitcast.37), calls=%async_computation | async-start | bytes 3932160 | tf_op jit(solution)/shard_map/all_to_all | solution.py:417
  14.4 2.0 abs_reduce_fusion
  20.0 6.7 %shard_map.147 = (bf16[528,768]{1,0:T(8,128)(2,1)}, bf16[512,768]{1,0:T(8,128)(2,1)}) custom-call(f32[1,1280]{1,0:T(1,128)S(1)} %bitcast.40, f32[3]{0:T(128)} %pad_maximum_fusion.meta_ref, bf16[2,640,768]{2,1,0:T(8,128)(2,1)} %src_ref.1), custom_call_target="tpu_custom_call" | custom-call | flops 2013265920 | bytes 3538944 | tf_op jit(solution)/shard_map/pallas_call | solution.py:61
  26.8 2.5 collective-permute-start.9
  29.2 1.6 collective-permute-start.13
  32.6 8.2 %pmax.7 = f32[]{:T(128)} all-reduce(f32[]{:T(128)S(6)} %convert_element_type.82), channel_id=1, replica_groups=mesh['data'=8,'expert'=4] {'expert'}, use_global_device_ids=true, to_apply=%region_3.4 | all-reduce | flops 1 | bytes 8 | tf_op jit(solution)/shard_map/pmax | solution.py:412
  40.9 3.0 fusion.13
  43.8 21.2 %collective-permute-done.13.refs_3_ = bf16[512,768]{1,0:T(8,128)(2,1)} collective-permute-done((bf16[512,768]{1,0:T(8,128)(2,1)}, bf16[512,768]{1,0:T(8,128)(2,1)}, u32[]{:S(2)}, u32[]{:S(2)}) %collective-permute-start.13) | collective-permute-done | bytes 786464 | tf_op jit(solution)/shard_map/ppermute | solution.py:405
  65.1 1.8 collective-permute-start.14
  67.1 1.8 collective-permute-start.10
  68.9 1.2 stack.18.meta_ref
  70.0 7.6 %shard_map.146 = (bf16[528,768]{1,0:T(8,128)(2,1)}, bf16[512,768]{1,0:T(8,128)(2,1)}) custom-call(f32[1,1280]{1,0:T(1,128)S(1)} %bitcast.41, f32[3]{0:T(128)} %stack.18.meta_ref, bf16[4,2,160,768]{3,2,1,0:T(8,128)(2,1)S(1)} %all-to-all-done.src_ref), custom_call_target="tpu_custom_call" | custom-call | flops 2013265920 | bytes 3538944 | tf_op jit(solution)/shard_map/pallas_call | solution.py:61
  77.7 1.6 collective-permute-start.2
  79.5 12.2 %convolution_convert_fusion = bf16[2,640,3072]{2,1,0:T(8,128)(2,1)} fusion(bf16[2,640,768]{2,1,0:T(8,128)(2,1)S(1)} %bitcast.39, bf16[2,3072,768]{2,1,0:T(8,128)(2,1)} %refs_6_.1), kind=kOutput, calls=%fused_computation.17 | convolution fusion | flops 6043729920 | bytes 19267584 | tf_op jit(solution)/shard_map/ecd,efd->ecf/dot_general | solution.py:426
  92.1 15.1 %fusion.8 = f32[2,640,768]{2,1,0:T(8,128)} fusion(bf16[2,768,3072]{2,1,0:T(8,128)(2,1)} %refs_5_.1, bf16[2,640,3072]{2,1,0:T(8,128)(2,1)} %convolution_convert_fusion, bf16[2,640,3072]{2,1,0:T(8,128)(2,1)} %param.21), kind=kOutput, calls=%fused_computation.15 | convolution fusion | flops 6071255040 | bytes 29097984 | tf_op jit(solution)/shard_map/ecf,edf->ecd/dot_general | solution.py:430
  107.4 1.7 collective-permute-start.17
  109.5 11.1 %collective-permute-done.2.refs_8_ = bf16[528,768]{1,0:T(8,128)(2,1)} collective-permute-done((bf16[528,768]{1,0:T(8,128)(2,1)}, bf16[528,768]{1,0:T(8,128)(2,1)}, u32[]{:S(2)}, u32[]{:S(2)}) %collective-permute-start.2) | collective-permute-done | bytes 811040 | tf_op jit(solution)/shard_map/ppermute | solution.py:405
  120.5 1.8 collective-permute-start.3
  122.6 18.3 %add_convert_fusion = bf16[2,640,768]{2,1,0:T(8,128)(2,1)S(1)} fusion(f32[2,640,768]{2,1,0:T(8,128)} %fusion.8, bf16[2,768,3072]{2,1,0:T(8,128)(2,1)} %refs_4_.1, bf16[2,640,3072]{2,1,0:T(8,128)(2,1)} %convolution_convert_fusion, bf16[2,640,3072]{2,1,0:T(8,128)(2,1)} %param.21, bf16[2,640,3072]{2,1,0:T(8,128)(2,1)} %param.22), kind=kOutput, calls=%fused_computation.19 | convolution fusion | flops 6092881920 | bytes 38928384 | tf_op jit(solution)/shard_map/ecf,edf->ecd/dot_general | solution.py:429
  140.8 1.4 copy.40
  142.2 4.4 %all-to-all-start.1 = ((bf16[4,2,160,768]{3,2,1,0:T(8,128)(2,1)}), bf16[4,2,160,768]{3,2,1,0:T(8,128)(2,1)}, u32[]{:S(2)}, u32[]{:S(2)}) async-start(bf16[4,2,160,768]{3,2,1,0:T(8,128)(2,1)} %bitcast.34), calls=%async_computation.1 | async-start | bytes 3932160 | tf_op jit(solution)/shard_map/all_to_all | solution.py:432
  146.7 1.2 slice.46
  147.9 1.8 collective-permute-start.15
  150.0 1.8 collective-permute-start.28
  151.8 11.9 %collective-permute-done.6.refs_6_ = bf16[528,768]{1,0:T(8,128)(2,1)} collective-permute-done((bf16[528,768]{1,0:T(8,128)(2,1)}, bf16[528,768]{1,0:T(8,128)(2,1)}, u32[]{:S(2)}, u32[]{:S(2)}) %collective-permute-start.6) | collective-permute-done | bytes 811040 | tf_op jit(solution)/shard_map/ppermute | solution.py:406
  164.1 1.6 collective-permute-start.4
  165.7 33.0 %shard_map.148 = (f32[2,768,384]{2,1,0:T(8,128)S(1)}, f32[2,768,384]{2,1,0:T(8,128)}, f32[2,384,768]{2,1,0:T(8,128)}) custom-call(s32[1]{0:T(128)} %bitcast.17.idx_ref, bf16[528,768]{1,0:T(8,128)(2,1)} %get-tuple-element.118.refs_0_, bf16[512,768]{1,0:T(8,128)(2,1)} %get-tuple-element.119.refs_1_, bf16[528,768]{1,0:T(8,128)(2,1)} %collective-permute-done.9.refs_2_, ...), custom_call_target="tpu_custom_call" | custom-call | flops 13589544960 | bytes 31457280 | tf_op jit(solution)/shard_map/pallas_call | solution.py:207
  198.7 1.2 slice.60
  201.2 1.2 slice.64
  202.4 23.8 %gather_fusion = bf16[1024,768]{1,0:T(8,128)(2,1)} fusion(bf16[8,160,768]{2,1,0:T(8,128)(2,1)} %bitcast.8, s32[1024]{0:T(1024)S(1)} %bitcast.35), kind=kCustom, calls=%fused_computation | custom fusion | bytes 3153920 | tf_op jit(solution)/shard_map/gather | solution.py:433
  226.2 2.9 fusion.14
  229.1 1.1 slice.61
  230.9 1.2 slice.65
  232.1 12.2 %collective-permute-start.26 = (bf16[512,768]{1,0:T(8,128)(2,1)}, bf16[512,768]{1,0:T(8,128)(2,1)}, u32[]{:S(2)}, u32[]{:S(2)}) collective-permute-start(bf16[512,768]{1,0:T(8,128)(2,1)} %collective-permute-done.25.refs_3_), channel_id=1, source_target_pairs={{8,0},{16,8},{24,16},{28,24},{20,28},{12,20},{4,12},{0,4},{9,1},{1... | collective-permute-start | bytes 2359304 | tf_op jit(solution)/shard_map/ppermute | solution.py:406
  244.3 2.0 collective-permute-start.23
  246.3 2.0 collective-permute-start.29
  248.3 24.1 %shard_map.149 = (f32[2,768,384]{2,1,0:T(8,128)S(1)}, f32[2,768,384]{2,1,0:T(8,128)}, f32[2,384,768]{2,1,0:T(8,128)}) custom-call(s32[1]{0:T(128)} %bitcast.17.idx_ref, bf16[528,768]{1,0:T(8,128)(2,1)} %copy-done.4, bf16[512,768]{1,0:T(8,128)(2,1)} %collective-permute-done.14.refs_1_, ...), custom_call_target="tpu_custom_call", output_to_operand_aliasing={{0}: (12, {}), {1}: (13, {}), {2}: (14, {})} | custom-call | flops 9059696640 | bytes 27262976 | tf_op jit(solution)/shard_map/pallas_call | solution.py:207
  272.4 1.2 slice.62
  274.2 1.2 slice.66
  275.5 18.2 %collective-permute-done.19.refs_7_ = bf16[512,768]{1,0:T(8,128)(2,1)} collective-permute-done((bf16[512,768]{1,0:T(8,128)(2,1)}, bf16[512,768]{1,0:T(8,128)(2,1)}, u32[]{:S(2)}, u32[]{:S(2)}) %collective-permute-start.19) | collective-permute-done | bytes 786464 | tf_op jit(solution)/shard_map/ppermute | solution.py:406
  293.7 2.5 collective-permute-start.20
  296.2 24.0 %shard_map.150 = (f32[2,768,384]{2,1,0:T(8,128)S(1)}, f32[2,768,384]{2,1,0:T(8,128)}, f32[2,384,768]{2,1,0:T(8,128)}) custom-call(s32[1]{0:T(128)} %bitcast.17.idx_ref, bf16[528,768]{1,0:T(8,128)(2,1)} %collective-permute-done.11.refs_0_, ...), custom_call_target="tpu_custom_call", output_to_operand_aliasing={{0}: (12, {}), {1}: (13, {}), {2}: (14, {})} | custom-call | flops 9059696640 | bytes 27262976 | tf_op jit(solution)/shard_map/pallas_call | solution.py:207
  320.3 7.4 %collective-permute-done.8.refs_2_ = bf16[528,768]{1,0:T(8,128)(2,1)} collective-permute-done((bf16[528,768]{1,0:T(8,128)(2,1)}, bf16[528,768]{1,0:T(8,128)(2,1)}, u32[]{:S(2)}, u32[]{:S(2)}) %collective-permute-start.8) | collective-permute-done | bytes 811040 | tf_op jit(solution)/shard_map/ppermute | solution.py:408
  327.7 1.1 slice.63
  331.4 0.9 copy-done.5
  332.3 16.2 %shard_map.151 = (f32[2,768,384]{2,1,0:T(8,128)S(1)}, f32[2,768,384]{2,1,0:T(8,128)}, f32[2,384,768]{2,1,0:T(8,128)}) custom-call(s32[1]{0:T(128)} %bitcast.17.idx_ref, bf16[528,768]{1,0:T(8,128)(2,1)} %copy-done.5, bf16[512,768]{1,0:T(8,128)(2,1)} %collective-permute-done.16.refs_1_, ...), custom_call_target="tpu_custom_call", output_to_operand_aliasing={{0}: (8, {}), {1}: (9, {}), {2}: (10, {})} | custom-call | flops 4529848320 | bytes 23068672 | tf_op jit(solution)/shard_map/pallas_call | solution.py:207
  348.5 1.4 copy-done
  (64 shorter events, 6.8 us)
Async XLA Ops:
  10.2 58.7 %all-to-all-start = ((bf16[4,2,160,768]{3,2,1,0:T(8,128)(2,1)}), bf16[4,2,160,768]{3,2,1,0:T(8,128)(2,1)S(1)}, u32[]{:S(2)}, u32[]{:S(2)}) async-start(bf16[4,2,160,768]{3,2,1,0:T(8,128)(2,1)} %bitcast.37), calls=%async_computation | async-start | bytes 3932160 | tf_op jit(solution)/shard_map/all_to_all | solution.py:417
  20.0 20.8 %copy-start.6 = (s32[1024,1]{0,1:T(1,128)S(1)}, s32[1024,1]{0,1:T(1,128)}, u32[]{:S(2)}) copy-start(s32[1024,1]{0,1:T(1,128)} %param.18) | copy-start | bytes 12292
  26.8 40.3 %collective-permute-start.9 = (bf16[528,768]{1,0:T(8,128)(2,1)}, bf16[528,768]{1,0:T(8,128)(2,1)}, u32[]{:S(2)}, u32[]{:S(2)}) collective-permute-start(bf16[528,768]{1,0:T(8,128)(2,1)} %get-tuple-element.118.refs_0_), channel_id=1, source_target_pairs={{0,8},{8,16},{16,24},{24,28},{28,20},{20,12},{12,4},{4,0},{1,9},{9... | collective-permute-start | bytes 2433032 | tf_op jit(solution)/shard_map/ppermute | solution.py:405
  29.2 35.8 %collective-permute-start.13 = (bf16[512,768]{1,0:T(8,128)(2,1)}, bf16[512,768]{1,0:T(8,128)(2,1)}, u32[]{:S(2)}, u32[]{:S(2)}) collective-permute-start(bf16[512,768]{1,0:T(8,128)(2,1)} %get-tuple-element.119.refs_1_), channel_id=1, source_target_pairs={{0,8},{8,16},{16,24},{24,28},{28,20},{20,12},{12,4},{4,0},{1,9},{9... | collective-permute-start | bytes 2359304 | tf_op jit(solution)/shard_map/ppermute | solution.py:405
  30.8 36.0 %collective-permute-start.24 = (bf16[512,768]{1,0:T(8,128)(2,1)}, bf16[512,768]{1,0:T(8,128)(2,1)}, u32[]{:S(2)}, u32[]{:S(2)}) collective-permute-start(bf16[512,768]{1,0:T(8,128)(2,1)} %get-tuple-element.119.refs_1_), channel_id=1, source_target_pairs={{8,0},{16,8},{24,16},{28,24},{20,28},{12,20},{4,12},{0,4},{9,1},{1... | collective-permute-start | bytes 2359304 | tf_op jit(solution)/shard_map/ppermute | solution.py:406
  32.6 59.1 %collective-permute-start.21 = (bf16[528,768]{1,0:T(8,128)(2,1)}, bf16[528,768]{1,0:T(8,128)(2,1)}, u32[]{:S(2)}, u32[]{:S(2)}) collective-permute-start(bf16[528,768]{1,0:T(8,128)(2,1)} %get-tuple-element.118.refs_0_), channel_id=1, source_target_pairs={{8,0},{16,8},{24,16},{28,24},{20,28},{12,20},{4,12},{0,4},{9,1},{1... | collective-permute-start | bytes 2433032 | tf_op jit(solution)/shard_map/ppermute | solution.py:406
  65.1 42.1 %collective-permute-start.14 = (bf16[512,768]{1,0:T(8,128)(2,1)}, bf16[512,768]{1,0:T(8,128)(2,1)}, u32[]{:S(2)}, u32[]{:S(2)}) collective-permute-start(bf16[512,768]{1,0:T(8,128)(2,1)} %collective-permute-done.13.refs_3_), channel_id=1, source_target_pairs={{0,8},{8,16},{16,24},{24,28},{28,20},{20,12},{12,4},{4,0},{1,9},{9... | collective-permute-start | bytes 2359304 | tf_op jit(solution)/shard_map/ppermute | solution.py:405
  66.9 40.6 %collective-permute-start.25 = (bf16[512,768]{1,0:T(8,128)(2,1)}, bf16[512,768]{1,0:T(8,128)(2,1)}, u32[]{:S(2)}, u32[]{:S(2)}) collective-permute-start(bf16[512,768]{1,0:T(8,128)(2,1)} %collective-permute-done.24.refs_5_), channel_id=1, source_target_pairs={{8,0},{16,8},{24,16},{28,24},{20,28},{12,20},{4,12},{0,4},{9,1},{1... | collective-permute-start | bytes 2359304 | tf_op jit(solution)/shard_map/ppermute | solution.py:406
  67.1 42.1 %collective-permute-start.10 = (bf16[528,768]{1,0:T(8,128)(2,1)}, bf16[528,768]{1,0:T(8,128)(2,1)S(1)}, u32[]{:S(2)}, u32[]{:S(2)}) collective-permute-start(bf16[528,768]{1,0:T(8,128)(2,1)} %collective-permute-done.9.refs_2_), channel_id=1, source_target_pairs={{0,8},{8,16},{16,24},{24,28},{28,20},{20,12},{12,4},{4,0},{1,9},{9... | collective-permute-start | bytes 2433032 | tf_op jit(solution)/shard_map/ppermute | solution.py:405
  68.9 10.4 %copy-start.3 = (bf16[4,2,160,768]{3,2,1,0:T(8,128)(2,1)}, bf16[4,2,160,768]{3,2,1,0:T(8,128)(2,1)S(1)}, u32[]{:S(2)}) copy-start(bf16[4,2,160,768]{3,2,1,0:T(8,128)(2,1)S(1)} %all-to-all-done.src_ref) | copy-start | bytes 5898244
  77.7 42.9 %collective-permute-start.2 = (bf16[528,768]{1,0:T(8,128)(2,1)}, bf16[528,768]{1,0:T(8,128)(2,1)}, u32[]{:S(2)}, u32[]{:S(2)}) collective-permute-start(bf16[528,768]{1,0:T(8,128)(2,1)} %get-tuple-element.117.refs_6_), channel_id=1, source_target_pairs={{0,8},{8,16},{16,24},{24,28},{28,20},{20,12},{12,4},{4,0},{1,9},{9... | collective-permute-start | bytes 2433032 | tf_op jit(solution)/shard_map/ppermute | solution.py:405
  79.4 12.2 %copy-start.7 = (bf16[528,768]{1,0:T(8,128)(2,1)S(1)}, bf16[528,768]{1,0:T(8,128)(2,1)}, u32[]{:S(2)}) copy-start(bf16[528,768]{1,0:T(8,128)(2,1)} %get-tuple-element.117.refs_6_) | copy-start | bytes 2433028
  91.6 30.7 %collective-permute-start.5 = (bf16[528,768]{1,0:T(8,128)(2,1)S(1)}, bf16[528,768]{1,0:T(8,128)(2,1)}, u32[]{:S(2)}, u32[]{:S(2)}) collective-permute-start(bf16[528,768]{1,0:T(8,128)(2,1)S(1)} %copy-done.7), channel_id=1, source_target_pairs={{8,0},{16,8},{24,16},{28,24},{20,28},{12,20},{4,12},{0,4},{9,1},{1... | collective-permute-start | bytes 2433032 | tf_op jit(solution)/shard_map/ppermute | solution.py:406
  107.2 40.7 %collective-permute-start.22 = (bf16[528,768]{1,0:T(8,128)(2,1)}, bf16[528,768]{1,0:T(8,128)(2,1)}, u32[]{:S(2)}, u32[]{:S(2)}) collective-permute-start(bf16[528,768]{1,0:T(8,128)(2,1)} %collective-permute-done.21.refs_4_), channel_id=1, source_target_pairs={{8,0},{16,8},{24,16},{28,24},{20,28},{12,20},{4,12},{0,4},{9,1},{1... | collective-permute-start | bytes 2433032 | tf_op jit(solution)/shard_map/ppermute | solution.py:406
  107.4 42.3 %collective-permute-start.17 = (bf16[512,768]{1,0:T(8,128)(2,1)}, bf16[512,768]{1,0:T(8,128)(2,1)}, u32[]{:S(2)}, u32[]{:S(2)}) collective-permute-start(bf16[512,768]{1,0:T(8,128)(2,1)} %get-tuple-element.120.refs_7_), channel_id=1, source_target_pairs={{8,0},{16,8},{24,16},{28,24},{20,28},{12,20},{4,12},{0,4},{9,1},{1... | collective-permute-start | bytes 2359304 | tf_op jit(solution)/shard_map/ppermute | solution.py:406
  109.2 135.1 %copy-start.4 = (bf16[528,768]{1,0:T(8,128)(2,1)}, bf16[528,768]{1,0:T(8,128)(2,1)S(1)}, u32[]{:S(2)}) copy-start(bf16[528,768]{1,0:T(8,128)(2,1)S(1)} %collective-permute-done.10.refs_0_) | copy-start | bytes 2433028
  109.2 40.8 %collective-permute-start.27 = (bf16[512,768]{1,0:T(8,128)(2,1)}, bf16[512,768]{1,0:T(8,128)(2,1)}, u32[]{:S(2)}, u32[]{:S(2)}) collective-permute-start(bf16[512,768]{1,0:T(8,128)(2,1)} %get-tuple-element.120.refs_7_), channel_id=1, source_target_pairs={{0,8},{8,16},{16,24},{24,28},{28,20},{20,12},{12,4},{4,0},{1,9},{9... | collective-permute-start | bytes 2359304 | tf_op jit(solution)/shard_map/ppermute | solution.py:405
  120.5 43.5 %collective-permute-start.3 = (bf16[528,768]{1,0:T(8,128)(2,1)}, bf16[528,768]{1,0:T(8,128)(2,1)}, u32[]{:S(2)}, u32[]{:S(2)}) collective-permute-start(bf16[528,768]{1,0:T(8,128)(2,1)} %collective-permute-done.2.refs_8_), channel_id=1, source_target_pairs={{0,8},{8,16},{16,24},{24,28},{28,20},{20,12},{12,4},{4,0},{1,9},{9... | collective-permute-start | bytes 2433032 | tf_op jit(solution)/shard_map/ppermute | solution.py:405
  122.3 41.3 %collective-permute-start.6 = (bf16[528,768]{1,0:T(8,128)(2,1)}, bf16[528,768]{1,0:T(8,128)(2,1)}, u32[]{:S(2)}, u32[]{:S(2)}) collective-permute-start(bf16[528,768]{1,0:T(8,128)(2,1)} %collective-permute-done.5.refs_10_), channel_id=1, source_target_pairs={{8,0},{16,8},{24,16},{28,24},{20,28},{12,20},{4,12},{0,4},{9,1},{1... | collective-permute-start | bytes 2433032 | tf_op jit(solution)/shard_map/ppermute | solution.py:406
  142.2 60.2 %all-to-all-start.1 = ((bf16[4,2,160,768]{3,2,1,0:T(8,128)(2,1)}), bf16[4,2,160,768]{3,2,1,0:T(8,128)(2,1)}, u32[]{:S(2)}, u32[]{:S(2)}) async-start(bf16[4,2,160,768]{3,2,1,0:T(8,128)(2,1)} %bitcast.34), calls=%async_computation.1 | async-start | bytes 3932160 | tf_op jit(solution)/shard_map/all_to_all | solution.py:432
  147.9 84.1 %collective-permute-start.15 = (bf16[512,768]{1,0:T(8,128)(2,1)}, bf16[512,768]{1,0:T(8,128)(2,1)}, u32[]{:S(2)}, u32[]{:S(2)}) collective-permute-start(bf16[512,768]{1,0:T(8,128)(2,1)} %collective-permute-done.14.refs_1_), channel_id=1, source_target_pairs={{0,8},{8,16},{16,24},{24,28},{28,20},{20,12},{12,4},{4,0},{1,9},{9... | collective-permute-start | bytes 2359304 | tf_op jit(solution)/shard_map/ppermute | solution.py:405
  149.7 94.5 %collective-permute-start.18 = (bf16[512,768]{1,0:T(8,128)(2,1)}, bf16[512,768]{1,0:T(8,128)(2,1)}, u32[]{:S(2)}, u32[]{:S(2)}) collective-permute-start(bf16[512,768]{1,0:T(8,128)(2,1)} %collective-permute-done.17.refs_11_), channel_id=1, source_target_pairs={{8,0},{16,8},{24,16},{28,24},{20,28},{12,20},{4,12},{0,4},{9,1},{1... | collective-permute-start | bytes 2359304 | tf_op jit(solution)/shard_map/ppermute | solution.py:406
  150.0 94.3 %collective-permute-start.28 = (bf16[512,768]{1,0:T(8,128)(2,1)}, bf16[512,768]{1,0:T(8,128)(2,1)}, u32[]{:S(2)}, u32[]{:S(2)}) collective-permute-start(bf16[512,768]{1,0:T(8,128)(2,1)} %collective-permute-done.27.refs_9_), channel_id=1, source_target_pairs={{0,8},{8,16},{16,24},{24,28},{28,20},{20,12},{12,4},{4,0},{1,9},{9... | collective-permute-start | bytes 2359304 | tf_op jit(solution)/shard_map/ppermute | solution.py:405
  163.7 82.6 %collective-permute-start.7 = (bf16[528,768]{1,0:T(8,128)(2,1)}, bf16[528,768]{1,0:T(8,128)(2,1)}, u32[]{:S(2)}, u32[]{:S(2)}) collective-permute-start(bf16[528,768]{1,0:T(8,128)(2,1)} %collective-permute-done.6.refs_6_), channel_id=1, source_target_pairs={{8,0},{16,8},{24,16},{28,24},{20,28},{12,20},{4,12},{0,4},{9,1},{1... | collective-permute-start | bytes 2433032 | tf_op jit(solution)/shard_map/ppermute | solution.py:406
  164.1 82.3 %collective-permute-start.4 = (bf16[528,768]{1,0:T(8,128)(2,1)}, bf16[528,768]{1,0:T(8,128)(2,1)}, u32[]{:S(2)}, u32[]{:S(2)}) collective-permute-start(bf16[528,768]{1,0:T(8,128)(2,1)} %collective-permute-done.3.refs_4_), channel_id=1, source_target_pairs={{0,8},{8,16},{16,24},{24,28},{28,20},{20,12},{12,4},{4,0},{1,9},{9... | collective-permute-start | bytes 2433032 | tf_op jit(solution)/shard_map/ppermute | solution.py:405
  232.1 43.4 %collective-permute-start.26 = (bf16[512,768]{1,0:T(8,128)(2,1)}, bf16[512,768]{1,0:T(8,128)(2,1)}, u32[]{:S(2)}, u32[]{:S(2)}) collective-permute-start(bf16[512,768]{1,0:T(8,128)(2,1)} %collective-permute-done.25.refs_3_), channel_id=1, source_target_pairs={{8,0},{16,8},{24,16},{28,24},{20,28},{12,20},{4,12},{0,4},{9,1},{1... | collective-permute-start | bytes 2359304 | tf_op jit(solution)/shard_map/ppermute | solution.py:406
  244.2 31.2 %collective-permute-start.11 = (bf16[528,768]{1,0:T(8,128)(2,1)S(1)}, bf16[528,768]{1,0:T(8,128)(2,1)}, u32[]{:S(2)}, u32[]{:S(2)}) collective-permute-start(bf16[528,768]{1,0:T(8,128)(2,1)S(1)} %collective-permute-done.10.refs_0_), channel_id=1, source_target_pairs={{0,8},{8,16},{16,24},{24,28},{28,20},{20,12},{12,4},{4,0},{1,9},{9... | collective-permute-start | bytes 2433032 | tf_op jit(solution)/shard_map/ppermute | solution.py:405
  244.3 51.9 %collective-permute-start.23 = (bf16[528,768]{1,0:T(8,128)(2,1)}, bf16[528,768]{1,0:T(8,128)(2,1)}, u32[]{:S(2)}, u32[]{:S(2)}) collective-permute-start(bf16[528,768]{1,0:T(8,128)(2,1)} %collective-permute-done.22.refs_2_), channel_id=1, source_target_pairs={{8,0},{16,8},{24,16},{28,24},{20,28},{12,20},{4,12},{0,4},{9,1},{1... | collective-permute-start | bytes 2433032 | tf_op jit(solution)/shard_map/ppermute | solution.py:406
  246.3 47.4 %collective-permute-start.19 = (bf16[512,768]{1,0:T(8,128)(2,1)}, bf16[512,768]{1,0:T(8,128)(2,1)}, u32[]{:S(2)}, u32[]{:S(2)}) collective-permute-start(bf16[512,768]{1,0:T(8,128)(2,1)} %collective-permute-done.18.refs_7_), channel_id=1, source_target_pairs={{8,0},{16,8},{24,16},{28,24},{20,28},{12,20},{4,12},{0,4},{9,1},{1... | collective-permute-start | bytes 2359304 | tf_op jit(solution)/shard_map/ppermute | solution.py:406
  246.3 49.9 %collective-permute-start.29 = (bf16[512,768]{1,0:T(8,128)(2,1)}, bf16[512,768]{1,0:T(8,128)(2,1)}, u32[]{:S(2)}, u32[]{:S(2)}) collective-permute-start(bf16[512,768]{1,0:T(8,128)(2,1)} %collective-permute-done.28.refs_5_), channel_id=1, source_target_pairs={{0,8},{8,16},{16,24},{24,28},{28,20},{20,12},{12,4},{4,0},{1,9},{9... | collective-permute-start | bytes 2359304 | tf_op jit(solution)/shard_map/ppermute | solution.py:405
  275.4 55.9 %collective-permute-start.16 = (bf16[512,768]{1,0:T(8,128)(2,1)}, bf16[512,768]{1,0:T(8,128)(2,1)}, u32[]{:S(2)}, u32[]{:S(2)}) collective-permute-start(bf16[512,768]{1,0:T(8,128)(2,1)} %collective-permute-done.15.refs_1_), channel_id=1, source_target_pairs={{0,8},{8,16},{16,24},{24,28},{28,20},{20,12},{12,4},{4,0},{1,9},{9... | collective-permute-start | bytes 2359304 | tf_op jit(solution)/shard_map/ppermute | solution.py:408
  275.5 55.9 %collective-permute-start.12 = (bf16[528,768]{1,0:T(8,128)(2,1)}, bf16[528,768]{1,0:T(8,128)(2,1)S(1)}, u32[]{:S(2)}, u32[]{:S(2)}) collective-permute-start(bf16[528,768]{1,0:T(8,128)(2,1)} %collective-permute-done.11.refs_0_), channel_id=1, source_target_pairs={{0,8},{8,16},{16,24},{24,28},{28,20},{20,12},{12,4},{4,0},{1,9},{9... | collective-permute-start | bytes 2433032 | tf_op jit(solution)/shard_map/ppermute | solution.py:408
  293.7 37.7 %collective-permute-start.20 = (bf16[512,768]{1,0:T(8,128)(2,1)}, bf16[512,768]{1,0:T(8,128)(2,1)}, u32[]{:S(2)}, u32[]{:S(2)}) collective-permute-start(bf16[512,768]{1,0:T(8,128)(2,1)} %collective-permute-done.19.refs_7_), channel_id=1, source_target_pairs={{8,0},{16,8},{24,16},{28,24},{20,28},{12,20},{4,12},{0,4},{9,1},{1... | collective-permute-start | bytes 2359304 | tf_op jit(solution)/shard_map/ppermute | solution.py:408
  296.2 31.5 %collective-permute-start.8 = (bf16[528,768]{1,0:T(8,128)(2,1)}, bf16[528,768]{1,0:T(8,128)(2,1)}, u32[]{:S(2)}, u32[]{:S(2)}) collective-permute-start(bf16[528,768]{1,0:T(8,128)(2,1)} %collective-permute-done.7.refs_6_), channel_id=1, source_target_pairs={{8,0},{16,8},{24,16},{28,24},{20,28},{12,20},{4,12},{0,4},{9,1},{1... | collective-permute-start | bytes 2433032 | tf_op jit(solution)/shard_map/ppermute | solution.py:408
  331.4 0.9 copy-start.5
  348.5 1.4 copy-start

commit v2 on v1

--- a/solution.py
+++ b/solution.py
@@ -14,23 +14,27 @@
 
 PACK = 1024
 META = 16
+TILE = 256
 RING = (0, 2, 4, 6, 7, 5, 3, 1)
 RIGHT = [(RING[i], RING[(i + 1) % 8]) for i in range(8)]
 LEFT = [(RING[(i + 1) % 8], RING[i]) for i in range(8)]
 
 
-def _pack_kernel(grouped, starts, pos_ref, meta_ref, src_ref, *refs):
+def _pack_kernel(grouped, el, starts, pos_ref, meta_ref, src_ref, *refs):
     n = len(starts)
-    outs, src, sem = refs[:n], refs[n], refs[n + 1]
+    outs, src, fl, sem = refs[:n], refs[n], refs[n + 1], refs[n + 2]
     cps = []
     if grouped:
-        np_, el, cap, _ = src_ref.shape
+        np_ = src_ref.shape[0]
+        cap = (src_ref.shape[1] - META) // el
         for p in range(np_):
             for e in range(el):
                 dst = src.at[pl.ds(e * np_ * cap + p * cap, cap)]
-                cps.append(pltpu.make_async_copy(src_ref.at[p, e], dst, sem.at[p * el + e]))
+                cps.append(pltpu.make_async_copy(src_ref.at[p, pl.ds(e * cap, cap)], dst, sem.at[p * el + e]))
+            cps.append(pltpu.make_async_copy(src_ref.at[p, pl.ds(el * cap, META)], fl.at[pl.ds(p * META, META)],
+                                             sem.at[np_ * el + p]))
     else:
-        el, rows, _ = src_ref.shape
+        rows = src_ref.shape[1]
         for e in range(el):
             cps.append(pltpu.make_async_copy(src_ref.at[e], src.at[pl.ds(e * rows, rows)], sem.at[e]))
     for c in cps:
@@ -47,36 +51,91 @@
             return 0
 
         lax.fori_loop(0, rows // 128, tile_body, 0)
-        if meta:
+        if meta and grouped:
+            v = fl[pl.ds(0, META), :].astype(F32)
+            for p in range(1, np_):
+                v = jnp.maximum(v, fl[pl.ds(p * META, META), :].astype(F32))
+            o[pl.ds(rows, META), :] = v.astype(BF16)
+        elif meta:
             k = lax.broadcasted_iota(jnp.int32, (META, o.shape[1]), 0)
-            v = jnp.where(k == 0, meta_ref[0], jnp.where(k == 1, meta_ref[1], meta_ref[2]))
+            v = jnp.where(k == 0, meta_ref[0], jnp.where(k == 1, meta_ref[1], jnp.where(k == 2, meta_ref[2], meta_ref[3])))
             o[pl.ds(rows, META), :] = v.astype(BF16)
 
 
-def _pack(src, pos, meta, starts):
+def _pack(src, pos, meta, starts, el, grouped):
     d = src.shape[-1]
     rows = pos.shape[1]
     vspec = pl.BlockSpec(memory_space=pltpu.VMEM)
     total = sum(r for _, r, _ in starts)
     return pl.pallas_call(
-        functools.partial(_pack_kernel, src.ndim == 4, starts),
+        functools.partial(_pack_kernel, grouped, el, starts),
         out_shape=[jax.ShapeDtypeStruct((r + META * m, d), BF16) for _, r, m in starts],
         in_specs=[vspec, pl.BlockSpec(memory_space=pltpu.SMEM), pl.BlockSpec(memory_space=pl.ANY)],
         out_specs=[vspec] * len(starts),
-        scratch_shapes=[pltpu.VMEM((rows, d), BF16), pltpu.SemaphoreType.DMA((8,))],
+        scratch_shapes=[pltpu.VMEM((rows, d), BF16), pltpu.VMEM((4 * META, d), BF16), pltpu.SemaphoreType.DMA((12,))],
         cost_estimate=pl.CostEstimate(flops=2 * total * rows * d, bytes_accessed=2 * (rows + total) * d, transcendentals=0),
     )(pos, meta, src)
+
+
+def _send_kernel(blk, over_ref, to_ref, v_ref, o_ref):
+    rows = o_ref.shape[0] // 8
+
+    def tile_body(i, _):
+        r = pl.multiple_of(i * rows, 8)
+        line = lax.broadcasted_iota(jnp.int32, (rows, v_ref.shape[0]), 0) + r
+        hot = jnp.where(to_ref[...] == line, 1.0, 0.0).astype(BF16)
+        o_ref[pl.ds(r, rows), :] = jnp.dot(hot, v_ref[...], preferred_element_type=F32).astype(BF16)
+        return 0
+
+    lax.fori_loop(0, 8, tile_body, 0)
+    for b in range(o_ref.shape[0] // blk):
+        o_ref[pl.ds((b + 1) * blk - META, META), :] = jnp.full((META, o_ref.shape[1]), over_ref[0], F32).astype(BF16)
+
+
+def _send(to, over, v, np_, blk):
+    t, d = v.shape
+    vspec = pl.BlockSpec(memory_space=pltpu.VMEM)
+    return pl.pallas_call(
+        functools.partial(_send_kernel, blk),
+        out_shape=jax.ShapeDtypeStruct((np_ * blk, d), BF16),
+        in_specs=[pl.BlockSpec(memory_space=pltpu.SMEM), vspec, vspec],
+        out_specs=vspec,
+        cost_estimate=pl.CostEstimate(flops=2 * t * np_ * blk * d, bytes_accessed=2 * (t + np_ * blk) * d, transcendentals=0),
+        name="send",
+    )(over, to, v)
+
+
+def _unpack_kernel(at_ref, src_ref, o_ref):
+    def tile_body(i, _):
+        r = pl.ds(pl.multiple_of(i * 128, 128), 128)
+        lane = lax.broadcasted_iota(jnp.int32, (128, src_ref.shape[0]), 1)
+        hot = jnp.where(at_ref[r, :] == lane, 1.0, 0.0).astype(BF16)
+        o_ref[r, :] = jnp.dot(hot, src_ref[...], preferred_element_type=F32).astype(BF16)
+        return 0
+
+    lax.fori_loop(0, o_ref.shape[0] // 128, tile_body, 0)
+
+
+def _unpack(at, src):
+    t, (rows, d) = at.shape[0], src.shape
+    vspec = pl.BlockSpec(memory_space=pltpu.VMEM)
+    return pl.pallas_call(
+        _unpack_kernel,
+        out_shape=jax.ShapeDtypeStruct((t, d), BF16),
+        in_specs=[vspec, vspec],
+        out_specs=vspec,
+        cost_estimate=pl.CostEstimate(flops=2 * t * rows * d, bytes_accessed=2 * (rows + t) * d, transcendentals=0),
+        name="unpack",
+    )(at, src)
 
 
 def _dwp_kernel(n, first, idx_ref, *refs):
     xc, yc = refs[:2 * n], refs[2 * n:4 * n]
     w1, w3, w2 = refs[4 * n:4 * n + 3]
-    o1, o3, o2 = refs[-17:-14]
-    x, y, xm, w13, w2s, dh, a, acc13, acc2, wsem, xsem, ysem, msem, osem = refs[-14:]
+    o1, o3, o2, oflag = refs[-19:-15]
+    x, y, xm, ym, w13, w2s, dh, a, acc13, acc2, wsem, xsem, ysem, msem, osem = refs[-15:]
     el, fs, d = w2s.shape
     hp = PACK // 2
-    rows = dh.shape[0] // n
-    gap = PACK - rows
     f0 = pl.multiple_of(idx_ref[0] * fs, 128)
     half = lambda j: pl.ds(j * fs, fs)
 
@@ -90,144 +149,139 @@
                 pltpu.make_async_copy(o3.at[e], acc13.at[e, :, half(1)], wsem.at[4, e]),
                 pltpu.make_async_copy(o2.at[e], acc2.at[e], wsem.at[5, e])]
 
-    def row_copies(c, s, refs_s):
-        lo, hi = refs_s
+    def row_copies(s, xp, yp):
         at = lambda k: pl.ds(pl.multiple_of(s * PACK + k * hp, 128), hp)
-        sem = xsem if c is x else ysem
-        cps = [pltpu.make_async_copy(lo.at[pl.ds(0, hp)], c.at[at(0)], sem.at[0, s]),
-               pltpu.make_async_copy(hi, c.at[at(1)], sem.at[1, s])]
-        if c is x:
-            cps.append(pltpu.make_async_copy(lo.at[pl.ds(hp, META)], xm.at[pl.ds(pl.multiple_of(s * META, META), META)], msem.at[s]))
-        return cps
+        mt = pl.ds(pl.multiple_of(s * META, META), META)
+        return [pltpu.make_async_copy(xp[0].at[pl.ds(hp, META)], xm.at[mt], msem.at[0, s]),
+                pltpu.make_async_copy(yp[0].at[pl.ds(hp, META)], ym.at[mt], msem.at[1, s]),
+                pltpu.make_async_copy(xp[0].at[pl.ds(0, hp)], x.at[at(0)], xsem.at[0, s]),
+                pltpu.make_async_copy(yp[0].at[pl.ds(0, hp)], y.at[at(0)], ysem.at[0, s]),
+                pltpu.make_async_copy(xp[1], x.at[at(1)], xsem.at[1, s]),
+                pltpu.make_async_copy(yp[1], y.at[at(1)], ysem.at[1, s])]
+
+    def out_copies(e):
+        return [pltpu.make_async_copy(acc13.at[e, :, half(0)], o1.at[e], osem.at[0, e]),
+                pltpu.make_async_copy(acc13.at[e, :, half(1)], o3.at[e], osem.at[1, e]),
+                pltpu.make_async_copy(acc2.at[e], o2.at[e], osem.at[2, e])]
 
     for c in w_copies(0):
         c.start()
     for s in range(n):
-        for c in row_copies(x, s, xc[2 * s:2 * s + 2]) + row_copies(y, s, yc[2 * s:2 * s + 2]):
+        for c in row_copies(s, xc[2 * s:2 * s + 2], yc[2 * s:2 * s + 2]):
             c.start()
+        if s == 0 and not first:
+            for c in prev_copies(0):
+                c.start()
     for c in w_copies(1):
         c.start()
-    if not first:
-        for e in range(el):
-            for c in prev_copies(e):
-                c.start()
-
-    per = rows // 128
+    if first:
+        acc13[...] = jnp.zeros_like(acc13)
+        acc2[...] = jnp.zeros_like(acc2)
+    else:
+        for c in prev_copies(1):
+            c.start()
 
     def expert_body(e, _):
-        off = e * gap
         sign = (1 - 2 * e).astype(F32)
         for c in w_copies(e):
             c.wait()
-
-        def rows_body(i, _):
-            s = i // per
-            t = i - s * per
-
-            @pl.when((e == 0) & (t == 0))
-            def _():
-                for c in row_copies(x, s, xc[:2]) + row_copies(y, s, yc[:2]):
-                    c.wait()
-
-            r = pl.ds(pl.multiple_of(s * PACK + off + t * 128, 128), 128)
-            m = xm[pl.ds(pl.multiple_of(s * META, META), META), :fs].astype(F32)
-            cut = m[0:1, :] * 8.0 + m[1:2, :]
-            row = (lax.broadcasted_iota(jnp.int32, (128, fs), 0) + (off + t * 128)).astype(F32)
-            keep = (cut - row - 0.5) * sign > 0.0
-            h = jnp.dot(x[r, :], w13[e], preferred_element_type=F32).astype(BF16).astype(F32)
-            da = lax.dot_general(y[r, :], w2s[e], (((1,), (1,)), ((), ())),
-                                 preferred_element_type=F32).astype(BF16).astype(F32)
-            h1 = jnp.where(keep, h[:, :fs], 0.0)
-            h3 = jnp.where(keep, h[:, fs:], 0.0)
-            da = jnp.where(keep, da, 0.0)
-            sg = jax.nn.sigmoid(h1)
-            silu = h1 * sg
-            o = pl.ds(pl.multiple_of(i * 128, 128), 128)
-            a[o, :] = (silu * h3).astype(BF16)
-            dh[o, :fs] = (da * h3 * sg * (1.0 + h1 * (1.0 - sg))).astype(BF16)
-            dh[o, fs:] = (da * silu).astype(BF16)
-            return 0
-
-        lax.fori_loop(0, per * n, rows_body, 0)
         if not first:
             for c in prev_copies(e):
                 c.wait()
 
-        def win(ref, s, cols):
-            return ref[pl.ds(pl.multiple_of(s * PACK + off, 128), rows), cols]
-
-        def acc(ref, m, parts):
-            val = parts[0]
-            for p in parts[1:]:
-                val = val + p
-            if first:
-                ref[e, m, :] = val
-            else:
-                ref[e, m, :] += val
-
-        def d13_body(i, _):
-            m = pl.ds(pl.multiple_of(i * 128, 128), 128)
-            acc(acc13, m, [lax.dot_general(win(x, s, m), dh[s * rows:(s + 1) * rows, :], (((0,), (0,)), ((), ())),
-                                           preferred_element_type=F32) for s in range(n)])
-            pltpu.make_async_copy(acc13.at[e, m, half(0)], o1.at[e, m], osem.at[0]).start()
-            pltpu.make_async_copy(acc13.at[e, m, half(1)], o3.at[e, m], osem.at[1]).start()
+        def group_body(s, _):
+            @pl.when(e == 0)
+            def _():
+                for c in row_copies(s, xc[:2], yc[:2]):
+                    c.wait()
+
+            m = xm[pl.ds(pl.multiple_of(s * META, META), META), :128].astype(F32)
+            cut = jnp.max(m[0:1, :] * 8.0 + m[1:2, :])
+            other = jnp.max(m[2:3, :] * 8.0 + m[3:4, :])
+            used = jnp.where(e == 0, cut, other).astype(jnp.int32)
+
+            def tile_body(k, _):
+                base = jnp.where(e == 0, k * TILE, PACK - TILE - k * TILE)
+                r = pl.ds(pl.multiple_of(s * PACK + base, TILE), TILE)
+                row = (lax.broadcasted_iota(jnp.int32, (TILE, fs), 0) + base).astype(F32)
+                keep = (cut - row - 0.5) * sign > 0.0
+                h = jnp.dot(x[r, :], w13[e], preferred_element_type=F32).astype(BF16).astype(F32)
+                da = lax.dot_general(y[r, :], w2s[e], (((1,), (1,)), ((), ())),
+                                     preferred_element_type=F32).astype(BF16).astype(F32)
+                h1 = jnp.where(keep, h[:, :fs], 0.0)
+                h3 = jnp.where(keep, h[:, fs:], 0.0)
+                da = jnp.where(keep, da, 0.0)
+                sg = jax.nn.sigmoid(h1)
+                silu = h1 * sg
+                a[...] = (silu * h3).astype(BF16)
+                dh[:, :fs] = (da * h3 * sg * (1.0 + h1 * (1.0 - sg))).astype(BF16)
+                dh[:, fs:] = (da * silu).astype(BF16)
+                for i in range(d // 256):
+                    m = slice(i * 256, (i + 1) * 256)
+                    acc13[e, m, :] += lax.dot_general(x[r, m], dh[...], (((0,), (0,)), ((), ())), preferred_element_type=F32)
+                acc2[e] += lax.dot_general(a[...], y[r, :], (((0,), (0,)), ((), ())), preferred_element_type=F32)
+                return 0
+
+            lax.fori_loop(0, (used + (TILE - 1)) // TILE, tile_body, 0)
             return 0
 
-        lax.fori_loop(0, d // 128, d13_body, 0)
-
-        def d2_body(i, _):
-            m = pl.ds(pl.multiple_of(i * 128, 128), 128)
-            acc(acc2, m, [lax.dot_general(a[s * rows:(s + 1) * rows, m], win(y, s, slice(None)), (((0,), (0,)), ((), ())),
-                                          preferred_element_type=F32) for s in range(n)])
-            pltpu.make_async_copy(acc2.at[e, m], o2.at[e, m], osem.at[2]).start()
-            return 0
-
-        lax.fori_loop(0, fs // 128, d2_body, 0)
+        lax.fori_loop(0, n, group_body, 0)
+        for c in out_copies(e):
+            c.start()
         return 0
 
     lax.fori_loop(0, el, expert_body, 0)
+    flag = ym[pl.ds(0, META), :].astype(F32)
+    for s in range(1, n):
+        flag = jnp.maximum(flag, ym[pl.ds(s * META, META), :].astype(F32))
+    if not first:
+        flag = jnp.maximum(flag, refs[4 * n + 6][...])
+    oflag[...] = flag
     for e in range(el):
-        pltpu.make_async_copy(acc13.at[e, :, half(0)], o1.at[e], osem.at[0]).wait()
-        pltpu.make_async_copy(acc13.at[e, :, half(1)], o3.at[e], osem.at[1]).wait()
-        pltpu.make_async_copy(acc2.at[e], o2.at[e], osem.at[2]).wait()
-
-
-def _dwp_call(idx, xs, ys, rows, w1, w3, w2, prev):
+        for c in out_copies(e):
+            c.wait()
+
+
+def _dwp_call(idx, xs, ys, w1, w3, w2, prev):
     el, d, f = w1.shape
     n = len(xs)
     fs = f // 8
     anyspec = pl.BlockSpec(memory_space=pl.ANY)
+    vspec = pl.BlockSpec(memory_space=pltpu.VMEM)
     outs = [jax.ShapeDtypeStruct((el, d, fs), F32), jax.ShapeDtypeStruct((el, d, fs), F32),
-            jax.ShapeDtypeStruct((el, fs, d), F32)]
+            jax.ShapeDtypeStruct((el, fs, d), F32), jax.ShapeDtypeStruct((META, d), F32)]
     args = [idx, *(c for p in xs for c in p), *(c for p in ys for c in p), w1, w3, w2]
+    specs = [pl.BlockSpec(memory_space=pltpu.SMEM)] + [anyspec] * (len(args) - 1)
     alias = {}
     if prev is not None:
         alias = {len(args) + i: i for i in range(3)}
         args += list(prev)
+        specs += [anyspec] * 3 + [vspec]
     return pl.pallas_call(
         functools.partial(_dwp_kernel, n, prev is None),
         out_shape=outs,
-        in_specs=[pl.BlockSpec(memory_space=pltpu.SMEM)] + [anyspec] * (len(args) - 1),
-        out_specs=[anyspec] * 3,
+        in_specs=specs,
+        out_specs=[anyspec] * 3 + [vspec],
         scratch_shapes=[
             pltpu.VMEM((n * PACK, d), BF16),
             pltpu.VMEM((n * PACK, d), BF16),
             pltpu.VMEM((n * META, d), BF16),
+            pltpu.VMEM((n * META, d), BF16),
             pltpu.VMEM((el, d, 2 * fs), BF16),
             pltpu.VMEM((el, fs, d), BF16),
-            pltpu.VMEM((n * rows, 2 * fs), BF16),
-            pltpu.VMEM((n * rows, fs), BF16),
+            pltpu.VMEM((TILE, 2 * fs), BF16),
+            pltpu.VMEM((TILE, fs), BF16),
             pltpu.VMEM((el, d, 2 * fs), F32),
             pltpu.VMEM((el, fs, d), F32),
             pltpu.SemaphoreType.DMA((6, el)),
             pltpu.SemaphoreType.DMA((2, n)),
             pltpu.SemaphoreType.DMA((2, n)),
-            pltpu.SemaphoreType.DMA((n,)),
-            pltpu.SemaphoreType.DMA((3,)),
+            pltpu.SemaphoreType.DMA((2, n)),
+            pltpu.SemaphoreType.DMA((3, el)),
         ],
         input_output_aliases=alias,
-        cost_estimate=pl.CostEstimate(flops=24 * n * rows * d * fs, bytes_accessed=n * 4 * 2**20 + 18 * 2**20,
-                                      transcendentals=2 * n * rows * fs),
+        cost_estimate=pl.CostEstimate(flops=12 * n * PACK * d * fs, bytes_accessed=n * 4 * 2**20 + 18 * 2**20,
+                                      transcendentals=n * PACK * fs),
     )(*args)
 
 
@@ -394,9 +448,12 @@
         rank = jnp.dot(used, (at < to).astype(BF16), preferred_element_type=F32)
         count = jnp.sum(used.astype(F32), axis=1)
         room = PACK - count[0]
-        back = jnp.where(rank[1] < room, PACK - 1 - rank[1], PACK + rank[1] - room)
-        pos = jnp.where(used > 0, jnp.stack([rank[0], back]), -1.0).reshape(1, el * rows)
-        cut = jnp.stack([jnp.floor(count[0] / 8.0), count[0] - 8.0 * jnp.floor(count[0] / 8.0)])
+        far = jnp.where(rank[1] < room, PACK - 1 - rank[1], PACK + rank[1] - room)
+        pos = jnp.where(used > 0, jnp.stack([rank[0], far]), -1.0).reshape(1, el * rows)
+        kept = jnp.stack([count[0], jnp.minimum(count[1], room)])
+        eighth = jnp.floor(kept / 8.0)
+        meta = jnp.stack([eighth, kept - 8.0 * eighth], axis=1).reshape(4)
+        over = (count[0] + count[1] > PACK).astype(F32)
         halves = ((0, PACK // 2, True), (PACK // 2, PACK // 2, False))
 
         def chain(c, last_right):
@@ -408,15 +465,16 @@
             r.append([lax.ppermute(v, 'data', perm) for v in last])
             return r, l
 
-        xr, xl = chain(_pack(xd, pos, jnp.append(cut, 0.0), halves), True)
-        over = lax.pmax((count[0] + count[1] > PACK).astype(F32), 'expert')
+        xr, xl = chain(_pack(xd, pos, meta, halves, el, False), True)
 
         v = (gates[:, :, None] * dy.astype(F32)[:, None, :]).astype(BF16)
-        col = jnp.where(slot >= 0, slot, cap)
-        send = jnp.zeros((np_ * el, cap, d), BF16).at[topk_idx, col].set(v, mode='drop')
-        recv = lax.all_to_all(send.reshape(np_, el, cap, d), 'expert', 0, 0, tiled=True)
-        dyd = jnp.swapaxes(recv, 0, 1).reshape(el, np_ * cap, d)
-        yr, yl = chain(_pack(recv, pos, jnp.stack([over, over, over]), halves), False)
+        blk = el * cap + META
+        ex, sl = topk_idx[:, 0], slot[:, 0]
+        row = jnp.where(sl >= 0, ex * cap + (ex // el) * META + sl, -1).reshape(1, -1)
+        send = _send(row, over.reshape(1), v[:, 0], np_, blk)
+        recv = lax.all_to_all(send.reshape(np_, blk, d), 'expert', 0, 0, tiled=True)
+        dyd = jnp.swapaxes(recv[:, :el * cap].reshape(np_, el, cap, d), 0, 1).reshape(el, np_ * cap, d)
+        yr, yl = chain(_pack(recv, pos, meta, halves, el, True), False)
         dg = jnp.einsum('tkd,td->tk', yd, dy, preferred_element_type=F32)
 
         h1f = h1.astype(F32)
@@ -429,23 +487,20 @@
         dxd = (jnp.einsum('ecf,edf->ecd', dh1, w1, preferred_element_type=F32)
                + jnp.einsum('ecf,edf->ecd', dh3, w3, preferred_element_type=F32)).astype(BF16)
         out = jnp.swapaxes(dxd.reshape(el, np_, cap, d), 0, 1)
-        back = lax.all_to_all(out, 'expert', 0, 0, tiled=True).reshape(np_ * el, cap, d)
-        got = back[topk_idx, jnp.minimum(col, cap - 1)].astype(F32)
-        dx = jnp.sum(jnp.where((slot >= 0)[:, :, None], got, 0.0), axis=1).astype(BF16)
+        back = lax.all_to_all(out, 'expert', 0, 0, tiled=True).reshape(np_ * el * cap, d)
+        dx = _unpack(jnp.where(sl >= 0, ex * cap + sl, -1)[:, None], back)
 
         acc = None
         for pick in (lambda r, l: (r[0], r[1], l[1]), lambda r, l: (r[2], l[2]),
                      lambda r, l: (r[3], l[3]), lambda r, l: (r[4],)):
-            acc = _dwp_call(idx, pick(xr, xl), pick(yr, yl), rows, w1, w3, w2, acc)
-
-        flags = [c[0][PACK // 2, 0] for c in yr + yl[1:]]
-        some = functools.reduce(jnp.maximum, flags) > 0
+            acc = _dwp_call(idx, pick(xr, xl), pick(yr, yl), w1, w3, w2, acc)
+
+        acc, some = acc[:3], acc[3][0, 0] > 0
         rest = ((PACK, el * rows - PACK, False),)
 
         def spill(acc):
-            zero = jnp.zeros(3, F32)
-            xo, = _pack(xd, pos, zero, rest)
-            yo, = _pack(recv, pos, zero, rest)
+            xo, = _pack(xd, pos, meta, rest, el, False)
+            yo, = _pack(recv, pos, meta, rest, el, True)
 
             def hop(_, st):
                 xo, yo, acc = st

time: 351 us -> 296 us (0.84)
  local copies, waits for them, and re-layouts: 38.8 us -> 6.67 us
  waiting for transfers between devices: 69.9 us -> 95.6 us
  Pallas kernels: 112 us -> 89.6 us
  other arithmetic: 18.3 us -> 9.6 us
  blocking collectives: 8.2 us -> 0 us
  between operations: 9.27 us -> 4.13 us
  starting transfers between devices: 48 us -> 43.7 us
    ppermute x12, waiting for transfers between devices: 30.1 us -> 78.4 us  [chain(): l.append([lax.ppermute(v, 'data', LEFT) for v in l[-1]])]
    pallas_call x4, Pallas kernels: 97.3 us -> 62.2 us  [_dwp_call(): pl.pallas_call(functools.partial(_dwp_kernel, n, prev is None), out_shape...]
    gather x1 -> x0, local copies, waits for them, and re-layouts: 23.8 us -> none  [body(): got = back[topk_idx, jnp.minimum(col, cap - 1)].astype(F32)]
    ppermute x12, waiting for transfers between devices: 32.3 us -> 17.2 us  [chain(): r.append([lax.ppermute(v, 'data', RIGHT) for v in r[-1]])]
    pallas_call x2 -> x4, Pallas kernels: 14.3 us -> 27.4 us  [the longest x2 14.2 us: _pack(): pl.pallas_call(functools.partial(_pack_kernel, grouped, el, starts), out_...]
    ppermute x12, starting transfers between devices: 18.6 us -> 8.98 us  [chain(): r.append([lax.ppermute(v, 'data', RIGHT) for v in r[-1]])]
    pmax x1 -> x0, blocking collectives: 8.2 us -> none  [body(): over = lax.pmax((count[0] + count[1] > PACK).astype(F32), 'expert')]
    unnamed x4 -> x1, other arithmetic: 8.12 us -> 0.01 us
  transfers between devices with their start and end apart: 30 -> 30, of which waited for: 5 -> 9; matrix products, arithmetic and copies ran while one was open for 26% -> 17% of each run, Pallas kernels for 27% -> 24%
where the time goes in v2:
time: 296 us; the launch traced here: 295 us
  waiting for transfers between devices  95.6 us (32%)
  Pallas kernels  89.6 us (30%)
  matrix products  45.8 us (15%)
  starting transfers between devices  43.7 us (15%)
  other arithmetic  9.6 us (3%)
  local copies, waits for them, and re-layouts  6.67 us (2%)
  between operations  4.13 us (1%)
    ppermute x12, waiting for transfers between devices, chain(): l.append([lax.ppermute(v, 'data', LEFT) for v in l[-1]])  78.4 us
    pallas_call x4, Pallas kernels, _dwp_call(): pl.pallas_call(functools.partial(_dwp_kernel, n, prev is None), out_shape...  62.2 us
    ppermute x12, starting transfers between devices, chain(): l.append([lax.ppermute(v, 'data', LEFT) for v in l[-1]])  20 us
    dot_general x1, matrix products, body(): jnp.einsum('ecf,edf->ecd', dh1, w1, preferred_element_type=F32)  18.3 us
    ppermute x12, waiting for transfers between devices, chain(): r.append([lax.ppermute(v, 'data', RIGHT) for v in r[-1]])  17.2 us
    dot_general x1, matrix products, body(): jnp.einsum('ecf,edf->ecd', dh3, w3, preferred_element_type=F32)  15.1 us
    pallas_call x2, Pallas kernels, _pack(): pl.pallas_call(functools.partial(_pack_kernel, grouped, el, starts), out_...  14.2 us
    dot_general x1, matrix products, body(): jnp.einsum('ecd,efd->ecf', dyd, w2, preferred_element_type=F32).astype(BF16)  12.2 us
  transfers between devices with their start and end apart: 30, of which 9 were waited for; matrix products, arithmetic and copies ran while one was open for 17% of the time, Pallas kernels for 24%

profile of v2, /device:TPU:0, one launch (start us, length us, event | category | flops | bytes accessed | tf_op | source)
XLA Modules:
  0.0 295.1 jit_solution(10368924170423881188)
XLA Ops:
  0.6 2.0 abs_reduce_fusion
  4.6 1.3 compare_select_fusion.to_ref
  6.0 4.5 %fusion.13 = (f32[1024]{0:T(1024)}, bf16[1024,768]{1,0:T(8,128)(2,1)}) fusion(bf16[1024,768]{1,0:T(8,128)(2,1)} %param.15, bf16[1024,1,768]{2,0,1:T(8,128)(2,1)} %param.19, f32[1024]{0:T(1024)} %bitcast.55), kind=kLoop, calls=%fused_computation.21 | loop fusion | flops 4717568 | bytes 4726784 | tf_op jit(solution)/shard_map/tkd,td->tk/dot_general | solution.py:478
  10.4 6.3 %send.1 = bf16[1344,768]{1,0:T(8,128)(2,1)} custom-call(f32[1]{0:T(128)} %bitcast.2.over_ref, s32[1,1024]{1,0:T(1,128)} %compare_select_fusion.to_ref, bf16[1024,768]{1,0:T(8,128)(2,1)} %get-tuple-element.168.v_ref), custom_call_target="tpu_custom_call" | custom-call | flops 2113929216 | bytes 3637248 | tf_op jit(solution)/shard_map/send/pallas_call | solution.py:98
  16.8 4.2 %all-to-all-start = ((bf16[4,336,768]{2,1,0:T(8,128)(2,1)}), bf16[4,336,768]{2,1,0:T(8,128)(2,1)S(1)}, u32[]{:S(2)}, u32[]{:S(2)}) async-start(bf16[4,336,768]{2,1,0:T(8,128)(2,1)} %bitcast.49), calls=%async_computation | async-start | bytes 4128768 | tf_op jit(solution)/shard_map/all_to_all | solution.py:475
  23.4 6.5 %shard_map.146 = (bf16[528,768]{1,0:T(8,128)(2,1)}, bf16[512,768]{1,0:T(8,128)(2,1)}) custom-call(f32[1,1280]{1,0:T(1,128)S(1)} %bitcast.52, f32[4]{0:T(128)S(1)} %reshape.276.meta_ref, bf16[2,640,768]{2,1,0:T(8,128)(2,1)} %src_ref.1), custom_call_target="tpu_custom_call" | custom-call | flops 2013265920 | bytes 3538944 | tf_op jit(solution)/shard_map/pallas_call | solution.py:70
  29.9 2.4 collective-permute-start.18
  32.5 1.9 collective-permute-start.21
  35.0 33.3 %collective-permute-done.21.refs_5_ = bf16[512,768]{1,0:T(8,128)(2,1)} collective-permute-done((bf16[512,768]{1,0:T(8,128)(2,1)}, bf16[512,768]{1,0:T(8,128)(2,1)}, u32[]{:S(2)}, u32[]{:S(2)}) %collective-permute-start.21) | collective-permute-done | bytes 786464 | tf_op jit(solution)/shard_map/ppermute | solution.py:463
  68.3 1.7 collective-permute-start.22
  70.3 1.7 collective-permute-start.19
  72.3 7.7 %shard_map.147 = (bf16[528,768]{1,0:T(8,128)(2,1)}, bf16[512,768]{1,0:T(8,128)(2,1)}) custom-call(f32[1,1280]{1,0:T(1,128)S(1)} %bitcast.53, f32[4]{0:T(128)S(1)} %reshape.276.meta_ref, bf16[4,336,768]{2,1,0:T(8,128)(2,1)S(1)} %all-to-all-done.src_ref), custom_call_target="tpu_custom_call" | custom-call | flops 2013265920 | bytes 3538944 | tf_op jit(solution)/shard_map/pallas_call | solution.py:70
  80.0 1.7 collective-permute-start.10
  82.1 12.2 %convolution_convert_fusion = bf16[2,640,3072]{2,1,0:T(8,128)(2,1)} fusion(bf16[2,640,768]{2,1,0:T(8,128)(2,1)S(1)} %bitcast.51, bf16[2,3072,768]{2,1,0:T(8,128)(2,1)} %refs_6_.1), kind=kOutput, calls=%fused_computation.15 | convolution fusion | flops 6043729920 | bytes 19267584 | tf_op jit(solution)/shard_map/ecd,efd->ecf/dot_general | solution.py:484
  94.7 1.7 collective-permute-start.14
  96.3 10.0 %collective-permute-done.19.refs_2_ = bf16[528,768]{1,0:T(8,128)(2,1)} collective-permute-done((bf16[528,768]{1,0:T(8,128)(2,1)}, bf16[528,768]{1,0:T(8,128)(2,1)}, u32[]{:S(2)}, u32[]{:S(2)}) %collective-permute-start.19) | collective-permute-done | bytes 811040 | tf_op jit(solution)/shard_map/ppermute | solution.py:463
  106.4 1.7 collective-permute-start.27
  108.1 1.6 collective-permute-start.8
  109.7 15.1 %fusion.8 = f32[2,640,768]{2,1,0:T(8,128)} fusion(bf16[2,768,3072]{2,1,0:T(8,128)(2,1)} %refs_5_.1, bf16[2,640,3072]{2,1,0:T(8,128)(2,1)} %convolution_convert_fusion, bf16[2,640,3072]{2,1,0:T(8,128)(2,1)} %param.21), kind=kOutput, calls=%fused_computation.13 | convolution fusion | flops 6071255040 | bytes 29097984 | tf_op jit(solution)/shard_map/ecf,edf->ecd/dot_general | solution.py:488
  124.8 14.8 %collective-permute-done.14.refs_11_ = bf16[512,768]{1,0:T(8,128)(2,1)} collective-permute-done((bf16[512,768]{1,0:T(8,128)(2,1)S(1)}, bf16[512,768]{1,0:T(8,128)(2,1)}, u32[]{:S(2)}, u32[]{:S(2)}) %collective-permute-start.14) | collective-permute-done | bytes 786464 | tf_op jit(solution)/shard_map/ppermute | solution.py:463
  139.6 1.4 collective-permute-start.23
  141.0 1.3 collective-permute-done.27.refs_9_
  142.7 1.7 collective-permute-start.15
  144.7 14.4 %collective-permute-done.8.refs_1_ = bf16[512,768]{1,0:T(8,128)(2,1)S(1)} collective-permute-done((bf16[512,768]{1,0:T(8,128)(2,1)}, bf16[512,768]{1,0:T(8,128)(2,1)S(1)}, u32[]{:S(2)}, u32[]{:S(2)}) %collective-permute-start.8) | collective-permute-done | bytes 786464 | tf_op jit(solution)/shard_map/ppermute | solution.py:462
  159.1 0.9 copy-done.5
  160.0 1.6 collective-permute-start.11
  161.5 18.3 %add_convert_fusion = bf16[2,640,768]{2,1,0:T(8,128)(2,1)S(1)} fusion(f32[2,640,768]{2,1,0:T(8,128)} %fusion.8, bf16[2,768,3072]{2,1,0:T(8,128)(2,1)} %refs_4_.1, bf16[2,640,3072]{2,1,0:T(8,128)(2,1)} %convolution_convert_fusion, bf16[2,640,3072]{2,1,0:T(8,128)(2,1)} %param.21, bf16[2,640,3072]{2,1,0:T(8,128)(2,1)} %param.22), kind=kOutput, calls=%fused_computation.16 | convolution fusion | flops 6092881920 | bytes 38928384 | tf_op jit(solution)/shard_map/ecf,edf->ecd/dot_general | solution.py:487
  179.8 1.4 copy.47
  181.2 4.4 %all-to-all-start.1 = ((bf16[4,2,160,768]{3,2,1,0:T(8,128)(2,1)}), bf16[4,2,160,768]{3,2,1,0:T(8,128)(2,1)}, u32[]{:S(2)}, u32[]{:S(2)}) async-start(bf16[4,2,160,768]{3,2,1,0:T(8,128)(2,1)} %bitcast.47), calls=%async_computation.1 | async-start | bytes 3932160 | tf_op jit(solution)/shard_map/all_to_all | solution.py:490
  186.0 0.9 add_select_fusion.at_ref
  186.9 1.6 collective-permute-start.20
  188.9 1.6 collective-permute-start.16
  190.5 1.5 collective-permute-done.28.refs_5_
  192.8 1.8 collective-permute-done.11.refs_6_
  194.5 1.1 collective-permute-start.12
  195.6 17.7 %shard_map.148 = (f32[2,768,384]{2,1,0:T(8,128)S(1)}, f32[2,768,384]{2,1,0:T(8,128)}, f32[2,384,768]{2,1,0:T(8,128)}, f32[16,768]{1,0:T(8,128)}) custom-call(s32[1]{0:T(128)} %bitcast.15.idx_ref, bf16[528,768]{1,0:T(8,128)(2,1)} %get-tuple-element.124.refs_0_, bf16[512,768]{1,0:T(8,128)(2,1)} %get-tuple-element.125.refs_1_, ...), custom_call_target="tpu_custom_call" | custom-call | flops 10871635968 | bytes 31457280 | tf_op jit(solution)/shard_map/pallas_call | solution.py:260
  213.3 2.5 collective-permute-start.26
  215.8 6.8 %unpack.1 = bf16[1024,768]{1,0:T(8,128)(2,1)} custom-call(s32[1024,1]{1,0:T(8,128)} %add_select_fusion.at_ref, bf16[1280,768]{1,0:T(8,128)(2,1)} %bitcast.12.src_ref), custom_call_target="tpu_custom_call" | custom-call | flops 2013265920 | bytes 3538944 | tf_op jit(solution)/shard_map/unpack/pallas_call | solution.py:122
  222.7 2.9 collective-permute-start.9
  225.6 3.1 %collective-permute-done.16.refs_7_ = bf16[512,768]{1,0:T(8,128)(2,1)} collective-permute-done((bf16[512,768]{1,0:T(8,128)(2,1)}, bf16[512,768]{1,0:T(8,128)(2,1)}, u32[]{:S(2)}, u32[]{:S(2)}) %collective-permute-start.16) | collective-permute-done | bytes 786464 | tf_op jit(solution)/shard_map/ppermute | solution.py:463
  228.8 1.5 collective-permute-start.5
  230.8 15.3 %collective-permute-done.12.refs_6_ = bf16[528,768]{1,0:T(8,128)(2,1)} collective-permute-done((bf16[528,768]{1,0:T(8,128)(2,1)}, bf16[528,768]{1,0:T(8,128)(2,1)}, u32[]{:S(2)}, u32[]{:S(2)}) %collective-permute-start.12) | collective-permute-done | bytes 811040 | tf_op jit(solution)/shard_map/ppermute | solution.py:463
  246.1 1.1 collective-permute-start.13
  247.2 15.9 %shard_map.149 = (f32[2,768,384]{2,1,0:T(8,128)S(1)}, f32[2,768,384]{2,1,0:T(8,128)}, f32[2,384,768]{2,1,0:T(8,128)}, f32[16,768]{1,0:T(8,128)}) custom-call(s32[1]{0:T(128)} %bitcast.15.idx_ref, bf16[528,768]{1,0:T(8,128)(2,1)} %collective-permute-done.3.refs_0_, ...), custom_call_target="tpu_custom_call", output_to_operand_aliasing={{0}: (12, {}), {1}: (13, {}), {2}: (14, {})} | custom-call | flops 7247757312 | bytes 27262976 | tf_op jit(solution)/shard_map/pallas_call | solution.py:260
  263.2 17.4 %shard_map.150 = (f32[2,768,384]{2,1,0:T(8,128)S(1)}, f32[2,768,384]{2,1,0:T(8,128)}, f32[2,384,768]{2,1,0:T(8,128)}, f32[16,768]{1,0:T(8,128)}) custom-call(s32[1]{0:T(128)} %bitcast.15.idx_ref, bf16[528,768]{1,0:T(8,128)(2,1)} %collective-permute-done.4.refs_0_, ...), custom_call_target="tpu_custom_call", output_to_operand_aliasing={{0}: (12, {}), {1}: (13, {}), {2}: (14, {})} | custom-call | flops 7247757312 | bytes 27262976 | tf_op jit(solution)/shard_map/pallas_call | solution.py:260
  280.7 11.1 %shard_map.151 = (f32[2,768,384]{2,1,0:T(8,128)S(1)}, f32[2,768,384]{2,1,0:T(8,128)}, f32[2,384,768]{2,1,0:T(8,128)}, f32[16,768]{1,0:T(8,128)}) custom-call(s32[1]{0:T(128)} %bitcast.15.idx_ref, bf16[528,768]{1,0:T(8,128)(2,1)} %collective-permute-done.5.refs_0_, ...), custom_call_target="tpu_custom_call", output_to_operand_aliasing={{0}: (8, {}), {1}: (9, {}), {2}: (10, {})} | custom-call | flops 3623878656 | bytes 23068672 | tf_op jit(solution)/shard_map/pallas_call | solution.py:260
  291.8 1.2 slice.28
  293.7 1.4 copy-done
  (62 shorter events, 6.5 us)
Async XLA Ops:
  16.8 55.6 %all-to-all-start = ((bf16[4,336,768]{2,1,0:T(8,128)(2,1)}), bf16[4,336,768]{2,1,0:T(8,128)(2,1)S(1)}, u32[]{:S(2)}, u32[]{:S(2)}) async-start(bf16[4,336,768]{2,1,0:T(8,128)(2,1)} %bitcast.49), calls=%async_computation | async-start | bytes 4128768 | tf_op jit(solution)/shard_map/all_to_all | solution.py:475
  21.6 12.8 %copy-start.6 = (s32[1024,1]{0,1:T(1,128)S(1)}, s32[1024,1]{0,1:T(1,128)}, u32[]{:S(2)}) copy-start(s32[1024,1]{0,1:T(1,128)} %param.18) | copy-start | bytes 12292
  23.4 11.4 %copy-start.7 = (s32[1024,1]{0,1:T(1,128)S(1)}, s32[1024,1]{0,1:T(1,128)}, u32[]{:S(2)}) copy-start(s32[1024,1]{0,1:T(1,128)} %param.17) | copy-start | bytes 12292
  29.9 40.4 %collective-permute-start.18 = (bf16[528,768]{1,0:T(8,128)(2,1)}, bf16[528,768]{1,0:T(8,128)(2,1)}, u32[]{:S(2)}, u32[]{:S(2)}) collective-permute-start(bf16[528,768]{1,0:T(8,128)(2,1)} %get-tuple-element.124.refs_0_), channel_id=1, source_target_pairs={{8,0},{16,8},{24,16},{28,24},{20,28},{12,20},{4,12},{0,4},{9,1},{1... | collective-permute-start | bytes 2433032 | tf_op jit(solution)/shard_map/ppermute | solution.py:463
  32.3 39.7 %collective-permute-start.2 = (bf16[528,768]{1,0:T(8,128)(2,1)}, bf16[528,768]{1,0:T(8,128)(2,1)}, u32[]{:S(2)}, u32[]{:S(2)}) collective-permute-start(bf16[528,768]{1,0:T(8,128)(2,1)} %get-tuple-element.124.refs_0_), channel_id=1, source_target_pairs={{0,8},{8,16},{16,24},{24,28},{28,20},{20,12},{12,4},{4,0},{1,9},{9... | collective-permute-start | bytes 2433032 | tf_op jit(solution)/shard_map/ppermute | solution.py:462
  32.5 35.8 %collective-permute-start.21 = (bf16[512,768]{1,0:T(8,128)(2,1)}, bf16[512,768]{1,0:T(8,128)(2,1)}, u32[]{:S(2)}, u32[]{:S(2)}) collective-permute-start(bf16[512,768]{1,0:T(8,128)(2,1)} %get-tuple-element.125.refs_1_), channel_id=1, source_target_pairs={{8,0},{16,8},{24,16},{28,24},{20,28},{12,20},{4,12},{0,4},{9,1},{1... | collective-permute-start | bytes 2359304 | tf_op jit(solution)/shard_map/ppermute | solution.py:463
  34.4 35.6 %collective-permute-start.6 = (bf16[512,768]{1,0:T(8,128)(2,1)}, bf16[512,768]{1,0:T(8,128)(2,1)}, u32[]{:S(2)}, u32[]{:S(2)}) collective-permute-start(bf16[512,768]{1,0:T(8,128)(2,1)} %get-tuple-element.125.refs_1_), channel_id=1, source_target_pairs={{0,8},{8,16},{16,24},{24,28},{28,20},{20,12},{12,4},{4,0},{1,9},{9... | collective-permute-start | bytes 2359304 | tf_op jit(solution)/shard_map/ppermute | solution.py:462
  68.3 26.0 %collective-permute-start.22 = (bf16[512,768]{1,0:T(8,128)(2,1)}, bf16[512,768]{1,0:T(8,128)(2,1)}, u32[]{:S(2)}, u32[]{:S(2)}) collective-permute-start(bf16[512,768]{1,0:T(8,128)(2,1)} %collective-permute-done.21.refs_5_), channel_id=1, source_target_pairs={{8,0},{16,8},{24,16},{28,24},{20,28},{12,20},{4,12},{0,4},{9,1},{1... | collective-permute-start | bytes 2359304 | tf_op jit(solution)/shard_map/ppermute | solution.py:463
  70.0 24.7 %collective-permute-start.7 = (bf16[512,768]{1,0:T(8,128)(2,1)}, bf16[512,768]{1,0:T(8,128)(2,1)}, u32[]{:S(2)}, u32[]{:S(2)}) collective-permute-start(bf16[512,768]{1,0:T(8,128)(2,1)} %collective-permute-done.6.refs_3_), channel_id=1, source_target_pairs={{0,8},{8,16},{16,24},{24,28},{28,20},{20,12},{12,4},{4,0},{1,9},{9... | collective-permute-start | bytes 2359304 | tf_op jit(solution)/shard_map/ppermute | solution.py:462
  70.3 36.1 %collective-permute-start.19 = (bf16[528,768]{1,0:T(8,128)(2,1)}, bf16[528,768]{1,0:T(8,128)(2,1)}, u32[]{:S(2)}, u32[]{:S(2)}) collective-permute-start(bf16[528,768]{1,0:T(8,128)(2,1)} %collective-permute-done.18.refs_4_), channel_id=1, source_target_pairs={{8,0},{16,8},{24,16},{28,24},{20,28},{12,20},{4,12},{0,4},{9,1},{1... | collective-permute-start | bytes 2433032 | tf_op jit(solution)/shard_map/ppermute | solution.py:463
  72.0 36.1 %collective-permute-start.3 = (bf16[528,768]{1,0:T(8,128)(2,1)}, bf16[528,768]{1,0:T(8,128)(2,1)}, u32[]{:S(2)}, u32[]{:S(2)}) collective-permute-start(bf16[528,768]{1,0:T(8,128)(2,1)} %collective-permute-done.2.refs_2_), channel_id=1, source_target_pairs={{0,8},{8,16},{16,24},{24,28},{28,20},{20,12},{12,4},{4,0},{1,9},{9... | collective-permute-start | bytes 2433032 | tf_op jit(solution)/shard_map/ppermute | solution.py:462
  72.3 9.6 %copy-start.3 = (bf16[4,336,768]{2,1,0:T(8,128)(2,1)}, bf16[4,336,768]{2,1,0:T(8,128)(2,1)S(1)}, u32[]{:S(2)}) copy-start(bf16[4,336,768]{2,1,0:T(8,128)(2,1)S(1)} %all-to-all-done.src_ref) | copy-start | bytes 6193156
  80.0 62.6 %collective-permute-start.10 = (bf16[528,768]{1,0:T(8,128)(2,1)}, bf16[528,768]{1,0:T(8,128)(2,1)}, u32[]{:S(2)}, u32[]{:S(2)}) collective-permute-start(bf16[528,768]{1,0:T(8,128)(2,1)} %get-tuple-element.126.refs_6_), channel_id=1, source_target_pairs={{8,0},{16,8},{24,16},{28,24},{20,28},{12,20},{4,12},{0,4},{9,1},{1... | collective-permute-start | bytes 2433032 | tf_op jit(solution)/shard_map/ppermute | solution.py:463
  82.1 12.3 %copy-start.8 = (bf16[528,768]{1,0:T(8,128)(2,1)S(1)}, bf16[528,768]{1,0:T(8,128)(2,1)}, u32[]{:S(2)}) copy-start(bf16[528,768]{1,0:T(8,128)(2,1)} %get-tuple-element.126.refs_6_) | copy-start | bytes 2433028
  82.1 12.6 %copy-start.9 = (bf16[512,768]{1,0:T(8,128)(2,1)S(1)}, bf16[512,768]{1,0:T(8,128)(2,1)}, u32[]{:S(2)}) copy-start(bf16[512,768]{1,0:T(8,128)(2,1)} %get-tuple-element.127.refs_7_) | copy-start | bytes 2359300
  94.3 50.0 %collective-permute-start.24 = (bf16[528,768]{1,0:T(8,128)(2,1)S(1)}, bf16[528,768]{1,0:T(8,128)(2,1)}, u32[]{:S(2)}, u32[]{:S(2)}) collective-permute-start(bf16[528,768]{1,0:T(8,128)(2,1)S(1)} %copy-done.8), channel_id=1, source_target_pairs={{0,8},{8,16},{16,24},{24,28},{28,20},{20,12},{12,4},{4,0},{1,9},{9... | collective-permute-start | bytes 2433032 | tf_op jit(solution)/shard_map/ppermute | solution.py:462
  94.7 44.9 %collective-permute-start.14 = (bf16[512,768]{1,0:T(8,128)(2,1)S(1)}, bf16[512,768]{1,0:T(8,128)(2,1)}, u32[]{:S(2)}, u32[]{:S(2)}) collective-permute-start(bf16[512,768]{1,0:T(8,128)(2,1)S(1)} %copy-done.9), channel_id=1, source_target_pairs={{8,0},{16,8},{24,16},{28,24},{20,28},{12,20},{4,12},{0,4},{9,1},{1... | collective-permute-start | bytes 2359304 | tf_op jit(solution)/shard_map/ppermute | solution.py:463
  106.4 35.9 %collective-permute-start.27 = (bf16[512,768]{1,0:T(8,128)(2,1)S(1)}, bf16[512,768]{1,0:T(8,128)(2,1)}, u32[]{:S(2)}, u32[]{:S(2)}) collective-permute-start(bf16[512,768]{1,0:T(8,128)(2,1)S(1)} %copy-done.9), channel_id=1, source_target_pairs={{0,8},{8,16},{16,24},{24,28},{28,20},{20,12},{12,4},{4,0},{1,9},{9... | collective-permute-start | bytes 2359304 | tf_op jit(solution)/shard_map/ppermute | solution.py:462
  108.1 50.9 %collective-permute-start.8 = (bf16[512,768]{1,0:T(8,128)(2,1)}, bf16[512,768]{1,0:T(8,128)(2,1)S(1)}, u32[]{:S(2)}, u32[]{:S(2)}) collective-permute-start(bf16[512,768]{1,0:T(8,128)(2,1)} %collective-permute-done.7.refs_1_), channel_id=1, source_target_pairs={{0,8},{8,16},{16,24},{24,28},{28,20},{20,12},{12,4},{4,0},{1,9},{9... | collective-permute-start | bytes 2359304 | tf_op jit(solution)/shard_map/ppermute | solution.py:462
  139.6 47.4 %collective-permute-start.23 = (bf16[512,768]{1,0:T(8,128)(2,1)}, bf16[512,768]{1,0:T(8,128)(2,1)}, u32[]{:S(2)}, u32[]{:S(2)}) collective-permute-start(bf16[512,768]{1,0:T(8,128)(2,1)} %collective-permute-done.22.refs_3_), channel_id=1, source_target_pairs={{8,0},{16,8},{24,16},{28,24},{20,28},{12,20},{4,12},{0,4},{9,1},{1... | collective-permute-start | bytes 2359304 | tf_op jit(solution)/shard_map/ppermute | solution.py:463
  142.3 46.2 %collective-permute-start.4 = (bf16[528,768]{1,0:T(8,128)(2,1)}, bf16[528,768]{1,0:T(8,128)(2,1)}, u32[]{:S(2)}, u32[]{:S(2)}) collective-permute-start(bf16[528,768]{1,0:T(8,128)(2,1)} %collective-permute-done.3.refs_0_), channel_id=1, source_target_pairs={{0,8},{8,16},{16,24},{24,28},{28,20},{20,12},{12,4},{4,0},{1,9},{9... | collective-permute-start | bytes 2433032 | tf_op jit(solution)/shard_map/ppermute | solution.py:462
  142.7 46.3 %collective-permute-start.15 = (bf16[512,768]{1,0:T(8,128)(2,1)}, bf16[512,768]{1,0:T(8,128)(2,1)}, u32[]{:S(2)}, u32[]{:S(2)}) collective-permute-start(bf16[512,768]{1,0:T(8,128)(2,1)} %collective-permute-done.14.refs_11_), channel_id=1, source_target_pairs={{8,0},{16,8},{24,16},{28,24},{20,28},{12,20},{4,12},{0,4},{9,1},{1... | collective-permute-start | bytes 2359304 | tf_op jit(solution)/shard_map/ppermute | solution.py:463
  144.3 47.6 %collective-permute-start.28 = (bf16[512,768]{1,0:T(8,128)(2,1)}, bf16[512,768]{1,0:T(8,128)(2,1)}, u32[]{:S(2)}, u32[]{:S(2)}) collective-permute-start(bf16[512,768]{1,0:T(8,128)(2,1)} %collective-permute-done.27.refs_9_), channel_id=1, source_target_pairs={{0,8},{8,16},{16,24},{24,28},{28,20},{20,12},{12,4},{4,0},{1,9},{9... | collective-permute-start | bytes 2359304 | tf_op jit(solution)/shard_map/ppermute | solution.py:462
  159.1 0.9 copy-start.5
  160.0 34.6 %collective-permute-start.11 = (bf16[528,768]{1,0:T(8,128)(2,1)}, bf16[528,768]{1,0:T(8,128)(2,1)}, u32[]{:S(2)}, u32[]{:S(2)}) collective-permute-start(bf16[528,768]{1,0:T(8,128)(2,1)} %collective-permute-done.10.refs_10_), channel_id=1, source_target_pairs={{8,0},{16,8},{24,16},{28,24},{20,28},{12,20},{4,12},{0,4},{9,1},{1... | collective-permute-start | bytes 2433032 | tf_op jit(solution)/shard_map/ppermute | solution.py:463
  181.2 34.6 %all-to-all-start.1 = ((bf16[4,2,160,768]{3,2,1,0:T(8,128)(2,1)}), bf16[4,2,160,768]{3,2,1,0:T(8,128)(2,1)}, u32[]{:S(2)}, u32[]{:S(2)}) async-start(bf16[4,2,160,768]{3,2,1,0:T(8,128)(2,1)} %bitcast.47), calls=%async_computation.1 | async-start | bytes 3932160 | tf_op jit(solution)/shard_map/all_to_all | solution.py:490
  186.9 35.8 %collective-permute-start.20 = (bf16[528,768]{1,0:T(8,128)(2,1)}, bf16[528,768]{1,0:T(8,128)(2,1)S(1)}, u32[]{:S(2)}, u32[]{:S(2)}) collective-permute-start(bf16[528,768]{1,0:T(8,128)(2,1)} %collective-permute-done.19.refs_2_), channel_id=1, source_target_pairs={{8,0},{16,8},{24,16},{28,24},{20,28},{12,20},{4,12},{0,4},{9,1},{1... | collective-permute-start | bytes 2433032 | tf_op jit(solution)/shard_map/ppermute | solution.py:463
  188.5 24.8 %collective-permute-start.25 = (bf16[528,768]{1,0:T(8,128)(2,1)}, bf16[528,768]{1,0:T(8,128)(2,1)}, u32[]{:S(2)}, u32[]{:S(2)}) collective-permute-start(bf16[528,768]{1,0:T(8,128)(2,1)} %collective-permute-done.24.refs_8_), channel_id=1, source_target_pairs={{0,8},{8,16},{16,24},{24,28},{28,20},{20,12},{12,4},{4,0},{1,9},{9... | collective-permute-start | bytes 2433032 | tf_op jit(solution)/shard_map/ppermute | solution.py:462
  188.9 39.8 %collective-permute-start.16 = (bf16[512,768]{1,0:T(8,128)(2,1)}, bf16[512,768]{1,0:T(8,128)(2,1)}, u32[]{:S(2)}, u32[]{:S(2)}) collective-permute-start(bf16[512,768]{1,0:T(8,128)(2,1)} %collective-permute-done.15.refs_7_), channel_id=1, source_target_pairs={{8,0},{16,8},{24,16},{28,24},{20,28},{12,20},{4,12},{0,4},{9,1},{1... | collective-permute-start | bytes 2359304 | tf_op jit(solution)/shard_map/ppermute | solution.py:463
  192.0 38.2 %collective-permute-start.29 = (bf16[512,768]{1,0:T(8,128)(2,1)}, bf16[512,768]{1,0:T(8,128)(2,1)}, u32[]{:S(2)}, u32[]{:S(2)}) collective-permute-start(bf16[512,768]{1,0:T(8,128)(2,1)} %collective-permute-done.28.refs_5_), channel_id=1, source_target_pairs={{0,8},{8,16},{16,24},{24,28},{28,20},{20,12},{12,4},{4,0},{1,9},{9... | collective-permute-start | bytes 2359304 | tf_op jit(solution)/shard_map/ppermute | solution.py:462
  194.5 51.6 %collective-permute-start.12 = (bf16[528,768]{1,0:T(8,128)(2,1)}, bf16[528,768]{1,0:T(8,128)(2,1)}, u32[]{:S(2)}, u32[]{:S(2)}) collective-permute-start(bf16[528,768]{1,0:T(8,128)(2,1)} %collective-permute-done.11.refs_6_), channel_id=1, source_target_pairs={{8,0},{16,8},{24,16},{28,24},{20,28},{12,20},{4,12},{0,4},{9,1},{1... | collective-permute-start | bytes 2433032 | tf_op jit(solution)/shard_map/ppermute | solution.py:463
  213.3 49.9 %collective-permute-start.26 = (bf16[528,768]{1,0:T(8,128)(2,1)}, bf16[528,768]{1,0:T(8,128)(2,1)}, u32[]{:S(2)}, u32[]{:S(2)}) collective-permute-start(bf16[528,768]{1,0:T(8,128)(2,1)} %collective-permute-done.25.refs_4_), channel_id=1, source_target_pairs={{0,8},{8,16},{16,24},{24,28},{28,20},{20,12},{12,4},{4,0},{1,9},{9... | collective-permute-start | bytes 2433032 | tf_op jit(solution)/shard_map/ppermute | solution.py:462
  222.7 40.5 %copy-start.4 = (bf16[528,768]{1,0:T(8,128)(2,1)}, bf16[528,768]{1,0:T(8,128)(2,1)S(1)}, u32[]{:S(2)}) copy-start(bf16[528,768]{1,0:T(8,128)(2,1)S(1)} %collective-permute-done.20.refs_2_) | copy-start | bytes 2433028
  222.7 58.0 %collective-permute-start.9 = (bf16[512,768]{1,0:T(8,128)(2,1)}, bf16[512,768]{1,0:T(8,128)(2,1)}, u32[]{:S(2)}, u32[]{:S(2)}) collective-permute-start(bf16[512,768]{1,0:T(8,128)(2,1)} %copy-done.5), channel_id=1, source_target_pairs={{0,8},{8,16},{16,24},{24,28},{28,20},{20,12},{12,4},{4,0},{1,9},{9... | collective-permute-start | bytes 2359304 | tf_op jit(solution)/shard_map/ppermute | solution.py:465
  228.8 51.9 %collective-permute-start.5 = (bf16[528,768]{1,0:T(8,128)(2,1)}, bf16[528,768]{1,0:T(8,128)(2,1)}, u32[]{:S(2)}, u32[]{:S(2)}) collective-permute-start(bf16[528,768]{1,0:T(8,128)(2,1)} %collective-permute-done.4.refs_0_), channel_id=1, source_target_pairs={{0,8},{8,16},{16,24},{24,28},{28,20},{20,12},{12,4},{4,0},{1,9},{9... | collective-permute-start | bytes 2433032 | tf_op jit(solution)/shard_map/ppermute | solution.py:465
  230.2 50.4 %collective-permute-start.17 = (bf16[512,768]{1,0:T(8,128)(2,1)}, bf16[512,768]{1,0:T(8,128)(2,1)}, u32[]{:S(2)}, u32[]{:S(2)}) collective-permute-start(bf16[512,768]{1,0:T(8,128)(2,1)} %collective-permute-done.16.refs_7_), channel_id=1, source_target_pairs={{8,0},{16,8},{24,16},{28,24},{20,28},{12,20},{4,12},{0,4},{9,1},{1... | collective-permute-start | bytes 2359304 | tf_op jit(solution)/shard_map/ppermute | solution.py:465
  246.1 34.5 %collective-permute-start.13 = (bf16[528,768]{1,0:T(8,128)(2,1)}, bf16[528,768]{1,0:T(8,128)(2,1)}, u32[]{:S(2)}, u32[]{:S(2)}) collective-permute-start(bf16[528,768]{1,0:T(8,128)(2,1)} %collective-permute-done.12.refs_6_), channel_id=1, source_target_pairs={{8,0},{16,8},{24,16},{28,24},{20,28},{12,20},{4,12},{0,4},{9,1},{1... | collective-permute-start | bytes 2433032 | tf_op jit(solution)/shard_map/ppermute | solution.py:465
  293.7 1.4 copy-start

commit v3 on v2

--- a/solution.py
+++ b/solution.py
@@ -12,9 +12,10 @@
 BF16 = jnp.bfloat16
 
 
-PACK = 1024
+PACK = 1088
 META = 16
 TILE = 256
+FRONT = 576
 RING = (0, 2, 4, 6, 7, 5, 3, 1)
 RIGHT = [(RING[i], RING[(i + 1) % 8]) for i in range(8)]
 LEFT = [(RING[(i + 1) % 8], RING[i]) for i in range(8)]
@@ -44,13 +45,13 @@
     pos = pos_ref[...]
     for o, (base, rows, meta) in zip(outs, starts):
         def tile_body(i, _, o=o, base=base):
-            r = pl.multiple_of(i * 128, 128)
-            row = (lax.broadcasted_iota(jnp.int32, (128, 1), 0) + (r + base)).astype(F32)
+            r = pl.multiple_of(i * 64, 64)
+            row = (lax.broadcasted_iota(jnp.int32, (64, 1), 0) + (r + base)).astype(F32)
             hot = jnp.where(pos == row, 1.0, 0.0).astype(BF16)
-            o[pl.ds(r, 128), :] = jnp.dot(hot, src[...], preferred_element_type=F32).astype(BF16)
+            o[pl.ds(r, 64), :] = jnp.dot(hot, src[...], preferred_element_type=F32).astype(BF16)
             return 0
 
-        lax.fori_loop(0, rows // 128, tile_body, 0)
+        lax.fori_loop(0, rows // 64, tile_body, 0)
         if meta and grouped:
             v = fl[pl.ds(0, META), :].astype(F32)
             for p in range(1, np_):
@@ -135,7 +136,7 @@
     o1, o3, o2, oflag = refs[-19:-15]
     x, y, xm, ym, w13, w2s, dh, a, acc13, acc2, wsem, xsem, ysem, msem, osem = refs[-15:]
     el, fs, d = w2s.shape
-    hp = PACK // 2
+    hp = FRONT
     f0 = pl.multiple_of(idx_ref[0] * fs, 128)
     half = lambda j: pl.ds(j * fs, fs)
 
@@ -150,7 +151,7 @@
                 pltpu.make_async_copy(o2.at[e], acc2.at[e], wsem.at[5, e])]
 
     def row_copies(s, xp, yp):
-        at = lambda k: pl.ds(pl.multiple_of(s * PACK + k * hp, 128), hp)
+        at = lambda k: pl.ds(pl.multiple_of(s * PACK + k * hp, 64), (hp, PACK - hp)[k])
         mt = pl.ds(pl.multiple_of(s * META, META), META)
         return [pltpu.make_async_copy(xp[0].at[pl.ds(hp, META)], xm.at[mt], msem.at[0, s]),
                 pltpu.make_async_copy(yp[0].at[pl.ds(hp, META)], ym.at[mt], msem.at[1, s]),
@@ -202,7 +203,7 @@
 
             def tile_body(k, _):
                 base = jnp.where(e == 0, k * TILE, PACK - TILE - k * TILE)
-                r = pl.ds(pl.multiple_of(s * PACK + base, TILE), TILE)
+                r = pl.ds(pl.multiple_of(s * PACK + base, 64), TILE)
                 row = (lax.broadcasted_iota(jnp.int32, (TILE, fs), 0) + base).astype(F32)
                 keep = (cut - row - 0.5) * sign > 0.0
                 h = jnp.dot(x[r, :], w13[e], preferred_element_type=F32).astype(BF16).astype(F32)
@@ -292,13 +293,13 @@
     x, y, w13, w2s, dh, a, acc13, acc2, wsem, xsem, ysem, osem = refs[-12:]
     rows = xs[0].shape[0]
     fs = w2s.shape[0]
-    tile = 128
+    tile = 64
     per = rows // tile
     f0 = pl.multiple_of(idx_ref[0] * fs, 128)
     half = lambda j: pl.ds(j * fs, fs)
 
     def row_copy(src, dst, j, sem):
-        return pltpu.make_async_copy(src, dst.at[pl.ds(pl.multiple_of(j * rows, 128), rows)], sem.at[j])
+        return pltpu.make_async_copy(src, dst.at[pl.ds(pl.multiple_of(j * rows, 64), rows)], sem.at[j])
 
     wcp = [
         pltpu.make_async_copy(w1.at[e, :, pl.ds(f0, fs)], w13.at[:, half(0)], wsem.at[0]),
@@ -330,7 +331,7 @@
             row_copy(xs[0], x, i // per, xsem).wait()
             row_copy(ys[0], y, i // per, ysem).wait()
 
-        r = pl.ds(pl.multiple_of(i * tile, 128), tile)
+        r = pl.ds(pl.multiple_of(i * tile, 64), tile)
         h = jnp.dot(x[r, :], w13[...], preferred_element_type=F32).astype(BF16).astype(F32)
         da = lax.dot_general(y[r, :], w2s[...], (((1,), (1,)), ((), ())),
                              preferred_element_type=F32).astype(BF16).astype(F32)
@@ -454,7 +455,7 @@
         eighth = jnp.floor(kept / 8.0)
         meta = jnp.stack([eighth, kept - 8.0 * eighth], axis=1).reshape(4)
         over = (count[0] + count[1] > PACK).astype(F32)
-        halves = ((0, PACK // 2, True), (PACK // 2, PACK // 2, False))
+        halves = ((0, FRONT, True), (FRONT, PACK - FRONT, False))
 
         def chain(c, last_right):
             r, l = [c], [c]
@@ -492,7 +493,7 @@
 
         acc = None
         for pick in (lambda r, l: (r[0], r[1], l[1]), lambda r, l: (r[2], l[2]),
-                     lambda r, l: (r[3], l[3]), lambda r, l: (r[4],)):
+                           lambda r, l: (r[3], l[3]), lambda r, l: (r[4],)):
             acc = _dwp_call(idx, pick(xr, xl), pick(yr, yl), w1, w3, w2, acc)
 
         acc, some = acc[:3], acc[3][0, 0] > 0
@@ -502,12 +503,17 @@
             xo, = _pack(xd, pos, meta, rest, el, False)
             yo, = _pack(recv, pos, meta, rest, el, True)
 
+            acc = _dw_call(1, idx, [xo], [yo], w1, w3, w2, acc, False)
+
             def hop(_, st):
-                xo, yo, acc = st
-                acc = _dw_call(1, idx, [xo], [yo], w1, w3, w2, acc, False)
-                return lax.ppermute(xo, 'data', RIGHT), lax.ppermute(yo, 'data', RIGHT), tuple(acc)
-
-            return lax.fori_loop(0, 8, hop, (xo, yo, acc))[2]
+                xa, ya, xb, yb, acc = st
+                xa, ya = (lax.ppermute(c, 'data', RIGHT) for c in (xa, ya))
+                xb, yb = (lax.ppermute(c, 'data', LEFT) for c in (xb, yb))
+                return xa, ya, xb, yb, tuple(_dw_call(1, idx, [xa, xb], [ya, yb], w1, w3, w2, acc, False))
+
+            xa, ya, _, _, acc = lax.fori_loop(0, 3, hop, (xo, yo, xo, yo, tuple(acc)))
+            xa, ya = (lax.ppermute(c, 'data', RIGHT) for c in (xa, ya))
+            return tuple(_dw_call(1, idx, [xa], [ya], w1, w3, w2, acc, False))
 
         acc = lax.cond(some, spill, lambda acc: acc, tuple(acc))
         dw1, dw3, dw2 = acc

time: 296 us -> 314 us (1.061)
  Pallas kernels: 89.6 us -> 99.1 us
  waiting for transfers between devices: 95.6 us -> 103 us
    ppermute x12, waiting for transfers between devices: 17.2 us -> 54.1 us  [chain(): r.append([lax.ppermute(v, 'data', RIGHT) for v in r[-1]])]
    ppermute x12, waiting for transfers between devices: 78.4 us -> 49 us  [chain(): l.append([lax.ppermute(v, 'data', LEFT) for v in l[-1]])]
    pallas_call x2, Pallas kernels: 14.2 us -> 23.3 us  [_pack(): pl.pallas_call(functools.partial(_pack_kernel, grouped, el, starts), out_...]
    ppermute x12, starting transfers between devices: 8.98 us -> 12.7 us  [chain(): r.append([lax.ppermute(v, 'data', RIGHT) for v in r[-1]])]
    ppermute x12, starting transfers between devices: 20 us -> 16.4 us  [chain(): l.append([lax.ppermute(v, 'data', LEFT) for v in l[-1]])]
  transfers between devices with their start and end apart: 30 -> 30, of which waited for: 9 -> 7; matrix products, arithmetic and copies ran while one was open for 17% -> 16% of each run, Pallas kernels for 24% -> 26%
where the time goes in v3:
time: 314 us; the launch traced here: 312 us
  waiting for transfers between devices  103 us (33%)
  Pallas kernels  99.1 us (32%)
  matrix products  45.8 us (15%)
  starting transfers between devices  44.6 us (14%)
  other arithmetic  9.56 us (3%)
  local copies, waits for them, and re-layouts  5.72 us (2%)
  between operations  4.15 us (1%)
    pallas_call x4, Pallas kernels, _dwp_call(): pl.pallas_call(functools.partial(_dwp_kernel, n, prev is None), out_shape...  62.6 us
    ppermute x12, waiting for transfers between devices, chain(): r.append([lax.ppermute(v, 'data', RIGHT) for v in r[-1]])  54.1 us
    ppermute x12, waiting for transfers between devices, chain(): l.append([lax.ppermute(v, 'data', LEFT) for v in l[-1]])  49 us
    pallas_call x2, Pallas kernels, _pack(): pl.pallas_call(functools.partial(_pack_kernel, grouped, el, starts), out_...  23.3 us
    dot_general x1, matrix products, body(): jnp.einsum('ecf,edf->ecd', dh1, w1, preferred_element_type=F32)  18.3 us
    ppermute x12, starting transfers between devices, chain(): l.append([lax.ppermute(v, 'data', LEFT) for v in l[-1]])  16.4 us
    dot_general x1, matrix products, body(): jnp.einsum('ecf,edf->ecd', dh3, w3, preferred_element_type=F32)  15.1 us
    ppermute x12, starting transfers between devices, chain(): r.append([lax.ppermute(v, 'data', RIGHT) for v in r[-1]])  12.7 us
  transfers between devices with their start and end apart: 30, of which 7 were waited for; matrix products, arithmetic and copies ran while one was open for 16% of the time, Pallas kernels for 26%

profile of v3, /device:TPU:0, one launch (start us, length us, event | category | flops | bytes accessed | tf_op | source)
XLA Modules:
  0.0 312.0 jit_solution(18407395374894594948)
XLA Ops:
  0.6 2.0 abs_reduce_fusion
  2.8 0.6 fusion.23
  4.6 1.3 compare_select_fusion.to_ref
  6.0 4.5 %fusion.13 = (f32[1024]{0:T(1024)}, bf16[1024,768]{1,0:T(8,128)(2,1)}) fusion(bf16[1024,768]{1,0:T(8,128)(2,1)} %param.15, bf16[1024,1,768]{2,0,1:T(8,128)(2,1)} %param.19, f32[1024]{0:T(1024)} %bitcast.55), kind=kLoop, calls=%fused_computation.21 | loop fusion | flops 4717568 | bytes 4726784 | tf_op jit(solution)/shard_map/tkd,td->tk/dot_general | solution.py:479
  10.4 6.4 %send.1 = bf16[1344,768]{1,0:T(8,128)(2,1)} custom-call(f32[1]{0:T(128)} %bitcast.2.over_ref, s32[1,1024]{1,0:T(1,128)} %compare_select_fusion.to_ref, bf16[1024,768]{1,0:T(8,128)(2,1)} %get-tuple-element.187.v_ref), custom_call_target="tpu_custom_call" | custom-call | flops 2113929216 | bytes 3637248 | tf_op jit(solution)/shard_map/send/pallas_call | solution.py:99
  16.8 4.2 %all-to-all-start = ((bf16[4,336,768]{2,1,0:T(8,128)(2,1)}), bf16[4,336,768]{2,1,0:T(8,128)(2,1)S(1)}, u32[]{:S(2)}, u32[]{:S(2)}) async-start(bf16[4,336,768]{2,1,0:T(8,128)(2,1)} %bitcast.49), calls=%async_computation | async-start | bytes 4128768 | tf_op jit(solution)/shard_map/all_to_all | solution.py:476
  22.5 0.6 multiply_subtract_fusion
  23.4 11.1 %shard_map.146 = (bf16[592,768]{1,0:T(8,128)(2,1)}, bf16[512,768]{1,0:T(8,128)(2,1)}) custom-call(f32[1,1280]{1,0:T(1,128)S(1)} %bitcast.52, f32[4]{0:T(128)S(1)} %reshape.276.meta_ref, bf16[2,640,768]{2,1,0:T(8,128)(2,1)} %src_ref.1), custom_call_target="tpu_custom_call" | custom-call | flops 2139095040 | bytes 3637248 | tf_op jit(solution)/shard_map/pallas_call | solution.py:71
  34.5 2.4 collective-permute-start.22
  37.1 2.0 collective-permute-start.10
  39.6 36.8 %collective-permute-done.10.refs_3_ = bf16[512,768]{1,0:T(8,128)(2,1)} collective-permute-done((bf16[512,768]{1,0:T(8,128)(2,1)}, bf16[512,768]{1,0:T(8,128)(2,1)}, u32[]{:S(2)}, u32[]{:S(2)}) %collective-permute-start.10) | collective-permute-done | bytes 786464 | tf_op jit(solution)/shard_map/ppermute | solution.py:463
  76.8 1.6 collective-permute-start.26
  78.4 1.6 collective-permute-start.23
  80.5 12.2 %shard_map.147 = (bf16[592,768]{1,0:T(8,128)(2,1)}, bf16[512,768]{1,0:T(8,128)(2,1)}) custom-call(f32[1,1280]{1,0:T(1,128)S(1)} %bitcast.53, f32[4]{0:T(128)S(1)} %reshape.276.meta_ref, bf16[4,336,768]{2,1,0:T(8,128)(2,1)S(1)} %all-to-all-done.src_ref), custom_call_target="tpu_custom_call" | custom-call | flops 2139095040 | bytes 3637248 | tf_op jit(solution)/shard_map/pallas_call | solution.py:71
  92.7 1.6 collective-permute-start.18
  94.6 12.2 %convolution_convert_fusion = bf16[2,640,3072]{2,1,0:T(8,128)(2,1)} fusion(bf16[2,640,768]{2,1,0:T(8,128)(2,1)S(1)} %bitcast.51, bf16[2,3072,768]{2,1,0:T(8,128)(2,1)} %refs_6_.1), kind=kOutput, calls=%fused_computation.15 | convolution fusion | flops 6043729920 | bytes 19267584 | tf_op jit(solution)/shard_map/ecd,efd->ecf/dot_general | solution.py:485
  107.2 1.6 collective-permute-start.14
  108.8 8.2 %collective-permute-done.23.refs_2_ = bf16[592,768]{1,0:T(8,128)(2,1)} collective-permute-done((bf16[592,768]{1,0:T(8,128)(2,1)}, bf16[592,768]{1,0:T(8,128)(2,1)}, u32[]{:S(2)}, u32[]{:S(2)}) %collective-permute-start.23) | collective-permute-done | bytes 909344 | tf_op jit(solution)/shard_map/ppermute | solution.py:464
  117.0 1.7 collective-permute-start.12
  119.0 15.1 %fusion.8 = f32[2,640,768]{2,1,0:T(8,128)} fusion(bf16[2,768,3072]{2,1,0:T(8,128)(2,1)} %refs_5_.1, bf16[2,640,3072]{2,1,0:T(8,128)(2,1)} %convolution_convert_fusion, bf16[2,640,3072]{2,1,0:T(8,128)(2,1)} %param.21), kind=kOutput, calls=%fused_computation.13 | convolution fusion | flops 6071255040 | bytes 29097984 | tf_op jit(solution)/shard_map/ecf,edf->ecd/dot_general | solution.py:489
  134.2 1.7 collective-permute-start.28
  135.9 1.6 collective-permute-start.8
  137.4 12.8 %collective-permute-done.12.refs_1_ = bf16[512,768]{1,0:T(8,128)(2,1)S(1)} collective-permute-done((bf16[512,768]{1,0:T(8,128)(2,1)}, bf16[512,768]{1,0:T(8,128)(2,1)S(1)}, u32[]{:S(2)}, u32[]{:S(2)}) %collective-permute-start.12) | collective-permute-done | bytes 786464 | tf_op jit(solution)/shard_map/ppermute | solution.py:463
  150.2 1.6 collective-permute-start.19
  151.8 18.3 %collective-permute-done.27.refs_3_ = bf16[512,768]{1,0:T(8,128)(2,1)S(1)} collective-permute-done((bf16[512,768]{1,0:T(8,128)(2,1)}, bf16[512,768]{1,0:T(8,128)(2,1)S(1)}, u32[]{:S(2)}, u32[]{:S(2)}) %collective-permute-start.27) | collective-permute-done | bytes 786464 | tf_op jit(solution)/shard_map/ppermute | solution.py:464
  170.1 1.7 collective-permute-start.32
  171.8 0.8 collective-permute-start.15
  172.6 18.3 %add_convert_fusion = bf16[2,640,768]{2,1,0:T(8,128)(2,1)S(1)} fusion(f32[2,640,768]{2,1,0:T(8,128)} %fusion.8, bf16[2,768,3072]{2,1,0:T(8,128)(2,1)} %refs_4_.1, bf16[2,640,3072]{2,1,0:T(8,128)(2,1)} %convolution_convert_fusion, bf16[2,640,3072]{2,1,0:T(8,128)(2,1)} %param.21, bf16[2,640,3072]{2,1,0:T(8,128)(2,1)} %param.22), kind=kOutput, calls=%fused_computation.16 | convolution fusion | flops 6092881920 | bytes 38928384 | tf_op jit(solution)/shard_map/ecf,edf->ecd/dot_general | solution.py:488
  190.9 1.4 copy.53
  192.3 4.4 %all-to-all-start.1 = ((bf16[4,2,160,768]{3,2,1,0:T(8,128)(2,1)}), bf16[4,2,160,768]{3,2,1,0:T(8,128)(2,1)}, u32[]{:S(2)}, u32[]{:S(2)}) async-start(bf16[4,2,160,768]{3,2,1,0:T(8,128)(2,1)} %bitcast.47), calls=%async_computation.1 | async-start | bytes 3932160 | tf_op jit(solution)/shard_map/all_to_all | solution.py:491
  197.1 0.9 add_select_fusion.at_ref
  198.0 1.6 collective-permute-start.24
  200.0 1.6 collective-permute-start.20
  201.6 4.6 %collective-permute-done.32.refs_5_ = bf16[512,768]{1,0:T(8,128)(2,1)} collective-permute-done((bf16[512,768]{1,0:T(8,128)(2,1)}, bf16[512,768]{1,0:T(8,128)(2,1)}, u32[]{:S(2)}, u32[]{:S(2)}) %collective-permute-start.32) | collective-permute-done | bytes 786464 | tf_op jit(solution)/shard_map/ppermute | solution.py:463
  206.5 1.6 collective-permute-start.16
  208.2 17.9 %shard_map.148 = (f32[2,768,384]{2,1,0:T(8,128)S(1)}, f32[2,768,384]{2,1,0:T(8,128)}, f32[2,384,768]{2,1,0:T(8,128)}, f32[16,768]{1,0:T(8,128)}) custom-call(s32[1]{0:T(128)} %bitcast.15.idx_ref, bf16[592,768]{1,0:T(8,128)(2,1)} %get-tuple-element.139.refs_0_, bf16[512,768]{1,0:T(8,128)(2,1)} %get-tuple-element.140.refs_1_, ...), custom_call_target="tpu_custom_call" | custom-call | flops 11551113216 | bytes 31457280 | tf_op jit(solution)/shard_map/pallas_call | solution.py:261
  226.0 1.9 collective-permute-start.30
  227.9 6.8 %unpack.1 = bf16[1024,768]{1,0:T(8,128)(2,1)} custom-call(s32[1024,1]{1,0:T(8,128)} %add_select_fusion.at_ref, bf16[1280,768]{1,0:T(8,128)(2,1)} %bitcast.12.src_ref), custom_call_target="tpu_custom_call" | custom-call | flops 2013265920 | bytes 3538944 | tf_op jit(solution)/shard_map/unpack/pallas_call | solution.py:123
  234.8 3.1 %collective-permute-start.13 = (bf16[512,768]{1,0:T(8,128)(2,1)}, bf16[512,768]{1,0:T(8,128)(2,1)}, u32[]{:S(2)}, u32[]{:S(2)}) collective-permute-start(bf16[512,768]{1,0:T(8,128)(2,1)} %copy-done.7), channel_id=1, source_target_pairs={{0,8},{8,16},{16,24},{24,28},{28,20},{20,12},{12,4},{4,0},{1,9},{9... | collective-permute-start | bytes 2359304 | tf_op jit(solution)/shard_map/ppermute | solution.py:466
  237.9 5.0 %collective-permute-done.20.refs_7_ = bf16[512,768]{1,0:T(8,128)(2,1)} collective-permute-done((bf16[512,768]{1,0:T(8,128)(2,1)}, bf16[512,768]{1,0:T(8,128)(2,1)}, u32[]{:S(2)}, u32[]{:S(2)}) %collective-permute-start.20) | collective-permute-done | bytes 786464 | tf_op jit(solution)/shard_map/ppermute | solution.py:464
  242.9 1.7 collective-permute-start.9
  244.9 17.5 %collective-permute-done.16.refs_6_ = bf16[592,768]{1,0:T(8,128)(2,1)} collective-permute-done((bf16[592,768]{1,0:T(8,128)(2,1)}, bf16[592,768]{1,0:T(8,128)(2,1)}, u32[]{:S(2)}, u32[]{:S(2)}) %collective-permute-start.16) | collective-permute-done | bytes 909344 | tf_op jit(solution)/shard_map/ppermute | solution.py:464
  262.4 1.6 collective-permute-start.17
  264.0 16.0 %shard_map.149 = (f32[2,768,384]{2,1,0:T(8,128)S(1)}, f32[2,768,384]{2,1,0:T(8,128)}, f32[2,384,768]{2,1,0:T(8,128)}, f32[16,768]{1,0:T(8,128)}) custom-call(s32[1]{0:T(128)} %bitcast.15.idx_ref, bf16[592,768]{1,0:T(8,128)(2,1)} %collective-permute-done.7.refs_0_, ...), custom_call_target="tpu_custom_call", output_to_operand_aliasing={{0}: (12, {}), {1}: (13, {}), {2}: (14, {})} | custom-call | flops 7700742144 | bytes 27262976 | tf_op jit(solution)/shard_map/pallas_call | solution.py:261
  280.0 17.5 %shard_map.150 = (f32[2,768,384]{2,1,0:T(8,128)S(1)}, f32[2,768,384]{2,1,0:T(8,128)}, f32[2,384,768]{2,1,0:T(8,128)}, f32[16,768]{1,0:T(8,128)}) custom-call(s32[1]{0:T(128)} %bitcast.15.idx_ref, bf16[592,768]{1,0:T(8,128)(2,1)} %collective-permute-done.8.refs_0_, ...), custom_call_target="tpu_custom_call", output_to_operand_aliasing={{0}: (12, {}), {1}: (13, {}), {2}: (14, {})} | custom-call | flops 7700742144 | bytes 27262976 | tf_op jit(solution)/shard_map/pallas_call | solution.py:261
  297.6 11.2 %shard_map.151 = (f32[2,768,384]{2,1,0:T(8,128)S(1)}, f32[2,768,384]{2,1,0:T(8,128)}, f32[2,384,768]{2,1,0:T(8,128)}, f32[16,768]{1,0:T(8,128)}) custom-call(s32[1]{0:T(128)} %bitcast.15.idx_ref, bf16[592,768]{1,0:T(8,128)(2,1)} %collective-permute-done.9.refs_0_, ...), custom_call_target="tpu_custom_call", output_to_operand_aliasing={{0}: (8, {}), {1}: (9, {}), {2}: (10, {})} | custom-call | flops 3850371072 | bytes 23068672 | tf_op jit(solution)/shard_map/pallas_call | solution.py:261
  308.8 1.2 slice.28
  310.7 1.4 copy-done
  (60 shorter events, 4.6 us)
Async XLA Ops:
  16.8 63.7 %all-to-all-start = ((bf16[4,336,768]{2,1,0:T(8,128)(2,1)}), bf16[4,336,768]{2,1,0:T(8,128)(2,1)S(1)}, u32[]{:S(2)}, u32[]{:S(2)}) async-start(bf16[4,336,768]{2,1,0:T(8,128)(2,1)} %bitcast.49), calls=%async_computation | async-start | bytes 4128768 | tf_op jit(solution)/shard_map/all_to_all | solution.py:476
  23.4 15.7 %copy-start.11 = (s32[1024,1]{0,1:T(1,128)S(1)}, s32[1024,1]{0,1:T(1,128)}, u32[]{:S(2)}) copy-start(s32[1024,1]{0,1:T(1,128)} %param.18) | copy-start | bytes 12292
  23.4 15.9 %copy-start.12 = (s32[1024,1]{0,1:T(1,128)S(1)}, s32[1024,1]{0,1:T(1,128)}, u32[]{:S(2)}) copy-start(s32[1024,1]{0,1:T(1,128)} %param.17) | copy-start | bytes 12292
  34.5 43.9 %collective-permute-start.22 = (bf16[592,768]{1,0:T(8,128)(2,1)}, bf16[592,768]{1,0:T(8,128)(2,1)}, u32[]{:S(2)}, u32[]{:S(2)}) collective-permute-start(bf16[592,768]{1,0:T(8,128)(2,1)} %get-tuple-element.139.refs_0_), channel_id=1, source_target_pairs={{8,0},{16,8},{24,16},{28,24},{20,28},{12,20},{4,12},{0,4},{9,1},{1... | collective-permute-start | bytes 2727944 | tf_op jit(solution)/shard_map/ppermute | solution.py:464
  36.9 43.1 %collective-permute-start.6 = (bf16[592,768]{1,0:T(8,128)(2,1)}, bf16[592,768]{1,0:T(8,128)(2,1)}, u32[]{:S(2)}, u32[]{:S(2)}) collective-permute-start(bf16[592,768]{1,0:T(8,128)(2,1)} %get-tuple-element.139.refs_0_), channel_id=1, source_target_pairs={{0,8},{8,16},{16,24},{24,28},{28,20},{20,12},{12,4},{4,0},{1,9},{9... | collective-permute-start | bytes 2727944 | tf_op jit(solution)/shard_map/ppermute | solution.py:463
  37.1 39.3 %collective-permute-start.10 = (bf16[512,768]{1,0:T(8,128)(2,1)}, bf16[512,768]{1,0:T(8,128)(2,1)}, u32[]{:S(2)}, u32[]{:S(2)}) collective-permute-start(bf16[512,768]{1,0:T(8,128)(2,1)} %get-tuple-element.140.refs_1_), channel_id=1, source_target_pairs={{0,8},{8,16},{16,24},{24,28},{28,20},{20,12},{12,4},{4,0},{1,9},{9... | collective-permute-start | bytes 2359304 | tf_op jit(solution)/shard_map/ppermute | solution.py:463
  39.0 37.8 %collective-permute-start.25 = (bf16[512,768]{1,0:T(8,128)(2,1)}, bf16[512,768]{1,0:T(8,128)(2,1)}, u32[]{:S(2)}, u32[]{:S(2)}) collective-permute-start(bf16[512,768]{1,0:T(8,128)(2,1)} %get-tuple-element.140.refs_1_), channel_id=1, source_target_pairs={{8,0},{16,8},{24,16},{28,24},{20,28},{12,20},{4,12},{0,4},{9,1},{1... | collective-permute-start | bytes 2359304 | tf_op jit(solution)/shard_map/ppermute | solution.py:464
  76.4 30.4 %collective-permute-start.11 = (bf16[512,768]{1,0:T(8,128)(2,1)}, bf16[512,768]{1,0:T(8,128)(2,1)}, u32[]{:S(2)}, u32[]{:S(2)}) collective-permute-start(bf16[512,768]{1,0:T(8,128)(2,1)} %collective-permute-done.10.refs_3_), channel_id=1, source_target_pairs={{0,8},{8,16},{16,24},{24,28},{28,20},{20,12},{12,4},{4,0},{1,9},{9... | collective-permute-start | bytes 2359304 | tf_op jit(solution)/shard_map/ppermute | solution.py:463
  76.8 30.4 %collective-permute-start.26 = (bf16[512,768]{1,0:T(8,128)(2,1)}, bf16[512,768]{1,0:T(8,128)(2,1)}, u32[]{:S(2)}, u32[]{:S(2)}) collective-permute-start(bf16[512,768]{1,0:T(8,128)(2,1)} %collective-permute-done.25.refs_5_), channel_id=1, source_target_pairs={{8,0},{16,8},{24,16},{28,24},{20,28},{12,20},{4,12},{0,4},{9,1},{1... | collective-permute-start | bytes 2359304 | tf_op jit(solution)/shard_map/ppermute | solution.py:464
  78.4 38.6 %collective-permute-start.23 = (bf16[592,768]{1,0:T(8,128)(2,1)}, bf16[592,768]{1,0:T(8,128)(2,1)}, u32[]{:S(2)}, u32[]{:S(2)}) collective-permute-start(bf16[592,768]{1,0:T(8,128)(2,1)} %collective-permute-done.22.refs_4_), channel_id=1, source_target_pairs={{8,0},{16,8},{24,16},{28,24},{20,28},{12,20},{4,12},{0,4},{9,1},{1... | collective-permute-start | bytes 2727944 | tf_op jit(solution)/shard_map/ppermute | solution.py:464
  80.0 38.7 %collective-permute-start.7 = (bf16[592,768]{1,0:T(8,128)(2,1)}, bf16[592,768]{1,0:T(8,128)(2,1)}, u32[]{:S(2)}, u32[]{:S(2)}) collective-permute-start(bf16[592,768]{1,0:T(8,128)(2,1)} %collective-permute-done.6.refs_2_), channel_id=1, source_target_pairs={{0,8},{8,16},{16,24},{24,28},{28,20},{20,12},{12,4},{4,0},{1,9},{9... | collective-permute-start | bytes 2727944 | tf_op jit(solution)/shard_map/ppermute | solution.py:463
  80.5 13.9 %copy-start.5 = (bf16[4,336,768]{2,1,0:T(8,128)(2,1)}, bf16[4,336,768]{2,1,0:T(8,128)(2,1)S(1)}, u32[]{:S(2)}) copy-start(bf16[4,336,768]{2,1,0:T(8,128)(2,1)S(1)} %all-to-all-done.src_ref) | copy-start | bytes 6193156
  92.7 41.5 %collective-permute-start.18 = (bf16[512,768]{1,0:T(8,128)(2,1)}, bf16[512,768]{1,0:T(8,128)(2,1)}, u32[]{:S(2)}, u32[]{:S(2)}) collective-permute-start(bf16[512,768]{1,0:T(8,128)(2,1)} %get-tuple-element.142.refs_7_), channel_id=1, source_target_pairs={{8,0},{16,8},{24,16},{28,24},{20,28},{12,20},{4,12},{0,4},{9,1},{1... | collective-permute-start | bytes 2359304 | tf_op jit(solution)/shard_map/ppermute | solution.py:464
  106.7 29.1 %collective-permute-start.31 = (bf16[512,768]{1,0:T(8,128)(2,1)}, bf16[512,768]{1,0:T(8,128)(2,1)}, u32[]{:S(2)}, u32[]{:S(2)}) collective-permute-start(bf16[512,768]{1,0:T(8,128)(2,1)} %get-tuple-element.142.refs_7_), channel_id=1, source_target_pairs={{0,8},{8,16},{16,24},{24,28},{28,20},{20,12},{12,4},{4,0},{1,9},{9... | collective-permute-start | bytes 2359304 | tf_op jit(solution)/shard_map/ppermute | solution.py:463
  107.2 64.6 %collective-permute-start.14 = (bf16[592,768]{1,0:T(8,128)(2,1)}, bf16[592,768]{1,0:T(8,128)(2,1)}, u32[]{:S(2)}, u32[]{:S(2)}) collective-permute-start(bf16[592,768]{1,0:T(8,128)(2,1)} %get-tuple-element.141.refs_6_), channel_id=1, source_target_pairs={{8,0},{16,8},{24,16},{28,24},{20,28},{12,20},{4,12},{0,4},{9,1},{1... | collective-permute-start | bytes 2727944 | tf_op jit(solution)/shard_map/ppermute | solution.py:464
  117.0 33.2 %collective-permute-start.12 = (bf16[512,768]{1,0:T(8,128)(2,1)}, bf16[512,768]{1,0:T(8,128)(2,1)S(1)}, u32[]{:S(2)}, u32[]{:S(2)}) collective-permute-start(bf16[512,768]{1,0:T(8,128)(2,1)} %collective-permute-done.11.refs_1_), channel_id=1, source_target_pairs={{0,8},{8,16},{16,24},{24,28},{28,20},{20,12},{12,4},{4,0},{1,9},{9... | collective-permute-start | bytes 2359304 | tf_op jit(solution)/shard_map/ppermute | solution.py:463
  118.7 51.4 %collective-permute-start.27 = (bf16[512,768]{1,0:T(8,128)(2,1)}, bf16[512,768]{1,0:T(8,128)(2,1)S(1)}, u32[]{:S(2)}, u32[]{:S(2)}) collective-permute-start(bf16[512,768]{1,0:T(8,128)(2,1)} %collective-permute-done.26.refs_3_), channel_id=1, source_target_pairs={{8,0},{16,8},{24,16},{28,24},{20,28},{12,20},{4,12},{0,4},{9,1},{1... | collective-permute-start | bytes 2359304 | tf_op jit(solution)/shard_map/ppermute | solution.py:464
  134.2 63.8 %collective-permute-start.28 = (bf16[592,768]{1,0:T(8,128)(2,1)}, bf16[592,768]{1,0:T(8,128)(2,1)}, u32[]{:S(2)}, u32[]{:S(2)}) collective-permute-start(bf16[592,768]{1,0:T(8,128)(2,1)} %get-tuple-element.141.refs_6_), channel_id=1, source_target_pairs={{0,8},{8,16},{16,24},{24,28},{28,20},{20,12},{12,4},{4,0},{1,9},{9... | collective-permute-start | bytes 2727944 | tf_op jit(solution)/shard_map/ppermute | solution.py:463
  135.9 63.7 %collective-permute-start.8 = (bf16[592,768]{1,0:T(8,128)(2,1)}, bf16[592,768]{1,0:T(8,128)(2,1)}, u32[]{:S(2)}, u32[]{:S(2)}) collective-permute-start(bf16[592,768]{1,0:T(8,128)(2,1)} %collective-permute-done.7.refs_0_), channel_id=1, source_target_pairs={{0,8},{8,16},{16,24},{24,28},{28,20},{20,12},{12,4},{4,0},{1,9},{9... | collective-permute-start | bytes 2727944 | tf_op jit(solution)/shard_map/ppermute | solution.py:463
  150.2 21.6 %copy-start.7 = (bf16[512,768]{1,0:T(8,128)(2,1)}, bf16[512,768]{1,0:T(8,128)(2,1)S(1)}, u32[]{:S(2)}) copy-start(bf16[512,768]{1,0:T(8,128)(2,1)S(1)} %collective-permute-done.12.refs_1_) | copy-start | bytes 2359300
  150.2 49.8 %collective-permute-start.19 = (bf16[512,768]{1,0:T(8,128)(2,1)}, bf16[512,768]{1,0:T(8,128)(2,1)}, u32[]{:S(2)}, u32[]{:S(2)}) collective-permute-start(bf16[512,768]{1,0:T(8,128)(2,1)} %collective-permute-done.18.refs_11_), channel_id=1, source_target_pairs={{8,0},{16,8},{24,16},{28,24},{20,28},{12,20},{4,12},{0,4},{9,1},{1... | collective-permute-start | bytes 2359304 | tf_op jit(solution)/shard_map/ppermute | solution.py:464
  170.1 1.7 copy-start.8
  170.1 36.0 %collective-permute-start.32 = (bf16[512,768]{1,0:T(8,128)(2,1)}, bf16[512,768]{1,0:T(8,128)(2,1)}, u32[]{:S(2)}, u32[]{:S(2)}) collective-permute-start(bf16[512,768]{1,0:T(8,128)(2,1)} %collective-permute-done.31.refs_9_), channel_id=1, source_target_pairs={{0,8},{8,16},{16,24},{24,28},{28,20},{20,12},{12,4},{4,0},{1,9},{9... | collective-permute-start | bytes 2359304 | tf_op jit(solution)/shard_map/ppermute | solution.py:463
  171.8 34.8 %collective-permute-start.15 = (bf16[592,768]{1,0:T(8,128)(2,1)}, bf16[592,768]{1,0:T(8,128)(2,1)}, u32[]{:S(2)}, u32[]{:S(2)}) collective-permute-start(bf16[592,768]{1,0:T(8,128)(2,1)} %collective-permute-done.14.refs_10_), channel_id=1, source_target_pairs={{8,0},{16,8},{24,16},{28,24},{20,28},{12,20},{4,12},{0,4},{9,1},{1... | collective-permute-start | bytes 2727944 | tf_op jit(solution)/shard_map/ppermute | solution.py:464
  192.3 35.6 %all-to-all-start.1 = ((bf16[4,2,160,768]{3,2,1,0:T(8,128)(2,1)}), bf16[4,2,160,768]{3,2,1,0:T(8,128)(2,1)}, u32[]{:S(2)}, u32[]{:S(2)}) async-start(bf16[4,2,160,768]{3,2,1,0:T(8,128)(2,1)} %bitcast.47), calls=%async_computation.1 | async-start | bytes 3932160 | tf_op jit(solution)/shard_map/all_to_all | solution.py:491
  198.0 36.8 %collective-permute-start.24 = (bf16[592,768]{1,0:T(8,128)(2,1)}, bf16[592,768]{1,0:T(8,128)(2,1)S(1)}, u32[]{:S(2)}, u32[]{:S(2)}) collective-permute-start(bf16[592,768]{1,0:T(8,128)(2,1)} %collective-permute-done.23.refs_2_), channel_id=1, source_target_pairs={{8,0},{16,8},{24,16},{28,24},{20,28},{12,20},{4,12},{0,4},{9,1},{1... | collective-permute-start | bytes 2727944 | tf_op jit(solution)/shard_map/ppermute | solution.py:464
  199.6 26.5 %collective-permute-start.29 = (bf16[592,768]{1,0:T(8,128)(2,1)}, bf16[592,768]{1,0:T(8,128)(2,1)}, u32[]{:S(2)}, u32[]{:S(2)}) collective-permute-start(bf16[592,768]{1,0:T(8,128)(2,1)} %collective-permute-done.28.refs_8_), channel_id=1, source_target_pairs={{0,8},{8,16},{16,24},{24,28},{28,20},{20,12},{12,4},{4,0},{1,9},{9... | collective-permute-start | bytes 2727944 | tf_op jit(solution)/shard_map/ppermute | solution.py:463
  200.0 42.9 %collective-permute-start.20 = (bf16[512,768]{1,0:T(8,128)(2,1)}, bf16[512,768]{1,0:T(8,128)(2,1)}, u32[]{:S(2)}, u32[]{:S(2)}) collective-permute-start(bf16[512,768]{1,0:T(8,128)(2,1)} %collective-permute-done.19.refs_7_), channel_id=1, source_target_pairs={{8,0},{16,8},{24,16},{28,24},{20,28},{12,20},{4,12},{0,4},{9,1},{1... | collective-permute-start | bytes 2359304 | tf_op jit(solution)/shard_map/ppermute | solution.py:464
  206.1 38.4 %collective-permute-start.33 = (bf16[512,768]{1,0:T(8,128)(2,1)}, bf16[512,768]{1,0:T(8,128)(2,1)}, u32[]{:S(2)}, u32[]{:S(2)}) collective-permute-start(bf16[512,768]{1,0:T(8,128)(2,1)} %collective-permute-done.32.refs_5_), channel_id=1, source_target_pairs={{0,8},{8,16},{16,24},{24,28},{28,20},{20,12},{12,4},{4,0},{1,9},{9... | collective-permute-start | bytes 2359304 | tf_op jit(solution)/shard_map/ppermute | solution.py:463
  206.5 55.8 %collective-permute-start.16 = (bf16[592,768]{1,0:T(8,128)(2,1)}, bf16[592,768]{1,0:T(8,128)(2,1)}, u32[]{:S(2)}, u32[]{:S(2)}) collective-permute-start(bf16[592,768]{1,0:T(8,128)(2,1)} %collective-permute-done.15.refs_6_), channel_id=1, source_target_pairs={{8,0},{16,8},{24,16},{28,24},{20,28},{12,20},{4,12},{0,4},{9,1},{1... | collective-permute-start | bytes 2727944 | tf_op jit(solution)/shard_map/ppermute | solution.py:464
  226.0 54.0 %collective-permute-start.30 = (bf16[592,768]{1,0:T(8,128)(2,1)}, bf16[592,768]{1,0:T(8,128)(2,1)}, u32[]{:S(2)}, u32[]{:S(2)}) collective-permute-start(bf16[592,768]{1,0:T(8,128)(2,1)} %collective-permute-done.29.refs_4_), channel_id=1, source_target_pairs={{0,8},{8,16},{16,24},{24,28},{28,20},{20,12},{12,4},{4,0},{1,9},{9... | collective-permute-start | bytes 2727944 | tf_op jit(solution)/shard_map/ppermute | solution.py:463
  234.8 45.2 %copy-start.6 = (bf16[592,768]{1,0:T(8,128)(2,1)}, bf16[592,768]{1,0:T(8,128)(2,1)S(1)}, u32[]{:S(2)}) copy-start(bf16[592,768]{1,0:T(8,128)(2,1)S(1)} %collective-permute-done.24.refs_2_) | copy-start | bytes 2727940
  234.8 62.8 %collective-permute-start.13 = (bf16[512,768]{1,0:T(8,128)(2,1)}, bf16[512,768]{1,0:T(8,128)(2,1)}, u32[]{:S(2)}, u32[]{:S(2)}) collective-permute-start(bf16[512,768]{1,0:T(8,128)(2,1)} %copy-done.7), channel_id=1, source_target_pairs={{0,8},{8,16},{16,24},{24,28},{28,20},{20,12},{12,4},{4,0},{1,9},{9... | collective-permute-start | bytes 2359304 | tf_op jit(solution)/shard_map/ppermute | solution.py:466
  242.9 54.7 %collective-permute-start.9 = (bf16[592,768]{1,0:T(8,128)(2,1)}, bf16[592,768]{1,0:T(8,128)(2,1)}, u32[]{:S(2)}, u32[]{:S(2)}) collective-permute-start(bf16[592,768]{1,0:T(8,128)(2,1)} %collective-permute-done.8.refs_0_), channel_id=1, source_target_pairs={{0,8},{8,16},{16,24},{24,28},{28,20},{20,12},{12,4},{4,0},{1,9},{9... | collective-permute-start | bytes 2727944 | tf_op jit(solution)/shard_map/ppermute | solution.py:466
  244.6 53.0 %collective-permute-start.21 = (bf16[512,768]{1,0:T(8,128)(2,1)}, bf16[512,768]{1,0:T(8,128)(2,1)}, u32[]{:S(2)}, u32[]{:S(2)}) collective-permute-start(bf16[512,768]{1,0:T(8,128)(2,1)} %collective-permute-done.20.refs_7_), channel_id=1, source_target_pairs={{8,0},{16,8},{24,16},{28,24},{20,28},{12,20},{4,12},{0,4},{9,1},{1... | collective-permute-start | bytes 2359304 | tf_op jit(solution)/shard_map/ppermute | solution.py:466
  262.4 35.2 %collective-permute-start.17 = (bf16[592,768]{1,0:T(8,128)(2,1)}, bf16[592,768]{1,0:T(8,128)(2,1)}, u32[]{:S(2)}, u32[]{:S(2)}) collective-permute-start(bf16[592,768]{1,0:T(8,128)(2,1)} %collective-permute-done.16.refs_6_), channel_id=1, source_target_pairs={{8,0},{16,8},{24,16},{28,24},{20,28},{12,20},{4,12},{0,4},{9,1},{1... | collective-permute-start | bytes 2727944 | tf_op jit(solution)/shard_map/ppermute | solution.py:466
  310.6 1.4 copy-start

commit v4 on v3

--- a/solution.py
+++ b/solution.py
@@ -15,7 +15,7 @@
 PACK = 1088
 META = 16
 TILE = 256
-FRONT = 576
+FRONT = 544
 RING = (0, 2, 4, 6, 7, 5, 3, 1)
 RIGHT = [(RING[i], RING[(i + 1) % 8]) for i in range(8)]
 LEFT = [(RING[(i + 1) % 8], RING[i]) for i in range(8)]
@@ -44,14 +44,16 @@
         c.wait()
     pos = pos_ref[...]
     for o, (base, rows, meta) in zip(outs, starts):
-        def tile_body(i, _, o=o, base=base):
-            r = pl.multiple_of(i * 64, 64)
-            row = (lax.broadcasted_iota(jnp.int32, (64, 1), 0) + (r + base)).astype(F32)
+        tile = rows // 2
+
+        def tile_body(i, _, o=o, base=base, tile=tile):
+            r = pl.multiple_of(i * tile, 16)
+            row = (lax.broadcasted_iota(jnp.int32, (tile, 1), 0) + (r + base)).astype(F32)
             hot = jnp.where(pos == row, 1.0, 0.0).astype(BF16)
-            o[pl.ds(r, 64), :] = jnp.dot(hot, src[...], preferred_element_type=F32).astype(BF16)
+            o[pl.ds(r, tile), :] = jnp.dot(hot, src[...], preferred_element_type=F32).astype(BF16)
             return 0
 
-        lax.fori_loop(0, rows // 64, tile_body, 0)
+        lax.fori_loop(0, 2, tile_body, 0)
         if meta and grouped:
             v = fl[pl.ds(0, META), :].astype(F32)
             for p in range(1, np_):
@@ -151,7 +153,7 @@
                 pltpu.make_async_copy(o2.at[e], acc2.at[e], wsem.at[5, e])]
 
     def row_copies(s, xp, yp):
-        at = lambda k: pl.ds(pl.multiple_of(s * PACK + k * hp, 64), (hp, PACK - hp)[k])
+        at = lambda k: pl.ds(pl.multiple_of(s * PACK + k * hp, 32), (hp, PACK - hp)[k])
         mt = pl.ds(pl.multiple_of(s * META, META), META)
         return [pltpu.make_async_copy(xp[0].at[pl.ds(hp, META)], xm.at[mt], msem.at[0, s]),
                 pltpu.make_async_copy(yp[0].at[pl.ds(hp, META)], ym.at[mt], msem.at[1, s]),

time: 314 us -> 312 us (level)
  Pallas kernels: 99.1 us -> 88.7 us
  waiting for transfers between devices: 103 us -> 110 us
    pallas_call x2, Pallas kernels: 23.3 us -> 13.1 us  [_pack(): pl.pallas_call(functools.partial(_pack_kernel, grouped, el, starts), out_...]
    ppermute x12, waiting for transfers between devices: 49 us -> 53.6 us  [chain(): l.append([lax.ppermute(v, 'data', LEFT) for v in l[-1]])]
  transfers between devices with their start and end apart: 30 -> 30, of which waited for: 7 -> 8; matrix products, arithmetic and copies ran while one was open for 16% -> 16% of each run, Pallas kernels for 26% -> 23%
where the time goes in v4:
time: 312 us; the launch traced here: 310 us
  waiting for transfers between devices  110 us (35%)
  Pallas kernels  88.7 us (28%)
  matrix products  45.8 us (15%)
  starting transfers between devices  43.6 us (14%)
  other arithmetic  9.57 us (3%)
  local copies, waits for them, and re-layouts  7.53 us (2%)
  between operations  4.15 us (1%)
    pallas_call x4, Pallas kernels, _dwp_call(): pl.pallas_call(functools.partial(_dwp_kernel, n, prev is None), out_shape...  62.4 us
    ppermute x12, waiting for transfers between devices, chain(): r.append([lax.ppermute(v, 'data', RIGHT) for v in r[-1]])  56.8 us
    ppermute x12, waiting for transfers between devices, chain(): l.append([lax.ppermute(v, 'data', LEFT) for v in l[-1]])  53.6 us
    dot_general x1, matrix products, body(): jnp.einsum('ecf,edf->ecd', dh1, w1, preferred_element_type=F32)  18.3 us
    ppermute x12, starting transfers between devices, chain(): l.append([lax.ppermute(v, 'data', LEFT) for v in l[-1]])  17.6 us
    dot_general x1, matrix products, body(): jnp.einsum('ecf,edf->ecd', dh3, w3, preferred_element_type=F32)  15.1 us
    pallas_call x2, Pallas kernels, _pack(): pl.pallas_call(functools.partial(_pack_kernel, grouped, el, starts), out_...  13.1 us
    dot_general x1, matrix products, body(): jnp.einsum('ecd,efd->ecf', dyd, w2, preferred_element_type=F32).astype(BF16)  12.2 us
  transfers between devices with their start and end apart: 30, of which 8 were waited for; matrix products, arithmetic and copies ran while one was open for 16% of the time, Pallas kernels for 23%

profile of v4, /device:TPU:0, one launch (start us, length us, event | category | flops | bytes accessed | tf_op | source)
XLA Modules:
  0.0 309.7 jit_solution(17929263716279855042)
XLA Ops:
  0.6 2.0 abs_reduce_fusion
  4.6 1.3 compare_select_fusion.to_ref
  6.0 4.5 %fusion.13 = (f32[1024]{0:T(1024)}, bf16[1024,768]{1,0:T(8,128)(2,1)}) fusion(bf16[1024,768]{1,0:T(8,128)(2,1)} %param.15, bf16[1024,1,768]{2,0,1:T(8,128)(2,1)} %param.19, f32[1024]{0:T(1024)} %bitcast.55), kind=kLoop, calls=%fused_computation.21 | loop fusion | flops 4717568 | bytes 4726784 | tf_op jit(solution)/shard_map/tkd,td->tk/dot_general | solution.py:481
  10.4 6.4 %send.1 = bf16[1344,768]{1,0:T(8,128)(2,1)} custom-call(f32[1]{0:T(128)} %bitcast.2.over_ref, s32[1,1024]{1,0:T(1,128)} %compare_select_fusion.to_ref, bf16[1024,768]{1,0:T(8,128)(2,1)} %get-tuple-element.187.v_ref), custom_call_target="tpu_custom_call" | custom-call | flops 2113929216 | bytes 3637248 | tf_op jit(solution)/shard_map/send/pallas_call | solution.py:101
  16.8 4.2 %all-to-all-start = ((bf16[4,336,768]{2,1,0:T(8,128)(2,1)}), bf16[4,336,768]{2,1,0:T(8,128)(2,1)S(1)}, u32[]{:S(2)}, u32[]{:S(2)}) async-start(bf16[4,336,768]{2,1,0:T(8,128)(2,1)} %bitcast.49), calls=%async_computation | async-start | bytes 4128768 | tf_op jit(solution)/shard_map/all_to_all | solution.py:478
  23.4 6.0 %shard_map.146 = (bf16[560,768]{1,0:T(8,128)(2,1)}, bf16[544,768]{1,0:T(8,128)(2,1)}) custom-call(f32[1,1280]{1,0:T(1,128)S(1)} %bitcast.52, f32[4]{0:T(128)S(1)} %reshape.276.meta_ref, bf16[2,640,768]{2,1,0:T(8,128)(2,1)} %src_ref.1), custom_call_target="tpu_custom_call" | custom-call | flops 2139095040 | bytes 3637248 | tf_op jit(solution)/shard_map/pallas_call | solution.py:73
  29.4 2.4 collective-permute-start.22
  32.0 2.0 collective-permute-start.10
  34.5 36.8 %collective-permute-done.10.refs_3_ = bf16[544,768]{1,0:T(8,128)(2,1)} collective-permute-done((bf16[544,768]{1,0:T(8,128)(2,1)}, bf16[544,768]{1,0:T(8,128)(2,1)}, u32[]{:S(2)}, u32[]{:S(2)}) %collective-permute-start.10) | collective-permute-done | bytes 835616 | tf_op jit(solution)/shard_map/ppermute | solution.py:465
  71.7 1.6 collective-permute-start.26
  73.3 1.6 collective-permute-start.23
  75.4 7.1 %shard_map.147 = (bf16[560,768]{1,0:T(8,128)(2,1)}, bf16[544,768]{1,0:T(8,128)(2,1)}) custom-call(f32[1,1280]{1,0:T(1,128)S(1)} %bitcast.53, f32[4]{0:T(128)S(1)} %reshape.276.meta_ref, bf16[4,336,768]{2,1,0:T(8,128)(2,1)S(1)} %all-to-all-done.src_ref), custom_call_target="tpu_custom_call" | custom-call | flops 2139095040 | bytes 3637248 | tf_op jit(solution)/shard_map/pallas_call | solution.py:73
  82.4 1.6 collective-permute-start.14
  84.3 12.2 %convolution_convert_fusion = bf16[2,640,3072]{2,1,0:T(8,128)(2,1)} fusion(bf16[2,640,768]{2,1,0:T(8,128)(2,1)S(1)} %bitcast.51, bf16[2,3072,768]{2,1,0:T(8,128)(2,1)} %refs_6_.1), kind=kOutput, calls=%fused_computation.15 | convolution fusion | flops 6043729920 | bytes 19267584 | tf_op jit(solution)/shard_map/ecd,efd->ecf/dot_general | solution.py:487
  97.0 1.6 collective-permute-start.18
  98.5 13.4 %collective-permute-done.23.refs_2_ = bf16[560,768]{1,0:T(8,128)(2,1)} collective-permute-done((bf16[560,768]{1,0:T(8,128)(2,1)}, bf16[560,768]{1,0:T(8,128)(2,1)}, u32[]{:S(2)}, u32[]{:S(2)}) %collective-permute-start.23) | collective-permute-done | bytes 860192 | tf_op jit(solution)/shard_map/ppermute | solution.py:466
  111.9 1.7 collective-permute-start.31
  113.6 1.6 collective-permute-start.12
  115.2 15.1 %fusion.8 = f32[2,640,768]{2,1,0:T(8,128)} fusion(bf16[2,768,3072]{2,1,0:T(8,128)(2,1)} %refs_5_.1, bf16[2,640,3072]{2,1,0:T(8,128)(2,1)} %convolution_convert_fusion, bf16[2,640,3072]{2,1,0:T(8,128)(2,1)} %param.21), kind=kOutput, calls=%fused_computation.13 | convolution fusion | flops 6071255040 | bytes 29097984 | tf_op jit(solution)/shard_map/ecf,edf->ecd/dot_general | solution.py:491
  130.3 16.3 %collective-permute-done.18.refs_11_ = bf16[544,768]{1,0:T(8,128)(2,1)} collective-permute-done((bf16[544,768]{1,0:T(8,128)(2,1)}, bf16[544,768]{1,0:T(8,128)(2,1)}, u32[]{:S(2)}, u32[]{:S(2)}) %collective-permute-start.18) | collective-permute-done | bytes 835616 | tf_op jit(solution)/shard_map/ppermute | solution.py:466
  146.6 1.3 collective-permute-start.27
  148.6 1.3 collective-permute-start.19
  150.7 15.0 %collective-permute-done.12.refs_1_ = bf16[544,768]{1,0:T(8,128)(2,1)S(1)} collective-permute-done((bf16[544,768]{1,0:T(8,128)(2,1)}, bf16[544,768]{1,0:T(8,128)(2,1)S(1)}, u32[]{:S(2)}, u32[]{:S(2)}) %collective-permute-start.12) | collective-permute-done | bytes 835616 | tf_op jit(solution)/shard_map/ppermute | solution.py:465
  165.6 0.9 copy-done.8
  166.6 1.6 collective-permute-start.15
  168.2 18.3 %add_convert_fusion = bf16[2,640,768]{2,1,0:T(8,128)(2,1)S(1)} fusion(f32[2,640,768]{2,1,0:T(8,128)} %fusion.8, bf16[2,768,3072]{2,1,0:T(8,128)(2,1)} %refs_4_.1, bf16[2,640,3072]{2,1,0:T(8,128)(2,1)} %convolution_convert_fusion, bf16[2,640,3072]{2,1,0:T(8,128)(2,1)} %param.21, bf16[2,640,3072]{2,1,0:T(8,128)(2,1)} %param.22), kind=kOutput, calls=%fused_computation.16 | convolution fusion | flops 6092881920 | bytes 38928384 | tf_op jit(solution)/shard_map/ecf,edf->ecd/dot_general | solution.py:490
  186.4 1.4 copy.53
  187.9 4.4 %all-to-all-start.1 = ((bf16[4,2,160,768]{3,2,1,0:T(8,128)(2,1)}), bf16[4,2,160,768]{3,2,1,0:T(8,128)(2,1)}, u32[]{:S(2)}, u32[]{:S(2)}) async-start(bf16[4,2,160,768]{3,2,1,0:T(8,128)(2,1)} %bitcast.47), calls=%async_computation.1 | async-start | bytes 3932160 | tf_op jit(solution)/shard_map/all_to_all | solution.py:493
  192.6 0.9 add_select_fusion.at_ref
  193.5 1.6 collective-permute-start.24
  195.5 1.6 collective-permute-start.20
  197.1 5.0 %collective-permute-done.32.refs_5_ = bf16[544,768]{1,0:T(8,128)(2,1)} collective-permute-done((bf16[544,768]{1,0:T(8,128)(2,1)}, bf16[544,768]{1,0:T(8,128)(2,1)}, u32[]{:S(2)}, u32[]{:S(2)}) %collective-permute-start.32) | collective-permute-done | bytes 835616 | tf_op jit(solution)/shard_map/ppermute | solution.py:465
  202.5 2.2 collective-permute-done.15.refs_6_
  204.7 1.3 collective-permute-start.16
  206.1 17.8 %shard_map.148 = (f32[2,768,384]{2,1,0:T(8,128)S(1)}, f32[2,768,384]{2,1,0:T(8,128)}, f32[2,384,768]{2,1,0:T(8,128)}, f32[16,768]{1,0:T(8,128)}) custom-call(s32[1]{0:T(128)} %bitcast.15.idx_ref, bf16[560,768]{1,0:T(8,128)(2,1)} %get-tuple-element.139.refs_0_, bf16[544,768]{1,0:T(8,128)(2,1)} %get-tuple-element.140.refs_1_, ...), custom_call_target="tpu_custom_call" | custom-call | flops 11551113216 | bytes 31457280 | tf_op jit(solution)/shard_map/pallas_call | solution.py:263
  223.9 2.2 collective-permute-start.30
  226.1 6.8 %unpack.1 = bf16[1024,768]{1,0:T(8,128)(2,1)} custom-call(s32[1024,1]{1,0:T(8,128)} %add_select_fusion.at_ref, bf16[1280,768]{1,0:T(8,128)(2,1)} %bitcast.12.src_ref), custom_call_target="tpu_custom_call" | custom-call | flops 2013265920 | bytes 3538944 | tf_op jit(solution)/shard_map/unpack/pallas_call | solution.py:125
  233.0 2.9 collective-permute-start.13
  235.8 5.2 %collective-permute-done.20.refs_7_ = bf16[544,768]{1,0:T(8,128)(2,1)} collective-permute-done((bf16[544,768]{1,0:T(8,128)(2,1)}, bf16[544,768]{1,0:T(8,128)(2,1)}, u32[]{:S(2)}, u32[]{:S(2)}) %collective-permute-start.20) | collective-permute-done | bytes 835616 | tf_op jit(solution)/shard_map/ppermute | solution.py:466
  241.1 1.4 collective-permute-start.9
  243.1 16.4 %collective-permute-done.16.refs_6_ = bf16[560,768]{1,0:T(8,128)(2,1)} collective-permute-done((bf16[560,768]{1,0:T(8,128)(2,1)}, bf16[560,768]{1,0:T(8,128)(2,1)}, u32[]{:S(2)}, u32[]{:S(2)}) %collective-permute-start.16) | collective-permute-done | bytes 860192 | tf_op jit(solution)/shard_map/ppermute | solution.py:466
  259.5 1.3 collective-permute-start.17
  260.9 16.0 %shard_map.149 = (f32[2,768,384]{2,1,0:T(8,128)S(1)}, f32[2,768,384]{2,1,0:T(8,128)}, f32[2,384,768]{2,1,0:T(8,128)}, f32[16,768]{1,0:T(8,128)}) custom-call(s32[1]{0:T(128)} %bitcast.15.idx_ref, bf16[560,768]{1,0:T(8,128)(2,1)} %collective-permute-done.7.refs_0_, ...), custom_call_target="tpu_custom_call", output_to_operand_aliasing={{0}: (12, {}), {1}: (13, {}), {2}: (14, {})} | custom-call | flops 7700742144 | bytes 27262976 | tf_op jit(solution)/shard_map/pallas_call | solution.py:263
  276.9 17.5 %shard_map.150 = (f32[2,768,384]{2,1,0:T(8,128)S(1)}, f32[2,768,384]{2,1,0:T(8,128)}, f32[2,384,768]{2,1,0:T(8,128)}, f32[16,768]{1,0:T(8,128)}) custom-call(s32[1]{0:T(128)} %bitcast.15.idx_ref, bf16[560,768]{1,0:T(8,128)(2,1)} %collective-permute-done.8.refs_0_, ...), custom_call_target="tpu_custom_call", output_to_operand_aliasing={{0}: (12, {}), {1}: (13, {}), {2}: (14, {})} | custom-call | flops 7700742144 | bytes 27262976 | tf_op jit(solution)/shard_map/pallas_call | solution.py:263
  294.4 0.9 copy-done.6
  295.3 11.2 %shard_map.151 = (f32[2,768,384]{2,1,0:T(8,128)S(1)}, f32[2,768,384]{2,1,0:T(8,128)}, f32[2,384,768]{2,1,0:T(8,128)}, f32[16,768]{1,0:T(8,128)}) custom-call(s32[1]{0:T(128)} %bitcast.15.idx_ref, bf16[560,768]{1,0:T(8,128)(2,1)} %copy-done.6, ...), custom_call_target="tpu_custom_call", output_to_operand_aliasing={{0}: (8, {}), {1}: (9, {}), {2}: (10, {})} | custom-call | flops 3850371072 | bytes 23068672 | tf_op jit(solution)/shard_map/pallas_call | solution.py:263
  306.5 1.2 slice.28
  308.3 1.4 copy-done
  (60 shorter events, 7.2 us)
Async XLA Ops:
  16.8 58.6 %all-to-all-start = ((bf16[4,336,768]{2,1,0:T(8,128)(2,1)}), bf16[4,336,768]{2,1,0:T(8,128)(2,1)S(1)}, u32[]{:S(2)}, u32[]{:S(2)}) async-start(bf16[4,336,768]{2,1,0:T(8,128)(2,1)} %bitcast.49), calls=%async_computation | async-start | bytes 4128768 | tf_op jit(solution)/shard_map/all_to_all | solution.py:478
  23.4 10.6 %copy-start.11 = (s32[1024,1]{0,1:T(1,128)S(1)}, s32[1024,1]{0,1:T(1,128)}, u32[]{:S(2)}) copy-start(s32[1024,1]{0,1:T(1,128)} %param.18) | copy-start | bytes 12292
  23.4 10.8 %copy-start.12 = (s32[1024,1]{0,1:T(1,128)S(1)}, s32[1024,1]{0,1:T(1,128)}, u32[]{:S(2)}) copy-start(s32[1024,1]{0,1:T(1,128)} %param.17) | copy-start | bytes 12292
  29.4 43.9 %collective-permute-start.22 = (bf16[560,768]{1,0:T(8,128)(2,1)}, bf16[560,768]{1,0:T(8,128)(2,1)}, u32[]{:S(2)}, u32[]{:S(2)}) collective-permute-start(bf16[560,768]{1,0:T(8,128)(2,1)} %get-tuple-element.139.refs_0_), channel_id=1, source_target_pairs={{8,0},{16,8},{24,16},{28,24},{20,28},{12,20},{4,12},{0,4},{9,1},{1... | collective-permute-start | bytes 2580488 | tf_op jit(solution)/shard_map/ppermute | solution.py:466
  31.8 43.1 %collective-permute-start.6 = (bf16[560,768]{1,0:T(8,128)(2,1)}, bf16[560,768]{1,0:T(8,128)(2,1)}, u32[]{:S(2)}, u32[]{:S(2)}) collective-permute-start(bf16[560,768]{1,0:T(8,128)(2,1)} %get-tuple-element.139.refs_0_), channel_id=1, source_target_pairs={{0,8},{8,16},{16,24},{24,28},{28,20},{20,12},{12,4},{4,0},{1,9},{9... | collective-permute-start | bytes 2580488 | tf_op jit(solution)/shard_map/ppermute | solution.py:465
  32.0 39.3 %collective-permute-start.10 = (bf16[544,768]{1,0:T(8,128)(2,1)}, bf16[544,768]{1,0:T(8,128)(2,1)}, u32[]{:S(2)}, u32[]{:S(2)}) collective-permute-start(bf16[544,768]{1,0:T(8,128)(2,1)} %get-tuple-element.140.refs_1_), channel_id=1, source_target_pairs={{0,8},{8,16},{16,24},{24,28},{28,20},{20,12},{12,4},{4,0},{1,9},{9... | collective-permute-start | bytes 2506760 | tf_op jit(solution)/shard_map/ppermute | solution.py:465
  33.9 37.8 %collective-permute-start.25 = (bf16[544,768]{1,0:T(8,128)(2,1)}, bf16[544,768]{1,0:T(8,128)(2,1)}, u32[]{:S(2)}, u32[]{:S(2)}) collective-permute-start(bf16[544,768]{1,0:T(8,128)(2,1)} %get-tuple-element.140.refs_1_), channel_id=1, source_target_pairs={{8,0},{16,8},{24,16},{28,24},{20,28},{12,20},{4,12},{0,4},{9,1},{1... | collective-permute-start | bytes 2506760 | tf_op jit(solution)/shard_map/ppermute | solution.py:466
  71.3 25.2 %collective-permute-start.11 = (bf16[544,768]{1,0:T(8,128)(2,1)}, bf16[544,768]{1,0:T(8,128)(2,1)}, u32[]{:S(2)}, u32[]{:S(2)}) collective-permute-start(bf16[544,768]{1,0:T(8,128)(2,1)} %collective-permute-done.10.refs_3_), channel_id=1, source_target_pairs={{0,8},{8,16},{16,24},{24,28},{28,20},{20,12},{12,4},{4,0},{1,9},{9... | collective-permute-start | bytes 2506760 | tf_op jit(solution)/shard_map/ppermute | solution.py:465
  71.7 25.3 %collective-permute-start.26 = (bf16[544,768]{1,0:T(8,128)(2,1)}, bf16[544,768]{1,0:T(8,128)(2,1)}, u32[]{:S(2)}, u32[]{:S(2)}) collective-permute-start(bf16[544,768]{1,0:T(8,128)(2,1)} %collective-permute-done.25.refs_5_), channel_id=1, source_target_pairs={{8,0},{16,8},{24,16},{28,24},{20,28},{12,20},{4,12},{0,4},{9,1},{1... | collective-permute-start | bytes 2506760 | tf_op jit(solution)/shard_map/ppermute | solution.py:466
  73.3 38.6 %collective-permute-start.23 = (bf16[560,768]{1,0:T(8,128)(2,1)}, bf16[560,768]{1,0:T(8,128)(2,1)}, u32[]{:S(2)}, u32[]{:S(2)}) collective-permute-start(bf16[560,768]{1,0:T(8,128)(2,1)} %collective-permute-done.22.refs_4_), channel_id=1, source_target_pairs={{8,0},{16,8},{24,16},{28,24},{20,28},{12,20},{4,12},{0,4},{9,1},{1... | collective-permute-start | bytes 2580488 | tf_op jit(solution)/shard_map/ppermute | solution.py:466
  74.9 38.7 %collective-permute-start.7 = (bf16[560,768]{1,0:T(8,128)(2,1)}, bf16[560,768]{1,0:T(8,128)(2,1)}, u32[]{:S(2)}, u32[]{:S(2)}) collective-permute-start(bf16[560,768]{1,0:T(8,128)(2,1)} %collective-permute-done.6.refs_2_), channel_id=1, source_target_pairs={{0,8},{8,16},{16,24},{24,28},{28,20},{20,12},{12,4},{4,0},{1,9},{9... | collective-permute-start | bytes 2580488 | tf_op jit(solution)/shard_map/ppermute | solution.py:465
  75.4 8.7 %copy-start.5 = (bf16[4,336,768]{2,1,0:T(8,128)(2,1)}, bf16[4,336,768]{2,1,0:T(8,128)(2,1)S(1)}, u32[]{:S(2)}) copy-start(bf16[4,336,768]{2,1,0:T(8,128)(2,1)S(1)} %all-to-all-done.src_ref) | copy-start | bytes 6193156
  82.4 66.2 %collective-permute-start.14 = (bf16[560,768]{1,0:T(8,128)(2,1)}, bf16[560,768]{1,0:T(8,128)(2,1)}, u32[]{:S(2)}, u32[]{:S(2)}) collective-permute-start(bf16[560,768]{1,0:T(8,128)(2,1)} %get-tuple-element.141.refs_6_), channel_id=1, source_target_pairs={{8,0},{16,8},{24,16},{28,24},{20,28},{12,20},{4,12},{0,4},{9,1},{1... | collective-permute-start | bytes 2580488 | tf_op jit(solution)/shard_map/ppermute | solution.py:466
  96.5 53.5 %collective-permute-start.28 = (bf16[560,768]{1,0:T(8,128)(2,1)}, bf16[560,768]{1,0:T(8,128)(2,1)}, u32[]{:S(2)}, u32[]{:S(2)}) collective-permute-start(bf16[560,768]{1,0:T(8,128)(2,1)} %get-tuple-element.141.refs_6_), channel_id=1, source_target_pairs={{0,8},{8,16},{16,24},{24,28},{28,20},{20,12},{12,4},{4,0},{1,9},{9... | collective-permute-start | bytes 2580488 | tf_op jit(solution)/shard_map/ppermute | solution.py:465
  97.0 49.7 %collective-permute-start.18 = (bf16[544,768]{1,0:T(8,128)(2,1)}, bf16[544,768]{1,0:T(8,128)(2,1)}, u32[]{:S(2)}, u32[]{:S(2)}) collective-permute-start(bf16[544,768]{1,0:T(8,128)(2,1)} %get-tuple-element.142.refs_7_), channel_id=1, source_target_pairs={{8,0},{16,8},{24,16},{28,24},{20,28},{12,20},{4,12},{0,4},{9,1},{1... | collective-permute-start | bytes 2506760 | tf_op jit(solution)/shard_map/ppermute | solution.py:466
  111.9 36.1 %collective-permute-start.31 = (bf16[544,768]{1,0:T(8,128)(2,1)}, bf16[544,768]{1,0:T(8,128)(2,1)}, u32[]{:S(2)}, u32[]{:S(2)}) collective-permute-start(bf16[544,768]{1,0:T(8,128)(2,1)} %get-tuple-element.142.refs_7_), channel_id=1, source_target_pairs={{0,8},{8,16},{16,24},{24,28},{28,20},{20,12},{12,4},{4,0},{1,9},{9... | collective-permute-start | bytes 2506760 | tf_op jit(solution)/shard_map/ppermute | solution.py:465
  113.6 52.1 %collective-permute-start.12 = (bf16[544,768]{1,0:T(8,128)(2,1)}, bf16[544,768]{1,0:T(8,128)(2,1)S(1)}, u32[]{:S(2)}, u32[]{:S(2)}) collective-permute-start(bf16[544,768]{1,0:T(8,128)(2,1)} %collective-permute-done.11.refs_1_), channel_id=1, source_target_pairs={{0,8},{8,16},{16,24},{24,28},{28,20},{20,12},{12,4},{4,0},{1,9},{9... | collective-permute-start | bytes 2506760 | tf_op jit(solution)/shard_map/ppermute | solution.py:465
  146.6 46.9 %collective-permute-start.27 = (bf16[544,768]{1,0:T(8,128)(2,1)}, bf16[544,768]{1,0:T(8,128)(2,1)}, u32[]{:S(2)}, u32[]{:S(2)}) collective-permute-start(bf16[544,768]{1,0:T(8,128)(2,1)} %collective-permute-done.26.refs_3_), channel_id=1, source_target_pairs={{8,0},{16,8},{24,16},{28,24},{20,28},{12,20},{4,12},{0,4},{9,1},{1... | collective-permute-start | bytes 2506760 | tf_op jit(solution)/shard_map/ppermute | solution.py:466
  148.0 47.1 %collective-permute-start.8 = (bf16[560,768]{1,0:T(8,128)(2,1)}, bf16[560,768]{1,0:T(8,128)(2,1)}, u32[]{:S(2)}, u32[]{:S(2)}) collective-permute-start(bf16[560,768]{1,0:T(8,128)(2,1)} %collective-permute-done.7.refs_0_), channel_id=1, source_target_pairs={{0,8},{8,16},{16,24},{24,28},{28,20},{20,12},{12,4},{4,0},{1,9},{9... | collective-permute-start | bytes 2580488 | tf_op jit(solution)/shard_map/ppermute | solution.py:465
  148.6 46.9 %collective-permute-start.19 = (bf16[544,768]{1,0:T(8,128)(2,1)}, bf16[544,768]{1,0:T(8,128)(2,1)}, u32[]{:S(2)}, u32[]{:S(2)}) collective-permute-start(bf16[544,768]{1,0:T(8,128)(2,1)} %collective-permute-done.18.refs_11_), channel_id=1, source_target_pairs={{8,0},{16,8},{24,16},{28,24},{20,28},{12,20},{4,12},{0,4},{9,1},{1... | collective-permute-start | bytes 2506760 | tf_op jit(solution)/shard_map/ppermute | solution.py:466
  150.0 52.1 %collective-permute-start.32 = (bf16[544,768]{1,0:T(8,128)(2,1)}, bf16[544,768]{1,0:T(8,128)(2,1)}, u32[]{:S(2)}, u32[]{:S(2)}) collective-permute-start(bf16[544,768]{1,0:T(8,128)(2,1)} %collective-permute-done.31.refs_9_), channel_id=1, source_target_pairs={{0,8},{8,16},{16,24},{24,28},{28,20},{20,12},{12,4},{4,0},{1,9},{9... | collective-permute-start | bytes 2506760 | tf_op jit(solution)/shard_map/ppermute | solution.py:465
  165.6 0.9 copy-start.8
  166.6 38.1 %collective-permute-start.15 = (bf16[560,768]{1,0:T(8,128)(2,1)}, bf16[560,768]{1,0:T(8,128)(2,1)}, u32[]{:S(2)}, u32[]{:S(2)}) collective-permute-start(bf16[560,768]{1,0:T(8,128)(2,1)} %collective-permute-done.14.refs_10_), channel_id=1, source_target_pairs={{8,0},{16,8},{24,16},{28,24},{20,28},{12,20},{4,12},{0,4},{9,1},{1... | collective-permute-start | bytes 2580488 | tf_op jit(solution)/shard_map/ppermute | solution.py:466
  187.9 38.2 %all-to-all-start.1 = ((bf16[4,2,160,768]{3,2,1,0:T(8,128)(2,1)}), bf16[4,2,160,768]{3,2,1,0:T(8,128)(2,1)}, u32[]{:S(2)}, u32[]{:S(2)}) async-start(bf16[4,2,160,768]{3,2,1,0:T(8,128)(2,1)} %bitcast.47), calls=%async_computation.1 | async-start | bytes 3932160 | tf_op jit(solution)/shard_map/all_to_all | solution.py:493
  193.5 39.4 %collective-permute-start.24 = (bf16[560,768]{1,0:T(8,128)(2,1)}, bf16[560,768]{1,0:T(8,128)(2,1)S(1)}, u32[]{:S(2)}, u32[]{:S(2)}) collective-permute-start(bf16[560,768]{1,0:T(8,128)(2,1)} %collective-permute-done.23.refs_2_), channel_id=1, source_target_pairs={{8,0},{16,8},{24,16},{28,24},{20,28},{12,20},{4,12},{0,4},{9,1},{1... | collective-permute-start | bytes 2580488 | tf_op jit(solution)/shard_map/ppermute | solution.py:466
  195.1 28.8 %collective-permute-start.29 = (bf16[560,768]{1,0:T(8,128)(2,1)}, bf16[560,768]{1,0:T(8,128)(2,1)}, u32[]{:S(2)}, u32[]{:S(2)}) collective-permute-start(bf16[560,768]{1,0:T(8,128)(2,1)} %collective-permute-done.28.refs_8_), channel_id=1, source_target_pairs={{0,8},{8,16},{16,24},{24,28},{28,20},{20,12},{12,4},{4,0},{1,9},{9... | collective-permute-start | bytes 2580488 | tf_op jit(solution)/shard_map/ppermute | solution.py:465
  195.5 45.5 %collective-permute-start.20 = (bf16[544,768]{1,0:T(8,128)(2,1)}, bf16[544,768]{1,0:T(8,128)(2,1)}, u32[]{:S(2)}, u32[]{:S(2)}) collective-permute-start(bf16[544,768]{1,0:T(8,128)(2,1)} %collective-permute-done.19.refs_7_), channel_id=1, source_target_pairs={{8,0},{16,8},{24,16},{28,24},{20,28},{12,20},{4,12},{0,4},{9,1},{1... | collective-permute-start | bytes 2506760 | tf_op jit(solution)/shard_map/ppermute | solution.py:466
  202.1 40.4 %collective-permute-start.33 = (bf16[544,768]{1,0:T(8,128)(2,1)}, bf16[544,768]{1,0:T(8,128)(2,1)}, u32[]{:S(2)}, u32[]{:S(2)}) collective-permute-start(bf16[544,768]{1,0:T(8,128)(2,1)} %collective-permute-done.32.refs_5_), channel_id=1, source_target_pairs={{0,8},{8,16},{16,24},{24,28},{28,20},{20,12},{12,4},{4,0},{1,9},{9... | collective-permute-start | bytes 2506760 | tf_op jit(solution)/shard_map/ppermute | solution.py:465
  204.7 54.8 %collective-permute-start.16 = (bf16[560,768]{1,0:T(8,128)(2,1)}, bf16[560,768]{1,0:T(8,128)(2,1)}, u32[]{:S(2)}, u32[]{:S(2)}) collective-permute-start(bf16[560,768]{1,0:T(8,128)(2,1)} %collective-permute-done.15.refs_6_), channel_id=1, source_target_pairs={{8,0},{16,8},{24,16},{28,24},{20,28},{12,20},{4,12},{0,4},{9,1},{1... | collective-permute-start | bytes 2580488 | tf_op jit(solution)/shard_map/ppermute | solution.py:466
  223.9 53.0 %collective-permute-start.30 = (bf16[560,768]{1,0:T(8,128)(2,1)}, bf16[560,768]{1,0:T(8,128)(2,1)}, u32[]{:S(2)}, u32[]{:S(2)}) collective-permute-start(bf16[560,768]{1,0:T(8,128)(2,1)} %collective-permute-done.29.refs_4_), channel_id=1, source_target_pairs={{0,8},{8,16},{16,24},{24,28},{28,20},{20,12},{12,4},{4,0},{1,9},{9... | collective-permute-start | bytes 2580488 | tf_op jit(solution)/shard_map/ppermute | solution.py:465
  233.0 2.9 copy-start.7
  233.0 61.4 %collective-permute-start.13 = (bf16[544,768]{1,0:T(8,128)(2,1)}, bf16[544,768]{1,0:T(8,128)(2,1)}, u32[]{:S(2)}, u32[]{:S(2)}) collective-permute-start(bf16[544,768]{1,0:T(8,128)(2,1)} %copy-done.8), channel_id=1, source_target_pairs={{0,8},{8,16},{16,24},{24,28},{28,20},{20,12},{12,4},{4,0},{1,9},{9... | collective-permute-start | bytes 2506760 | tf_op jit(solution)/shard_map/ppermute | solution.py:468
  241.1 53.3 %collective-permute-start.9 = (bf16[560,768]{1,0:T(8,128)(2,1)}, bf16[560,768]{1,0:T(8,128)(2,1)S(1)}, u32[]{:S(2)}, u32[]{:S(2)}) collective-permute-start(bf16[560,768]{1,0:T(8,128)(2,1)} %collective-permute-done.8.refs_0_), channel_id=1, source_target_pairs={{0,8},{8,16},{16,24},{24,28},{28,20},{20,12},{12,4},{4,0},{1,9},{9... | collective-permute-start | bytes 2580488 | tf_op jit(solution)/shard_map/ppermute | solution.py:468
  242.5 51.9 %collective-permute-start.21 = (bf16[544,768]{1,0:T(8,128)(2,1)}, bf16[544,768]{1,0:T(8,128)(2,1)}, u32[]{:S(2)}, u32[]{:S(2)}) collective-permute-start(bf16[544,768]{1,0:T(8,128)(2,1)} %collective-permute-done.20.refs_7_), channel_id=1, source_target_pairs={{8,0},{16,8},{24,16},{28,24},{20,28},{12,20},{4,12},{0,4},{9,1},{1... | collective-permute-start | bytes 2506760 | tf_op jit(solution)/shard_map/ppermute | solution.py:468
  259.5 34.9 %collective-permute-start.17 = (bf16[560,768]{1,0:T(8,128)(2,1)}, bf16[560,768]{1,0:T(8,128)(2,1)}, u32[]{:S(2)}, u32[]{:S(2)}) collective-permute-start(bf16[560,768]{1,0:T(8,128)(2,1)} %collective-permute-done.16.refs_6_), channel_id=1, source_target_pairs={{8,0},{16,8},{24,16},{28,24},{20,28},{12,20},{4,12},{0,4},{9,1},{1... | collective-permute-start | bytes 2580488 | tf_op jit(solution)/shard_map/ppermute | solution.py:468
  294.4 0.9 copy-start.6
  308.3 1.4 copy-start
